TPU v7x, 32 devices: a whole 2x2x4 slice. The times are simulated.
32 devices in a mesh: dp: 8 (over y, x, core), tensor: 4 (over z).
Axes of the slice: x: 2, y: 2, z: 4, core: 2. Of those that a mesh axis runs over, the one named last changes fastest.
Arguments:
- tokens: bfloat16 [1024, 8, 1280], P('tensor', 'dp'), may hold values from -6 to 6
- cotangent: bfloat16 [1024, 8, 1280], P('tensor', 'dp'), may hold values from -6 to 6
- qkv_weight: float32 [3, 1280, 1280], P(None, 'dp', 'tensor'), may hold values from -0.15625 to 0.15625
- out_weight: float32 [1280, 1280], P('tensor', 'dp'), may hold values from -1.25 to 1.25
- expand_weight: float32 [1280, 5120], P('dp', 'tensor'), may hold values from -0.15625 to 0.15625
- reduce_weight: float32 [5120, 1280], P('tensor', 'dp'), may hold values from -0.078125 to 0.078125
- gains_biases: float32 [15360], P(('dp', 'tensor')), may hold values from -1 to 2, as said below
- rel_tables: float32 [2, 63, 80], replicated, may hold values from -1.5 to 1.5
- qkv_moment: float32 [3, 1280, 1280], P(None, 'dp', 'tensor'), may hold values from -192 to 192
- out_moment: float32 [1280, 1280], P('tensor', 'dp'), may hold values from -192 to 192
- expand_moment: float32 [1280, 5120], P('dp', 'tensor'), may hold values from -192 to 192
- reduce_moment: float32 [5120, 1280], P('tensor', 'dp'), may hold values from -192 to 192
- gains_moment: float32 [15360], P(('dp', 'tensor')), may hold values from -640 to 640
- rel_moment: float32 [2, 63, 80], replicated, may hold values from -1536 to 1536
- qkv_average: float32 [3, 1280, 1280], P(None, 'dp', 'tensor'), may hold values from -0.15625 to 0.15625
- out_average: float32 [1280, 1280], P('tensor', 'dp'), may hold values from -1.25 to 1.25
- expand_average: float32 [1280, 5120], P('dp', 'tensor'), may hold values from -0.15625 to 0.15625
- reduce_average: float32 [5120, 1280], P('tensor', 'dp'), may hold values from -0.078125 to 0.078125
- gains_average: float32 [15360], P(('dp', 'tensor')), may hold values from 0.1 to 1.9
- rel_average: float32 [2, 63, 80], replicated, may hold values from -1.5 to 1.5
Outputs:
- block_out: bfloat16 [1024, 8, 1280], P('tensor', 'dp')
- token_grad: float32 [1024, 8, 1280], P('tensor', 'dp')
- qkv_grad: float32 [3, 1280, 1280], P(None, 'dp', 'tensor')
- out_grad: float32 [1280, 1280], P('tensor', 'dp')
- expand_grad: float32 [1280, 5120], P('dp', 'tensor')
- reduce_grad: float32 [5120, 1280], P('tensor', 'dp')
- gains_grad: float32 [15360], P(('dp', 'tensor'))
- rel_grad: float32 [2, 63, 80], replicated
- new_qkv: float32 [3, 1280, 1280], P(None, 'dp', 'tensor')
- new_out: float32 [1280, 1280], P('tensor', 'dp')
- new_expand: float32 [1280, 5120], P('dp', 'tensor')
- new_reduce: float32 [5120, 1280], P('tensor', 'dp')
- new_gains: float32 [15360], P(('dp', 'tensor'))
- new_rel: float32 [2, 63, 80], replicated
- moment_qkv: float32 [3, 1280, 1280], P(None, 'dp', 'tensor')
- moment_out: float32 [1280, 1280], P('tensor', 'dp')
- moment_expand: float32 [1280, 5120], P('dp', 'tensor')
- moment_reduce: float32 [5120, 1280], P('tensor', 'dp')
- moment_gains: float32 [15360], P(('dp', 'tensor'))
- moment_rel: float32 [2, 63, 80], replicated
- average_qkv: float32 [3, 1280, 1280], P(None, 'dp', 'tensor')
- average_out: float32 [1280, 1280], P('tensor', 'dp')
- average_expand: float32 [1280, 5120], P('dp', 'tensor')
- average_reduce: float32 [5120, 1280], P('tensor', 'dp')
- average_gains: float32 [15360], P(('dp', 'tensor'))
- average_rel: float32 [2, 63, 80], replicated
Inputs may be any that keep to these rules, and one draw needn't show every extreme that they name: `gains_biases`: the two norm gains lie between 0.5 and 1.5.
All inputs are finite; a program needn't handle non-finite values.
Results may differ from a plain program's by a relative error of at most 0.015.
The roundings to bfloat16 on the way count: a program that leaves them out, or rounds other values in their place, can miss the bound.
Values may be sent and summed in bfloat16 or wider, within the bound.
A program may use at most 192 MiB of HBM per device.

v0:
```python
import jax
import jax.numpy as jnp
from jax import lax
from jax.sharding import PartitionSpec as P

EPSILON = 1e-06
MOMENTUM = 0.5
AVERAGING = 0.5
RATE_MAIN = 0.0003
RATE_TABLES = 0.01
NARROW = jnp.bfloat16
SINGLE = jnp.float32


def offset_table(grid_side):
    table_shape = (grid_side, grid_side, 2 * grid_side - 1)
    first_axis = lax.broadcasted_iota(jnp.int32, table_shape, 0)
    second_axis = lax.broadcasted_iota(jnp.int32, table_shape, 1)
    third_axis = lax.broadcasted_iota(jnp.int32, table_shape, 2)
    return (third_axis == first_axis - second_axis + grid_side - 1).astype(SINGLE)


def normalize(values, gain_row, shift_row):
    center = values - jnp.mean(values, axis=-1, keepdims=True)
    inverse = lax.rsqrt(jnp.mean(center * center, axis=-1, keepdims=True) + EPSILON)
    scaled = center * inverse
    return (scaled * gain_row + shift_row, scaled, inverse)


def normalize_back(grad_output, scaled, inverse, gain_row):
    grad_scaled = grad_output * gain_row
    mean_plain = jnp.mean(grad_scaled, axis=-1, keepdims=True)
    mean_cross = jnp.mean(grad_scaled * scaled, axis=-1, keepdims=True)
    grad_values = inverse * (grad_scaled - mean_plain - scaled * mean_cross)
    return (grad_values, jnp.sum(grad_output * scaled, axis=0), jnp.sum(grad_output, axis=0))


def gelu_slope(values):
    cumulative = 0.5 * (1.0 + lax.erf(values * 0.7071067811865476))
    density = 0.3989422804014327 * jnp.exp(-0.5 * values * values)
    return cumulative + values * density


def contract_rows(left_side, right_side):
    return lax.dot_general(
        left_side, right_side, (((0,), (0,)), ((), ())), preferred_element_type=SINGLE
    )


def contract_cols(left_side, right_side):
    return lax.dot_general(
        left_side, right_side, (((1,), (1,)), ((), ())), preferred_element_type=SINGLE
    )


def to_images(row_values, seq_length, image_count, head_size):
    return row_values.reshape(seq_length, image_count, -1, head_size).transpose(1, 0, 2, 3)


def from_images(image_values):
    image_count, seq_length = (image_values.shape[0], image_values.shape[1])
    return image_values.transpose(1, 0, 2, 3).reshape(seq_length * image_count, -1)


def block_scores(query_block, key_rows, rows_block, rel_cols):
    block_len, head_count, head_size = query_block.shape
    grid_side = rel_cols.shape[0]
    grid_rows = block_len // grid_side
    shaped = query_block.reshape(grid_rows, grid_side, head_count, head_size)
    row_bias = jnp.einsum("abhc,akc->habk", shaped, rows_block, preferred_element_type=SINGLE)
    col_bias = jnp.einsum("abhc,bkc->habk", shaped, rel_cols, preferred_element_type=SINGLE)
    dot_scores = jnp.einsum(
        "qhc,khc->hqk", query_block, key_rows, preferred_element_type=SINGLE
    ) * head_size ** (-0.5)
    scores = dot_scores.reshape(head_count, grid_rows, grid_side, grid_side, grid_side)
    scores = scores + row_bias[..., :, None] + col_bias[..., None, :]
    return scores.reshape(head_count, block_len, grid_side * grid_side)


def attend_image(query_rows, key_rows, value_rows, rel_rows, rel_cols):
    seq_length, head_count, head_size = query_rows.shape
    grid_side = rel_rows.shape[0]
    block_len = min(512, seq_length)
    block_count = seq_length // block_len

    def one_block(inputs):
        query_block, rows_block = inputs
        scores = block_scores(query_block, key_rows, rows_block, rel_cols)
        highest = jnp.max(scores, axis=-1, keepdims=True)
        logsum = highest + jnp.log(jnp.sum(jnp.exp(scores - highest), axis=-1, keepdims=True))
        weights_low = jnp.exp(scores - logsum).astype(NARROW)
        context = jnp.einsum("hqk,khc->qhc", weights_low, value_rows, preferred_element_type=SINGLE)
        return (context.astype(NARROW), logsum[..., 0])

    blocks_in = (
        query_rows.reshape(block_count, block_len, head_count, head_size),
        rel_rows.reshape(block_count, block_len // grid_side, grid_side, head_size),
    )
    contexts, logsums = lax.map(one_block, blocks_in)
    return (contexts.reshape(seq_length, head_count, head_size), logsums)


def attend_back(query_rows, key_rows, value_rows, logsums, grad_context, rel_rows, rel_cols):
    seq_length, head_count, head_size = query_rows.shape
    grid_side = rel_rows.shape[0]
    block_len = min(512, seq_length)
    block_count = seq_length // block_len
    grid_rows = block_len // grid_side
    score_scale = head_size ** (-0.5)

    def one_block(carry, inputs):
        grad_keys, grad_values, grad_cols = carry
        query_block, rows_block, logsum, grad_block = inputs
        scores = block_scores(query_block, key_rows, rows_block, rel_cols)
        weights_soft = jnp.exp(scores - logsum[..., None])
        grad_values = grad_values + jnp.einsum(
            "hqk,qhc->khc", weights_soft.astype(NARROW), grad_block, preferred_element_type=SINGLE
        )
        grad_soft = jnp.einsum(
            "qhc,khc->hqk", grad_block, value_rows, preferred_element_type=SINGLE
        )
        inner_sum = jnp.sum(weights_soft * grad_soft, axis=-1, keepdims=True)
        grad_scores = (weights_soft * (grad_soft - inner_sum)).astype(NARROW)
        grad_keys = grad_keys + score_scale * jnp.einsum(
            "hqk,qhc->khc", grad_scores, query_block, preferred_element_type=SINGLE
        )
        split_grad = grad_scores.reshape(head_count, grid_rows, grid_side, grid_side, grid_side)
        grad_row_bias = jnp.sum(split_grad, axis=-1, dtype=SINGLE).astype(NARROW)
        grad_col_bias = jnp.sum(split_grad, axis=-2, dtype=SINGLE).astype(NARROW)
        shaped = query_block.reshape(grid_rows, grid_side, head_count, head_size)
        from_bias = jnp.einsum(
            "habk,akc->abhc", grad_row_bias, rows_block, preferred_element_type=SINGLE
        )
        from_bias = from_bias + jnp.einsum(
            "habk,bkc->abhc", grad_col_bias, rel_cols, preferred_element_type=SINGLE
        )
        grad_query = score_scale * jnp.einsum(
            "hqk,khc->qhc", grad_scores, key_rows, preferred_element_type=SINGLE
        )
        grad_query = grad_query + from_bias.reshape(block_len, head_count, head_size)
        grad_rows_block = jnp.einsum(
            "habk,abhc->akc", grad_row_bias, shaped, preferred_element_type=SINGLE
        )
        grad_cols = grad_cols + jnp.einsum(
            "habk,abhc->bkc", grad_col_bias, shaped, preferred_element_type=SINGLE
        )
        return ((grad_keys, grad_values, grad_cols), (grad_query.astype(NARROW), grad_rows_block))

    zeros_keys = jnp.zeros((seq_length, head_count, head_size), SINGLE)
    carry_init = (zeros_keys, zeros_keys, jnp.zeros((grid_side, grid_side, head_size), SINGLE))
    blocks_in = (
        query_rows.reshape(block_count, block_len, head_count, head_size),
        rel_rows.reshape(block_count, grid_rows, grid_side, head_size),
        logsums,
        grad_context.reshape(block_count, block_len, head_count, head_size),
    )
    carry_out, stacked = lax.scan(one_block, carry_init, blocks_in)
    grad_keys, grad_values, grad_cols = carry_out
    grad_query, grad_rows = stacked
    return (
        grad_query.reshape(seq_length, head_count, head_size),
        grad_keys.astype(NARROW),
        grad_values.astype(NARROW),
        grad_rows.reshape(grid_side, grid_side, head_size),
        grad_cols,
    )


def advance(weight, moment, average, gradient, rate_value):
    new_moment = MOMENTUM * moment + gradient
    new_weight = weight - rate_value * (gradient + MOMENTUM * new_moment)
    new_average = AVERAGING * average + (1.0 - AVERAGING) * new_weight
    return (new_weight, new_moment, new_average)


def local(
    tokens,
    cotangent,
    qkv_weight,
    out_weight,
    expand_weight,
    reduce_weight,
    gains_biases,
    rel_tables,
    qkv_moment,
    out_moment,
    expand_moment,
    reduce_moment,
    gains_moment,
    rel_moment,
    qkv_average,
    out_average,
    expand_average,
    reduce_average,
    gains_average,
    rel_average,
):
    local_seq, local_images, model_width = tokens.shape
    tensor_count = lax.axis_size("tensor")
    tensor_index = lax.axis_index("tensor")
    local_rows = local_seq * local_images
    seq_length = local_seq * tensor_count
    head_width = qkv_weight.shape[2]
    hidden_width = expand_weight.shape[1]
    head_size = rel_tables.shape[2]
    grid_side = (rel_tables.shape[1] + 1) // 2
    qkv_full, out_full, expand_full, reduce_full = (
        lax.all_gather(qkv_weight.astype(NARROW), "dp", axis=1, tiled=True),
        lax.all_gather(out_weight.astype(NARROW), "dp", axis=1, tiled=True),
        lax.all_gather(expand_weight.astype(NARROW), "dp", axis=0, tiled=True),
        lax.all_gather(reduce_weight.astype(NARROW), "dp", axis=1, tiled=True),
    )
    qkv_joined = qkv_full.transpose(1, 0, 2).reshape(model_width, 3 * head_width)
    params_all = lax.all_gather(gains_biases, ("dp", "tensor"), axis=0, tiled=True)

    def segment(position):
        return params_all[position * model_width : (position + 1) * model_width]

    query_bias = lax.dynamic_slice_in_dim(
        params_all, 2 * model_width + tensor_index * head_width, head_width
    )
    value_bias = lax.dynamic_slice_in_dim(
        params_all, 3 * model_width + tensor_index * head_width, head_width
    )
    offsets = offset_table(grid_side)
    offsets_low = offsets.astype(NARROW)
    rel_low = rel_tables.astype(NARROW)
    rel_rows = jnp.einsum(
        "akr,rc->akc", offsets_low, rel_low[0], preferred_element_type=SINGLE
    ).astype(NARROW)
    rel_cols = jnp.einsum(
        "akr,rc->akc", offsets_low, rel_low[1], preferred_element_type=SINGLE
    ).astype(NARROW)
    token_rows = tokens.reshape(local_rows, model_width).astype(SINGLE)
    normed_one, scaled_one, inverse_one = normalize(token_rows, segment(0), segment(1))
    gathered_one = lax.all_gather(normed_one.astype(NARROW), "tensor", axis=0, tiled=True)
    projected = jnp.dot(gathered_one, qkv_joined, preferred_element_type=SINGLE)
    query_rows = (projected[:, :head_width] + query_bias).astype(NARROW)
    key_rows = projected[:, head_width : 2 * head_width].astype(NARROW)
    value_rows = (projected[:, 2 * head_width :] + value_bias).astype(NARROW)
    image_query = to_images(query_rows, seq_length, local_images, head_size)
    image_keys = to_images(key_rows, seq_length, local_images, head_size)
    image_values = to_images(value_rows, seq_length, local_images, head_size)

    def forward_image(triple):
        return attend_image(triple[0], triple[1], triple[2], rel_rows, rel_cols)

    contexts, logsums = lax.map(forward_image, (image_query, image_keys, image_values))
    context_rows = from_images(contexts)
    mid_rows = token_rows + (
        lax.psum_scatter(
            jnp.dot(context_rows, out_full, preferred_element_type=SINGLE),
            "tensor",
            scatter_dimension=0,
            tiled=True,
        )
        + segment(4)
    )
    normed_two, scaled_two, inverse_two = normalize(mid_rows, segment(5), segment(6))
    normed_two_low = normed_two.astype(NARROW)
    expand_bias = lax.dynamic_slice_in_dim(
        params_all, 8 * model_width + tensor_index * hidden_width, hidden_width
    )
    gathered_two = lax.all_gather(normed_two_low, "tensor", axis=0, tiled=True)
    hidden_pre = jnp.dot(gathered_two, expand_full, preferred_element_type=SINGLE) + expand_bias
    hidden_low = jax.nn.gelu(hidden_pre, approximate=False).astype(NARROW)
    mlp_sum = lax.psum_scatter(
        jnp.dot(hidden_low, reduce_full, preferred_element_type=SINGLE).astype(jnp.bfloat16),
        "tensor",
        scatter_dimension=0,
        tiled=True,
    ).astype(jnp.float32)
    block_rows = mid_rows + (mlp_sum + segment(7))
    block_out = block_rows.astype(NARROW).reshape(tokens.shape)
    qkv_back, out_back, expand_back, reduce_back = (
        lax.all_gather(qkv_weight.astype(NARROW), "dp", axis=1, tiled=True),
        lax.all_gather(out_weight.astype(NARROW), "dp", axis=1, tiled=True),
        lax.all_gather(expand_weight.astype(NARROW), "dp", axis=0, tiled=True),
        lax.all_gather(reduce_weight.astype(NARROW), "dp", axis=1, tiled=True),
    )
    qkv_back_joined = qkv_back.transpose(1, 0, 2).reshape(model_width, 3 * head_width)
    cotangent_rows = cotangent.reshape(local_rows, model_width)
    grad_block = cotangent_rows.astype(SINGLE)
    grad_reduce_bias = jnp.sum(grad_block, axis=0)
    shard_rows = lax.all_gather(cotangent_rows, "tensor", axis=0, tiled=True)
    part_hidden = contract_cols(shard_rows, reduce_back)
    grad_hidden = part_hidden
    grad_hidden, grad_reduce = (grad_hidden, contract_rows(hidden_low, shard_rows))
    grad_pre = (grad_hidden * gelu_slope(hidden_pre)).astype(NARROW)
    grad_expand = contract_rows(gathered_two, grad_pre)
    grad_expand_bias = jnp.sum(grad_pre, axis=0, dtype=SINGLE)
    expand_bias_full = lax.dynamic_update_slice_in_dim(
        jnp.zeros((hidden_width * tensor_count,), SINGLE),
        grad_expand_bias,
        tensor_index * hidden_width,
        0,
    )
    grad_normed_two = lax.psum_scatter(
        contract_cols(grad_pre, expand_back).astype(jnp.bfloat16),
        "tensor",
        scatter_dimension=0,
        tiled=True,
    ).astype(jnp.float32)
    grad_mid_norm, grad_gain_two, grad_shift_two = normalize_back(
        grad_normed_two, scaled_two, inverse_two, segment(5)
    )
    grad_mid = grad_block + grad_mid_norm
    grad_attn_low = grad_mid.astype(NARROW)
    grad_out_bias = jnp.sum(grad_attn_low, axis=0, dtype=SINGLE)
    shard_rows = lax.all_gather(grad_attn_low, "tensor", axis=0, tiled=True)
    part_context = contract_cols(shard_rows, out_back)
    grad_context = part_context
    grad_context, grad_out = (grad_context, contract_rows(context_rows, shard_rows))
    image_grad = to_images(grad_context.astype(NARROW), seq_length, local_images, head_size)

    def backward_image(group_in):
        return attend_back(
            group_in[0], group_in[1], group_in[2], group_in[3], group_in[4], rel_rows, rel_cols
        )

    query_grads, key_grads, value_grads, rows_grads, cols_grads = lax.map(
        backward_image, (image_query, image_keys, image_values, logsums, image_grad)
    )
    grad_query_rows = from_images(query_grads)
    grad_value_rows = from_images(value_grads)
    grad_qkv_rows = jnp.concatenate(
        [grad_query_rows, from_images(key_grads), grad_value_rows], axis=1
    )
    grad_query_bias = jnp.sum(grad_query_rows, axis=0, dtype=SINGLE)
    grad_value_bias = jnp.sum(grad_value_rows, axis=0, dtype=SINGLE)
    grad_qkv = (
        contract_rows(gathered_one, grad_qkv_rows)
        .reshape(model_width, 3, head_width)
        .transpose(1, 0, 2)
    )
    grad_normed_one = lax.psum_scatter(
        contract_cols(grad_qkv_rows, qkv_back_joined).astype(jnp.bfloat16),
        "tensor",
        scatter_dimension=0,
        tiled=True,
    ).astype(jnp.float32)
    grad_token_norm, grad_gain_one, grad_shift_one = normalize_back(
        grad_normed_one, scaled_one, inverse_one, segment(0)
    )
    token_grad = (grad_mid + grad_token_norm).reshape(tokens.shape)
    table_rows = jnp.einsum(
        "akr,akc->rc", offsets, jnp.sum(rows_grads, axis=0), precision=lax.Precision.HIGHEST
    )
    table_cols = jnp.einsum(
        "akr,akc->rc", offsets, jnp.sum(cols_grads, axis=0), precision=lax.Precision.HIGHEST
    )
    rel_grad = lax.psum(jnp.stack([table_rows, table_cols]), ("dp", "tensor"))
    width_zeros = jnp.zeros((model_width,), SINGLE)
    grad_small = jnp.concatenate(
        [
            grad_gain_one,
            grad_shift_one,
            lax.dynamic_update_slice_in_dim(
                width_zeros, grad_query_bias, tensor_index * head_width, 0
            ),
            lax.dynamic_update_slice_in_dim(
                width_zeros, grad_value_bias, tensor_index * head_width, 0
            ),
            grad_out_bias,
            grad_gain_two,
            grad_shift_two,
            grad_reduce_bias,
            expand_bias_full,
        ]
    )
    gains_grad = lax.psum_scatter(grad_small, ("dp", "tensor"), scatter_dimension=0, tiled=True)
    qkv_grad, out_grad, expand_grad, reduce_grad = (
        lax.psum_scatter(grad_qkv, "dp", scatter_dimension=1, tiled=True),
        lax.psum_scatter(grad_out, "dp", scatter_dimension=1, tiled=True),
        lax.psum_scatter(grad_expand, "dp", scatter_dimension=0, tiled=True),
        lax.psum_scatter(grad_reduce, "dp", scatter_dimension=1, tiled=True),
    )
    new_qkv, moment_qkv, average_qkv = advance(
        qkv_weight, qkv_moment, qkv_average, qkv_grad, RATE_MAIN
    )
    new_out, moment_out, average_out = advance(
        out_weight, out_moment, out_average, out_grad, RATE_MAIN
    )
    new_expand, moment_expand, average_expand = advance(
        expand_weight, expand_moment, expand_average, expand_grad, RATE_MAIN
    )
    new_reduce, moment_reduce, average_reduce = advance(
        reduce_weight, reduce_moment, reduce_average, reduce_grad, RATE_MAIN
    )
    new_gains, moment_gains, average_gains = advance(
        gains_biases, gains_moment, gains_average, gains_grad, RATE_MAIN
    )
    new_rel, moment_rel, average_rel = advance(
        rel_tables, rel_moment, rel_average, rel_grad, RATE_TABLES
    )
    return (
        block_out,
        token_grad,
        qkv_grad,
        out_grad,
        expand_grad,
        reduce_grad,
        gains_grad,
        rel_grad,
        new_qkv,
        new_out,
        new_expand,
        new_reduce,
        new_gains,
        new_rel,
        moment_qkv,
        moment_out,
        moment_expand,
        moment_reduce,
        moment_gains,
        moment_rel,
        average_qkv,
        average_out,
        average_expand,
        average_reduce,
        average_gains,
        average_rel,
    )


def solution(mesh):
    placed = (
        P("tensor", "dp", None),
        P("tensor", "dp", None),
        P(None, "dp", "tensor"),
        P("tensor", "dp"),
        P("dp", "tensor"),
        P("tensor", "dp"),
        P(("dp", "tensor")),
        P(),
        P(None, "dp", "tensor"),
        P("tensor", "dp"),
        P("dp", "tensor"),
        P("tensor", "dp"),
        P(("dp", "tensor")),
        P(),
        P(None, "dp", "tensor"),
        P("tensor", "dp"),
        P("dp", "tensor"),
        P("tensor", "dp"),
        P(("dp", "tensor")),
        P(),
    )
    return jax.shard_map(
        local,
        mesh=mesh,
        in_specs=placed,
        out_specs=(
            P("tensor", "dp", None),
            P("tensor", "dp", None),
            P(None, "dp", "tensor"),
            P("tensor", "dp"),
            P("dp", "tensor"),
            P("tensor", "dp"),
            P(("dp", "tensor")),
            P(),
            P(None, "dp", "tensor"),
            P("tensor", "dp"),
            P("dp", "tensor"),
            P("tensor", "dp"),
            P(("dp", "tensor")),
            P(),
            P(None, "dp", "tensor"),
            P("tensor", "dp"),
            P("dp", "tensor"),
            P("tensor", "dp"),
            P(("dp", "tensor")),
            P(),
            P(None, "dp", "tensor"),
            P("tensor", "dp"),
            P("dp", "tensor"),
            P("tensor", "dp"),
            P(("dp", "tensor")),
            P(),
        ),
        check_vma=False,
    )
```

profile of v0, /device:TPU:0, one launch (start us, length us, event | category | flops | bytes accessed | tf_op | source)
XLA Modules:
  0.0 1512.9 jit_solution(3587377294178821955)
XLA Ops:
  10.2 42.7 %all-reduce = f32[15360]{0:T(1024)S(1)} all-reduce(f32[15360]{0:T(1024)S(1)} %dynamic-update-slice), channel_id=1, replica_groups=mesh['dp'=8,'tensor'=4] {'dp','tensor'}, use_global_device_ids=true, to_apply=%add | all-reduce | flops 15360 | bytes 122880
  58.3 12.7 all_gather.34
  72.2 3.9 copy.120
  76.1 36.6 %all-gather.9.cloned.1.call-done = bf16[1024,1280]{1,0:T(8,128)(2,1)} async-done(((bf16[256,1280]{1,0:T(8,128)(2,1)}), bf16[1024,1280]{1,0:T(8,128)(2,1)}) %all-gather.9.cloned.1.call-update) | async-done | bytes 2621456 | tf_op jit(solution)/shard_map/all_gather | solution.py:236
  112.7 4.5 fusion.118
  121.6 181.6 %while.58 = (s32[]{:T(128)}, bf16[2,512,4,80]{1,3,2,0:T(8,128)(2,1)}, f32[2,4,512]{2,1,0:T(4,128)S(1)}, bf16[2,512,4,80]{3,1,2,0:T(8,128)(2,1)}, bf16[1024,4,80]...) while((s32[]{:T(128)}, ...), condition=%wide.region_5.6_spmd, body=%wide.region_2.5_spmd.sunk | while | flops 708999168 | bytes 105874104 | solution.py:99
  124.8 11.5 add.488
  136.3 26.1 %add.489 = f32[4,512,1024]{2,1,0:T(8,128)} reshape(f32[4,16,32,32,32]{4,3,2,1,0:T(8,128)} %add.488) | data formatting | bytes 16777216 | tf_op jit(solution)/shard_map/while/body/eval_jaxpr/while/body/eval_jaxpr/add | solution.py:76
  163.3 11.1 add.486
  174.4 26.1 %add.487 = f32[4,512,1024]{2,1,0:T(8,128)} reshape(f32[4,16,32,32,32]{4,3,2,1,0:T(8,128)} %add.486) | data formatting | bytes 16777216 | tf_op jit(solution)/shard_map/while/body/eval_jaxpr/while/body/eval_jaxpr/add | solution.py:76
  200.4 7.2 fusion.197
  215.5 11.5 add.488
  226.9 26.1 %add.489 = f32[4,512,1024]{2,1,0:T(8,128)} reshape(f32[4,16,32,32,32]{4,3,2,1,0:T(8,128)} %add.488) | data formatting | bytes 16777216 | tf_op jit(solution)/shard_map/while/body/eval_jaxpr/while/body/eval_jaxpr/add | solution.py:76
  253.9 11.1 add.486
  265.0 26.1 %add.487 = f32[4,512,1024]{2,1,0:T(8,128)} reshape(f32[4,16,32,32,32]{4,3,2,1,0:T(8,128)} %add.486) | data formatting | bytes 16777216 | tf_op jit(solution)/shard_map/while/body/eval_jaxpr/while/body/eval_jaxpr/add | solution.py:76
  291.1 7.2 fusion.197
  305.2 3.9 fusion.119
  311.2 90.8 %reduce-scatter.9.cloned.1.call-done = f32[256,1280]{1,0:T(8,128)} async-done(((f32[1024,1280]{1,0:T(8,128)}), f32[256,1280]{1,0:T(8,128)}) %reduce-scatter.9.cloned.1.call-update) | async-done | bytes 1310736 | tf_op jit(solution)/shard_map/reduce_scatter | solution.py:251
  405.6 31.9 %all-gather.15.cloned.1.call-done = bf16[1280,1280]{1,0:T(8,128)(2,1)} async-done(((bf16[160,1280]{1,0:T(8,128)(2,1)}), bf16[1280,1280]{1,0:T(8,128)(2,1)}) %all-gather.15.cloned.1.call-update) | async-done | bytes 3276816 | tf_op jit(solution)/shard_map/all_gather | solution.py:210
  437.5 56.8 %all-gather.13.cloned.1.call-done = bf16[1024,1280]{1,0:T(8,128)(2,1)} async-done(((bf16[256,1280]{1,0:T(8,128)(2,1)}), bf16[1024,1280]{1,0:T(8,128)(2,1)}) %all-gather.13.cloned.1.call-update) | async-done | bytes 2621456 | tf_op jit(solution)/shard_map/all_gather | solution.py:264
  494.3 17.8 %fusion.56 = (bf16[1024,1280]{1,0:T(8,128)(2,1)}, f32[1024,1280]{1,0:T(8,128)}) fusion(f32[1280]{0:T(1024)S(1)} %copy-done.54, bf16[1024,1280]{1,0:T(8,128)(2,1)} %all-gather.13.cloned.1.call-done, bf16[1280,1280]{1,0:T(8,128)(2,1)} %all-gather.15.cloned.1.call-done), kind=kOutput, calls=%fused_computation.74 | convolution fusion | flops 3441950720 | bytes 13767680 | tf_op jit(solution)/shard_map/dot_general | solution.py:265
  512.1 37.1 %all-gather.21.cloned.1.call-done = bf16[1024,1,1280]{2,0,1:T(8,128)(2,1)} async-done(((bf16[256,1,1280]{2,0,1:T(8,128)(2,1)}), bf16[1024,1,1280]{2,0,1:T(8,128)(2,1)}) %all-gather.21.cloned.1.call-update) | async-done | bytes 2621456 | tf_op jit(solution)/shard_map/all_gather | solution.py:285
  549.2 8.9 fusion.70
  558.2 61.9 %reduce-scatter.23.cloned.1.call-done = f32[1280,160]{0,1:T(8,128)} async-done(((f32[1280,1280]{0,1:T(8,128)}), f32[1280,160]{0,1:T(8,128)}) %reduce-scatter.23.cloned.1.call-update) | async-done | bytes 819216 | tf_op jit(solution)/shard_map/reduce_scatter | solution.py:376
  620.1 4.0 add_multiply_fusion
  624.1 32.8 %all-gather.17.cloned.1.call-done = bf16[1280,1280]{0,1:T(8,128)(2,1)} async-done(((bf16[1280,160]{0,1:T(8,128)(2,1)}), bf16[1280,1280]{0,1:T(8,128)(2,1)}) %all-gather.17.cloned.1.call-update) | async-done | bytes 3276816 | tf_op jit(solution)/shard_map/all_gather | solution.py:211
  657.0 9.1 convert_reduce_fusion
  667.6 4.9 convolution_convert_fusion.1
  672.5 7.9 convolution_convert_fusion.2
  680.5 44.4 %reduce-scatter.13.cloned.1.call-done = bf16[256,1280]{1,0:T(8,128)(2,1)} async-done(((bf16[1024,1280]{1,0:T(8,128)(2,1)}), bf16[256,1280]{1,0:T(8,128)(2,1)}) %reduce-scatter.13.cloned.1.call-update) | async-done | bytes 655376 | tf_op jit(solution)/shard_map/reduce_scatter | solution.py:298
  727.2 51.7 %reduce-scatter.11.cloned.1.call-done = bf16[256,1280]{1,0:T(8,128)(2,1)} async-done(((bf16[1024,1280]{1,0:T(8,128)(2,1)}), bf16[256,1280]{1,0:T(8,128)(2,1)}) %reduce-scatter.11.cloned.1.call-update) | async-done | bytes 655376 | tf_op jit(solution)/shard_map/reduce_scatter | solution.py:267
  778.9 4.1 convert_reduce_fusion.5
  783.1 54.4 %all-gather.19.cloned.1.call-done = bf16[1024,1280]{1,0:T(8,128)(2,1)} async-done(((bf16[256,1280]{1,0:T(8,128)(2,1)}), bf16[1024,1280]{1,0:T(8,128)(2,1)}) %all-gather.19.cloned.1.call-update) | async-done | bytes 2621456 | tf_op jit(solution)/shard_map/all_gather | solution.py:310
  842.8 295.7 %while.59 = (s32[]{:T(128)}, f32[1024,4,80]{0,2,1:T(8,128)}, f32[1024,4,80]{0,2,1:T(8,128)}, f32[32,32,80]{2,1,0:T(8,128)}, bf16[2,512,4,80]{1,3,2,0:T(8,128)(2,...) while((s32[]{:T(128)}, f32[1024,4,80]{0,2,1:T(8,128)}, ...), condition=%wide.region_17.18_spmd.clone, body=%wide.region_13.17_spmd.clone.sunk | while | flops 1768126464 | bytes 221555152 | solution.py:157
  847.0 11.5 add.498
  858.5 26.1 %add.499 = f32[4,512,1024]{2,1,0:T(8,128)} reshape(f32[4,16,32,32,32]{4,3,2,1,0:T(8,128)} %add.498) | data formatting | bytes 16777216 | tf_op jit(solution)/shard_map/while/body/eval_jaxpr/while/body/eval_jaxpr/add | solution.py:76
  885.5 11.1 add.496
  896.6 26.2 %add.497 = f32[4,512,1024]{2,1,0:T(8,128)} reshape(f32[4,16,32,32,32]{4,3,2,1,0:T(8,128)} %add.496) | data formatting | bytes 16777216 | tf_op jit(solution)/shard_map/while/body/eval_jaxpr/while/body/eval_jaxpr/add | solution.py:76
  924.1 7.8 multiply_reduce_fusion.3
  937.5 20.3 %reshape.264 = bf16[4,16,32,32,32]{4,3,2,1,0:T(8,128)(2,1)} reshape(bf16[4,512,1024]{2,1,0:T(8,128)(2,1)} %multiply_convert_fusion.2) | data formatting | bytes 8388608 | tf_op jit(solution)/shard_map/while/body/eval_jaxpr/while/body/eval_jaxpr/reshape | solution.py:127
  957.8 12.7 fusion.223
  973.7 4.8 fusion.227
  980.7 3.4 fusion.221
  984.1 5.8 fusion.222
  994.0 11.5 add.498
  1005.5 26.1 %add.499 = f32[4,512,1024]{2,1,0:T(8,128)} reshape(f32[4,16,32,32,32]{4,3,2,1,0:T(8,128)} %add.498) | data formatting | bytes 16777216 | tf_op jit(solution)/shard_map/while/body/eval_jaxpr/while/body/eval_jaxpr/add | solution.py:76
  1032.5 11.1 add.496
  1043.6 26.2 %add.497 = f32[4,512,1024]{2,1,0:T(8,128)} reshape(f32[4,16,32,32,32]{4,3,2,1,0:T(8,128)} %add.496) | data formatting | bytes 16777216 | tf_op jit(solution)/shard_map/while/body/eval_jaxpr/while/body/eval_jaxpr/add | solution.py:76
  1071.1 7.8 multiply_reduce_fusion.3
  1084.5 20.3 %reshape.264 = bf16[4,16,32,32,32]{4,3,2,1,0:T(8,128)(2,1)} reshape(bf16[4,512,1024]{2,1,0:T(8,128)(2,1)} %multiply_convert_fusion.2) | data formatting | bytes 8388608 | tf_op jit(solution)/shard_map/while/body/eval_jaxpr/while/body/eval_jaxpr/reshape | solution.py:127
  1104.8 12.7 fusion.223
  1120.7 4.8 fusion.227
  1128.7 3.4 fusion.221
  1132.1 6.1 fusion.222
  1143.0 4.3 convolution_convert_fusion
  1147.4 8.9 fusion.121
  1157.4 4.7 fusion.120
  1166.4 32.1 %reduce-scatter.15.cloned.1.call-done = bf16[256,1280]{1,0:T(8,128)(2,1)} async-done(((bf16[1024,1280]{1,0:T(8,128)(2,1)}), bf16[256,1280]{1,0:T(8,128)(2,1)}) %reduce-scatter.15.cloned.1.call-update) | async-done | bytes 655376 | tf_op jit(solution)/shard_map/reduce_scatter | solution.py:336
  1201.4 6.8 fusion.101
  1208.3 7.6 copy.127
  1215.9 49.2 %reduce-scatter.21.cloned.1.call-done = f32[160,1280]{1,0:T(8,128)} async-done(((f32[1280,1280]{1,0:T(8,128)}), f32[160,1280]{1,0:T(8,128)}) %reduce-scatter.21.cloned.1.call-update) | async-done | bytes 819216 | tf_op jit(solution)/shard_map/reduce_scatter | solution.py:375
  1268.4 40.8 %reduce-scatter.19.cloned.1.call-done = f32[320,160]{0,1:T(8,128)} async-done(((f32[320,1280]{0,1:T(8,128)}), f32[320,160]{0,1:T(8,128)}) %reduce-scatter.19.cloned.1.call-update) | async-done | bytes 204816 | tf_op jit(solution)/shard_map/reduce_scatter | solution.py:374
  1314.4 125.9 %all-reduce.5.cloned.1.call-done = (f32[15360]{0:T(1024)}, f32[2,63,80]{2,1,0:T(8,128)}) async-done(((f32[15360]{0:T(1024)}, f32[2,63,80]{2,1,0:T(8,128)}), (f32[15360]{0:T(1024)}, f32[2,63,80]{2,1,0:T(8,128)})) %all-reduce.5.cloned.1.call-update) | async-done | bytes 101776
  1446.1 57.4 %reduce-scatter.17.cloned.1.call-done = f32[3,160,320]{2,1,0:T(8,128)} async-done(((f32[3,1280,320]{2,1,0:T(8,128)}), f32[3,160,320]{2,1,0:T(8,128)}) %reduce-scatter.17.cloned.1.call-update) | async-done | bytes 614416 | tf_op jit(solution)/shard_map/reduce_scatter | solution.py:373
  (304 shorter events, 113.3 us)
Async XLA Ops:
  7.2 49.7 %copy-start.12 = (bf16[256,1,1280]{2,0,1:T(8,128)(2,1)S(1)}, bf16[256,1,1280]{2,0,1:T(8,128)(2,1)}, u32[]{:S(2)}) copy-start(bf16[256,1,1280]{2,0,1:T(8,128)(2,1)} %param.24) | copy-start | bytes 1966084
  7.2 51.0 %copy-start.37 = (f32[2,63,80]{2,0,1:T(2,128)S(1)}, f32[2,63,80]{2,0,1:T(2,128)}, u32[]{:S(2)}) copy-start(f32[2,63,80]{2,0,1:T(2,128)} %param.31) | copy-start | bytes 120964
  7.2 51.0 %copy-start.31 = (f32[320,160]{0,1:T(8,128)S(1)}, f32[320,160]{0,1:T(8,128)}, u32[]{:S(2)}) copy-start(f32[320,160]{0,1:T(8,128)} %param.27) | copy-start | bytes 614404
  7.2 65.0 %all-gather.11.cloned.1.call-start = ((), (), s32[]{:S(2)}) async-start(), calls=%async_computation.9 | async-start | bytes 3317760 | tf_op jit(solution)/shard_map/all_gather | solution.py:208
  9.3 103.4 %all-gather.9.cloned.1.call-start = ((), (), s32[]{:S(2)}) async-start(), calls=%async_computation.8 | async-start | bytes 3276800 | tf_op jit(solution)/shard_map/all_gather | solution.py:236
  58.1 343.8 %reduce-scatter.9.cloned.1.call-start = ((), (), s32[]{:S(2)}) async-start(), calls=%async_computation.10 | async-start | bytes 6553600 | tf_op jit(solution)/shard_map/reduce_scatter | solution.py:251
  76.1 36.6 %copy-start.29 = (bf16[3,1280,320]{1,2,0:T(8,128)(2,1)}, bf16[3,1280,320]{1,2,0:T(8,128)(2,1)S(1)}, u32[]{:S(2)}) copy-start(bf16[3,1280,320]{1,2,0:T(8,128)(2,1)S(1)} %copy.120) | copy-start | bytes 7372804
  305.2 3.9 copy-start.20
  309.1 92.8 %copy-start.13 = (bf16[256,1,1280]{2,0,1:T(8,128)(2,1)S(1)}, bf16[256,1,1280]{2,0,1:T(8,128)(2,1)}, u32[]{:S(2)}) copy-start(bf16[256,1,1280]{2,0,1:T(8,128)(2,1)} %param.24) | copy-start | bytes 1966084
  309.1 92.8 %copy-start.46 = (f32[1280]{0:T(1024)S(1)}, f32[1280]{0:T(1024)}, u32[]{:S(2)}) copy-start(f32[1280]{0:T(1024)} %get-tuple-element.613) | copy-start | bytes 15364
  309.2 94.6 %copy-start.39 = (f32[1280]{0:T(1024)S(1)}, f32[1280]{0:T(1024)}, u32[]{:S(2)}) copy-start(f32[1280]{0:T(1024)} %get-tuple-element.612) | copy-start | bytes 15364
  309.2 94.6 %copy-start.45 = (f32[1280]{0:T(1024)S(1)}, f32[1280]{0:T(1024)}, u32[]{:S(2)}) copy-start(f32[1280]{0:T(1024)} %get-tuple-element.611) | copy-start | bytes 15364
  309.2 128.3 %all-gather.15.cloned.1.call-start = ((), (), s32[]{:S(2)}) async-start(), calls=%async_computation.12 | async-start | bytes 3686400 | tf_op jit(solution)/shard_map/all_gather | solution.py:210
  311.1 183.1 %all-gather.13.cloned.1.call-start = ((), (), s32[]{:S(2)}) async-start(), calls=%async_computation.11 | async-start | bytes 3276800 | tf_op jit(solution)/shard_map/all_gather | solution.py:264
  401.9 92.3 %copy-start.54 = (f32[1280]{0:T(1024)S(1)}, f32[1280]{0:T(1024)}, u32[]{:S(2)}) copy-start(f32[1280]{0:T(1024)} %get-tuple-element.610) | copy-start | bytes 15364
  405.0 144.2 %all-gather.21.cloned.1.call-start = ((), (), s32[]{:S(2)}) async-start(), calls=%async_computation.22 | async-start | bytes 3276800 | tf_op jit(solution)/shard_map/all_gather | solution.py:285
  405.6 214.5 %reduce-scatter.23.cloned.1.call-start = ((), (), s32[]{:S(2)}) async-start(), calls=%async_computation.21 | async-start | bytes 7372800 | tf_op jit(solution)/shard_map/reduce_scatter | solution.py:376
  558.1 98.8 %all-gather.17.cloned.1.call-start = ((), (), s32[]{:S(2)}) async-start(), calls=%async_computation.13 | async-start | bytes 3686400 | tf_op jit(solution)/shard_map/all_gather | solution.py:211
  624.1 100.8 %reduce-scatter.13.cloned.1.call-start = ((), (), s32[]{:S(2)}) async-start(), calls=%async_computation.15 | async-start | bytes 3276800 | tf_op jit(solution)/shard_map/reduce_scatter | solution.py:298
  657.0 10.6 copy-start.59
  672.5 106.4 %reduce-scatter.11.cloned.1.call-start = ((), (), s32[]{:S(2)}) async-start(), calls=%async_computation.14 | async-start | bytes 3276800 | tf_op jit(solution)/shard_map/reduce_scatter | solution.py:267
  680.4 98.5 %copy-start.16 = (bf16[256,1,1280]{2,0,1:T(8,128)(2,1)S(1)}, bf16[256,1,1280]{2,0,1:T(8,128)(2,1)}, u32[]{:S(2)}) copy-start(bf16[256,1,1280]{2,0,1:T(8,128)(2,1)} %param.25) | copy-start | bytes 1966084
  680.4 98.5 %copy-start.44 = (f32[1280]{0:T(1024)S(1)}, f32[1280]{0:T(1024)}, u32[]{:S(2)}) copy-start(f32[1280]{0:T(1024)} %get-tuple-element.609) | copy-start | bytes 15364
  680.4 157.0 %all-gather.19.cloned.1.call-start = ((), (), s32[]{:S(2)}) async-start(), calls=%async_computation.16 | async-start | bytes 3276800 | tf_op jit(solution)/shard_map/all_gather | solution.py:310
  783.0 415.5 %reduce-scatter.15.cloned.1.call-start = ((), (), s32[]{:S(2)}) async-start(), calls=%async_computation.17 | async-start | bytes 3276800 | tf_op jit(solution)/shard_map/reduce_scatter | solution.py:336
  858.5 26.1 %copy-start.9 = (bf16[32,32,80]{2,1,0:T(8,128)(2,1)S(1)}, bf16[32,32,80]{2,1,0:T(8,128)(2,1)}, u32[]{:S(2)}) copy-start(bf16[32,32,80]{2,1,0:T(8,128)(2,1)} %copy-done.8) | copy-start | bytes 491524 | tf_op jit(solution)/shard_map/while/body/eval_jaxpr/while
  896.6 26.2 %copy-start.7 = (bf16[1024,4,80]{0,2,1:T(8,128)(2,1)S(1)}, bf16[1024,4,80]{0,2,1:T(8,128)(2,1)}, u32[]{:S(2)}) copy-start(bf16[1024,4,80]{0,2,1:T(8,128)(2,1)} %get-tuple-element.837) | copy-start | bytes 1966084 | tf_op jit(solution)/shard_map/while/body/eval_jaxpr/while
  896.6 26.2 %copy-start.10 = (bf16[2,512,4,80]{1,3,2,0:T(8,128)(2,1)S(1)}, bf16[2,512,4,80]{1,3,2,0:T(8,128)(2,1)}, u32[]{:S(2)}) copy-start(bf16[2,512,4,80]{1,3,2,0:T(8,128)(2,1)} %get-tuple-element.836) | copy-start | bytes 1966084 | tf_op jit(solution)/shard_map/while/body/eval_jaxpr/while
  973.7 7.0 copy-start.3
  984.1 5.8 copy-start.4
  984.1 5.8 copy-start.2
  1005.5 26.1 %copy-start.9 = (bf16[32,32,80]{2,1,0:T(8,128)(2,1)S(1)}, bf16[32,32,80]{2,1,0:T(8,128)(2,1)}, u32[]{:S(2)}) copy-start(bf16[32,32,80]{2,1,0:T(8,128)(2,1)} %copy-done.8) | copy-start | bytes 491524 | tf_op jit(solution)/shard_map/while/body/eval_jaxpr/while
  1043.6 26.2 %copy-start.7 = (bf16[1024,4,80]{0,2,1:T(8,128)(2,1)S(1)}, bf16[1024,4,80]{0,2,1:T(8,128)(2,1)}, u32[]{:S(2)}) copy-start(bf16[1024,4,80]{0,2,1:T(8,128)(2,1)} %get-tuple-element.837) | copy-start | bytes 1966084 | tf_op jit(solution)/shard_map/while/body/eval_jaxpr/while
  1043.6 26.2 %copy-start.10 = (bf16[2,512,4,80]{1,3,2,0:T(8,128)(2,1)S(1)}, bf16[2,512,4,80]{1,3,2,0:T(8,128)(2,1)}, u32[]{:S(2)}) copy-start(bf16[2,512,4,80]{1,3,2,0:T(8,128)(2,1)} %get-tuple-element.836) | copy-start | bytes 1966084 | tf_op jit(solution)/shard_map/while/body/eval_jaxpr/while
  1120.7 8.1 copy-start.3
  1132.1 6.1 copy-start.4
  1132.1 6.1 copy-start.2
  1138.5 4.6 copy-start.30
  1147.4 117.8 %reduce-scatter.21.cloned.1.call-start = ((), (), s32[]{:S(2)}) async-start(), calls=%async_computation.20 | async-start | bytes 7372800 | tf_op jit(solution)/shard_map/reduce_scatter | solution.py:375
  1156.3 5.9 copy-start.17
  1156.3 6.0 copy-start.56
  1156.4 6.3 copy-start.18
  1156.4 152.8 %reduce-scatter.19.cloned.1.call-start = ((), (), s32[]{:S(2)}) async-start(), calls=%async_computation.19 | async-start | bytes 2211840 | tf_op jit(solution)/shard_map/reduce_scatter | solution.py:374
  1162.1 36.5 %copy-start.14 = (bf16[256,1,1280]{2,0,1:T(8,128)(2,1)S(1)}, bf16[256,1,1280]{2,0,1:T(8,128)(2,1)}, u32[]{:S(2)}) copy-start(bf16[256,1,1280]{2,0,1:T(8,128)(2,1)} %param.24) | copy-start | bytes 1966084
  1162.1 36.5 %copy-start.41 = (f32[1280]{0:T(1024)S(1)}, f32[1280]{0:T(1024)}, u32[]{:S(2)}) copy-start(f32[1280]{0:T(1024)} %copy-done.40) | copy-start | bytes 15364
  1162.1 36.5 %copy-start.51 = (f32[256]{0:T(256)S(1)}, f32[256]{0:T(256)}, u32[]{:S(2)}) copy-start(f32[256]{0:T(256)} %copy-done.50) | copy-start | bytes 3076
  1162.1 36.5 %copy-start.53 = (f32[256]{0:T(256)S(1)}, f32[256]{0:T(256)}, u32[]{:S(2)}) copy-start(f32[256]{0:T(256)} %copy-done.52) | copy-start | bytes 3076
  1162.1 38.3 %copy-start.49 = (f32[1280]{0:T(1024)S(1)}, f32[1280]{0:T(1024)}, u32[]{:S(2)}) copy-start(f32[1280]{0:T(1024)} %get-tuple-element.593) | copy-start | bytes 15364
  1162.1 38.3 %copy-start.48 = (f32[1280]{0:T(1024)S(1)}, f32[1280]{0:T(1024)}, u32[]{:S(2)}) copy-start(f32[1280]{0:T(1024)} %get-tuple-element.521) | copy-start | bytes 15364
  1162.1 38.3 %copy-start.47 = (f32[1280]{0:T(1024)S(1)}, f32[1280]{0:T(1024)}, u32[]{:S(2)}) copy-start(f32[1280]{0:T(1024)} %get-tuple-element.527) | copy-start | bytes 15364
  1162.1 278.1 %all-reduce.5.cloned.1.call-start = ((), (), s32[]{:S(2)}) async-start(), calls=%async_computation.23 | async-start | bytes 253952
  1162.3 39.1 %copy-start.35 = (bf16[1024,4,80]{0,2,1:T(8,128)(2,1)S(1)}, bf16[1024,4,80]{0,2,1:T(8,128)(2,1)}, u32[]{:S(2)}) copy-start(bf16[1024,4,80]{0,2,1:T(8,128)(2,1)} %copy-done.34) | copy-start | bytes 1966084
  1201.1 302.4 %reduce-scatter.17.cloned.1.call-start = ((), (), s32[]{:S(2)}) async-start(), calls=%async_computation.18 | async-start | bytes 6635520 | tf_op jit(solution)/shard_map/reduce_scatter | solution.py:373
  1215.9 49.3 %copy-start.24 = (f32[160,1280]{1,0:T(8,128)S(1)}, f32[160,1280]{1,0:T(8,128)}, u32[]{:S(2)}) copy-start(f32[160,1280]{1,0:T(8,128)} %param.28) | copy-start | bytes 2457604
  1215.9 95.5 %copy-start.19 = (f32[256,1280]{1,0:T(8,128)S(1)}, f32[256,1280]{1,0:T(8,128)}, u32[]{:S(2)}) copy-start(f32[256,1280]{1,0:T(8,128)} %get-tuple-element.595) | copy-start | bytes 3932164
  1215.9 95.5 %copy-start.28 = (bf16[256,1280]{1,0:T(8,128)(2,1)S(1)}, bf16[256,1280]{1,0:T(8,128)(2,1)}, u32[]{:S(2)}) copy-start(bf16[256,1280]{1,0:T(8,128)(2,1)} %reduce-scatter.15.cloned.1.call-done) | copy-start | bytes 1966084
  1311.4 130.4 %copy-start.38 = (f32[2,63,80]{2,0,1:T(2,128)S(1)}, f32[2,63,80]{2,0,1:T(2,128)}, u32[]{:S(2)}) copy-start(f32[2,63,80]{2,0,1:T(2,128)} %param.31) | copy-start | bytes 120964
  1311.4 130.4 %copy-start.42 = (f32[2,63,80]{2,0,1:T(2,128)S(1)}, f32[2,63,80]{2,0,1:T(2,128)}, u32[]{:S(2)}) copy-start(f32[2,63,80]{2,0,1:T(2,128)} %param.43) | copy-start | bytes 120964
  1311.4 133.3 %copy-start.55 = (f32[480]{0:T(512)S(1)}, f32[480]{0:T(512)}, u32[]{:S(2)}) copy-start(f32[480]{0:T(512)} %param.30) | copy-start | bytes 5764
  1311.4 133.3 %copy-start.57 = (f32[480]{0:T(512)S(1)}, f32[480]{0:T(512)}, u32[]{:S(2)}) copy-start(f32[480]{0:T(512)} %param.42) | copy-start | bytes 5764
  1311.5 133.3 %copy-start.58 = (f32[480]{0:T(512)S(1)}, f32[480]{0:T(512)}, u32[]{:S(2)}) copy-start(f32[480]{0:T(512)} %param.36) | copy-start | bytes 5764
  1311.5 192.0 %copy-start.25 = (f32[3,160,320]{2,1,0:T(8,128)S(1)}, f32[3,160,320]{2,1,0:T(8,128)}, u32[]{:S(2)}) copy-start(f32[3,160,320]{2,1,0:T(8,128)} %param.26) | copy-start | bytes 1843204
  1312.0 191.5 %copy-start.32 = (f32[3,160,320]{2,1,0:T(8,128)S(1)}, f32[3,160,320]{2,1,0:T(8,128)}, u32[]{:S(2)}) copy-start(f32[3,160,320]{2,1,0:T(8,128)} %param.38) | copy-start | bytes 1843204
  1312.0 191.5 %copy-start.33 = (f32[3,160,320]{2,1,0:T(8,128)S(1)}, f32[3,160,320]{2,1,0:T(8,128)}, u32[]{:S(2)}) copy-start(f32[3,160,320]{2,1,0:T(8,128)} %param.32) | copy-start | bytes 1843204
  (26 other events, 44.7 us)
Sparse Core Ops, SparseCore 0:
  10.5 34.3 all-gather.10
  58.2 54.4 all-gather.8
  309.3 92.5 reduce-scatter.8
  404.2 33.2 all-gather.14
  439.5 54.7 all-gather.12
  495.7 53.5 all-gather.20
  558.3 61.7 reduce-scatter.22
  624.2 32.7 all-gather.16
  672.6 52.2 reduce-scatter.12
  727.0 51.8 reduce-scatter.10
  783.1 54.2 all-gather.18
  1147.5 51.0 reduce-scatter.14
  1202.6 62.5 reduce-scatter.20
  1269.0 40.1 reduce-scatter.18
  1315.9 124.2 all-reduce.4
  1444.2 59.2 reduce-scatter.16
where the time goes:
time: 1520 us; the launch traced here: 1510 us
  waiting for transfers between devices  805 us (53%)
  local copies, waits for them, and re-layouts  396 us (26%)
  matrix products  170 us (11%)
  other arithmetic  70 us (5%)
  blocking collectives  55.4 us (4%)
    add x16, local copies, waits for them, and re-layouts, block_scores(): scores = scores + row_bias[..., :, None] + col_bias[..., None, :]  299 us
    unnamed x17, waiting for transfers between devices  127 us
    reduce_scatter x1, waiting for transfers between devices, local(): lax.psum_scatter(jnp.dot(context_rows, out_full, preferred_element_type=S...  90.8 us
    reduce_scatter x1, waiting for transfers between devices, local(): lax.psum_scatter(grad_reduce, 'dp', scatter_dimension=1, tiled=True)  61.9 us
    reduce_scatter x1, waiting for transfers between devices, local(): lax.psum_scatter(grad_qkv, 'dp', scatter_dimension=1, tiled=True)  57.4 us
    all_gather x1, waiting for transfers between devices, local(): gathered_two = lax.all_gather(normed_two_low, 'tensor', axis=0, tiled=True)  56.8 us
    all_gather x1, waiting for transfers between devices, local(): shard_rows = lax.all_gather(grad_attn_low, 'tensor', axis=0, tiled=True)  54.4 us
    reduce_scatter x1, waiting for transfers between devices, local(): lax.psum_scatter(jnp.dot(hidden_low, reduce_full, preferred_element_type=...  51.7 us
  transfers between devices with their start and end apart: 16, of which 15 were waited for; matrix products, arithmetic and copies ran while one was open for 6% of the time, Pallas kernels for 0%

commit v1 on v0

v1 whole, which is shorter than its diff:
```python
import functools
import jax
import jax.numpy as jnp
from jax import lax
from jax.experimental import pallas as pl
from jax.experimental.pallas import tpu as pltpu
from jax.sharding import PartitionSpec as P

EPSILON = 1e-06
MOMENTUM = 0.5
AVERAGING = 0.5
RATE_MAIN = 0.0003
RATE_TABLES = 0.01
NARROW = jnp.bfloat16
SINGLE = jnp.float32


def normalize(values, gain_row, shift_row):
    center = values - jnp.mean(values, axis=-1, keepdims=True)
    inverse = lax.rsqrt(jnp.mean(center * center, axis=-1, keepdims=True) + EPSILON)
    scaled = center * inverse
    return (scaled * gain_row + shift_row, scaled, inverse)


def normalize_back(grad_output, scaled, inverse, gain_row):
    grad_scaled = grad_output * gain_row
    mean_plain = jnp.mean(grad_scaled, axis=-1, keepdims=True)
    mean_cross = jnp.mean(grad_scaled * scaled, axis=-1, keepdims=True)
    grad_values = inverse * (grad_scaled - mean_plain - scaled * mean_cross)
    return (grad_values, jnp.sum(grad_output * scaled, axis=0), jnp.sum(grad_output, axis=0))


def gelu_slope(values):
    cumulative = 0.5 * (1.0 + lax.erf(values * 0.7071067811865476))
    density = 0.3989422804014327 * jnp.exp(-0.5 * values * values)
    return cumulative + values * density


def contract_rows(left_side, right_side):
    return lax.dot_general(
        left_side, right_side, (((0,), (0,)), ((), ())), preferred_element_type=SINGLE
    )


def contract_cols(left_side, right_side):
    return lax.dot_general(
        left_side, right_side, (((1,), (1,)), ((), ())), preferred_element_type=SINGLE
    )


def dot_nt(left, right):
    return lax.dot_general(left, right, (((1,), (1,)), ((), ())), preferred_element_type=SINGLE)


def dot_tn(left, right):
    return lax.dot_general(left, right, (((0,), (0,)), ((), ())), preferred_element_type=SINGLE)


def dot_nn(left, right):
    return lax.dot_general(left, right, (((1,), (0,)), ((), ())), preferred_element_type=SINGLE)


def forward_kernel(
    heads, size, grid_side, block, qkv_ref, table_ref, hot_ref,
    out_ref, bias_ref, lse_ref, query_ext, key_ext, bias_wide, context_t,
):
    seq = qkv_ref.shape[0]
    width = heads * size
    scale = size ** (-0.5)
    lane = lax.broadcasted_iota(jnp.int32, (grid_side, 128), 1)
    query_ext[:, 0:128] = jnp.zeros((seq, 128), NARROW)
    key_ext[:, 0:128] = jnp.zeros((seq, 128), NARROW)
    key_ext[:, 128:256] = hot_ref[...]
    for head in range(heads):
        low = head * size
        query = qkv_ref[:, low : low + size]
        value = qkv_ref[:, 2 * width + low : 2 * width + low + size]
        query_ext[:, 0:size] = query
        key_ext[:, 0:size] = qkv_ref[:, width + low : width + low + size]
        bias_wide[...] = dot_nt(query, table_ref[...])
        for row in range(grid_side):
            rows = pl.ds(row * grid_side, grid_side)
            group = bias_wide[rows, :]
            part_row = pltpu.roll(group, (128 - grid_side + 1 + row) % 128, 1)
            part_col = pltpu.roll(group, 65 - 32 + grid_side, 1, stride=1, stride_axis=0)
            both = jnp.where(
                lane < grid_side, part_row, jnp.where(lane < 2 * grid_side, part_col, 0.0)
            ) * (size ** 0.5)
            high = both.astype(NARROW).astype(SINGLE)
            rest = pltpu.roll(both - high, 64, 1)
            mixed = jnp.where(lane < 64, high, rest).astype(NARROW)
            query_ext[rows, 128:256] = mixed
        bias_ref[head] = query_ext[:, 128:256]
        for start in range(0, seq, block):
            scores = dot_nt(key_ext[...], query_ext[start : start + block, :])
            highest = jnp.max(scores, axis=0, keepdims=True)
            powers = jnp.exp((scores - highest) * scale)
            total = jnp.sum(powers, axis=0, keepdims=True)
            weights = (powers * (1.0 / total)).astype(NARROW)
            lse_ref[head, :, start : start + block] = highest * scale + jnp.log(total)
            context_t[low : low + size, start : start + block] = dot_tn(value, weights)
    out_ref[...] = context_t[...].T.astype(NARROW)


def backward_kernel(
    heads, size, grid_side, block, qkv_ref, grad_ref, bias_ref, lse_ref, table_ref, hot_ref, rev_ref,
    out_ref, rel_ref, query_ext, key_ext, key_rev, spread, grad_keys, grad_values, grad_query,
):
    seq = qkv_ref.shape[0]
    width = heads * size
    scale = size ** (-0.5)
    lane = lax.broadcasted_iota(jnp.int32, (grid_side, 128), 1)
    query_ext[:, 0:128] = jnp.zeros((seq, 128), NARROW)
    key_ext[:, 0:128] = jnp.zeros((seq, 128), NARROW)
    key_ext[:, 128:256] = hot_ref[...]
    key_rev[:, 0:128] = jnp.zeros((seq, 128), NARROW)
    key_rev[:, 128:256] = rev_ref[...]
    rel_total = jnp.zeros(rel_ref.shape, SINGLE)
    for head in range(heads):
        low = head * size
        query = qkv_ref[:, low : low + size]
        key = qkv_ref[:, width + low : width + low + size]
        value = qkv_ref[:, 2 * width + low : 2 * width + low + size]
        grad = grad_ref[:, low : low + size]
        query_ext[:, 0:size] = query
        query_ext[:, 128:256] = bias_ref[head]
        key_ext[:, 0:size] = key
        key_rev[:, 0:size] = key
        for start in range(0, seq, block):
            part = slice(start, start + block)
            scores = dot_nt(key_ext[...], query_ext[part, :])
            soft = jnp.exp(scores * scale - lse_ref[head, :, part])
            grad_part = grad[part]
            grad_soft = dot_nt(value, grad_part)
            inner = jnp.sum(soft * grad_soft, axis=0, keepdims=True)
            grad_scores = (soft * (grad_soft - inner)).astype(NARROW)
            add_values = dot_nn(soft.astype(NARROW), grad_part)
            add_keys = dot_nn(grad_scores, query[part])
            if start == 0:
                grad_values[...] = add_values
                grad_keys[...] = add_keys
            else:
                grad_values[...] += add_values
                grad_keys[...] += add_keys
            turned = dot_tn(key_rev[...], grad_scores).T
            grad_query[part, :] = turned[:, 0:128]
            sums = turned[:, 128:256].astype(NARROW).astype(SINGLE)
            for inside in range(block // grid_side):
                row = start // grid_side + inside
                group = sums[inside * grid_side : (inside + 1) * grid_side]
                part_row = jnp.where(lane < grid_side, group, 0.0)
                part_col = jnp.where((lane >= grid_side) & (lane < 2 * grid_side), group, 0.0)
                if row:
                    part_row = pltpu.roll(part_row, row, 1)
                part_col = pltpu.roll(part_col, 64 - grid_side, 1, stride=1, stride_axis=0)
                spread[row * grid_side : (row + 1) * grid_side, :] = (part_row + part_col).astype(NARROW)
        total_query = grad_query[:, 0:size] * scale + dot_nn(spread[...], table_ref[...])
        out_ref[:, low : low + size] = total_query.astype(NARROW)
        out_ref[:, width + low : width + low + size] = (grad_keys[...] * scale).astype(NARROW)
        out_ref[:, 2 * width + low : 2 * width + low + size] = grad_values[...].astype(NARROW)
        rel_total = rel_total + dot_tn(spread[...], query)
    rel_ref[...] = rel_total


def attention_tables(rel_low, grid_side):
    offsets = rel_low.shape[1]
    pad = ((0, 0), (0, 64 - offsets), (0, 0))
    plain = jnp.pad(rel_low, pad).reshape(128, -1)
    turned = jnp.pad(rel_low[:, ::-1], pad).reshape(128, -1)
    seq = grid_side * grid_side
    token = lax.broadcasted_iota(jnp.int32, (seq, 128), 0)
    lane = lax.broadcasted_iota(jnp.int32, (seq, 128), 1)
    inside = lane % 64
    row, col = (token // grid_side, token % grid_side)
    hot = jnp.where(inside < grid_side, inside == row, inside - grid_side == col)
    hot = (hot & (inside < 2 * grid_side)).astype(NARROW)
    back = jnp.where(lane < grid_side, grid_side - 1 - lane == row, 2 * grid_side - 1 - lane == col)
    back = (back & (lane < 2 * grid_side)).astype(NARROW)
    return plain, turned, hot, back


def whole_vmem(count):
    return [pl.BlockSpec(memory_space=pltpu.VMEM)] * count


def attend_forward(qkv_rows, turned, hot, heads, size, grid_side):
    seq = qkv_rows.shape[0]
    block = min(256, seq)
    return pl.pallas_call(
        functools.partial(forward_kernel, heads, size, grid_side, block),
        out_shape=(
            jax.ShapeDtypeStruct((seq, heads * size), NARROW),
            jax.ShapeDtypeStruct((heads, seq, 128), NARROW),
            jax.ShapeDtypeStruct((heads, 1, seq), SINGLE),
        ),
        in_specs=whole_vmem(3),
        out_specs=tuple(whole_vmem(3)),
        scratch_shapes=[
            pltpu.VMEM((seq, 256), NARROW),
            pltpu.VMEM((seq, 256), NARROW),
            pltpu.VMEM((seq, 128), SINGLE),
            pltpu.VMEM((heads * size, seq), SINGLE),
        ],
        compiler_params=pltpu.CompilerParams(vmem_limit_bytes=40 << 20),
        name="attend_forward",
    )(qkv_rows, turned, hot)


def attend_backward(qkv_rows, grad_rows, bias, lse, plain, hot, back, heads, size, grid_side):
    seq = qkv_rows.shape[0]
    block = min(256, seq)
    return pl.pallas_call(
        functools.partial(backward_kernel, heads, size, grid_side, block),
        out_shape=(
            jax.ShapeDtypeStruct((seq, 3 * heads * size), NARROW),
            jax.ShapeDtypeStruct((128, size), SINGLE),
        ),
        in_specs=whole_vmem(7),
        out_specs=tuple(whole_vmem(2)),
        scratch_shapes=[
            pltpu.VMEM((seq, 256), NARROW),
            pltpu.VMEM((seq, 256), NARROW),
            pltpu.VMEM((seq, 256), NARROW),
            pltpu.VMEM((seq, 128), NARROW),
            pltpu.VMEM((seq, size), SINGLE),
            pltpu.VMEM((seq, size), SINGLE),
            pltpu.VMEM((seq, 128), SINGLE),
        ],
        compiler_params=pltpu.CompilerParams(vmem_limit_bytes=48 << 20),
        name="attend_backward",
    )(qkv_rows, grad_rows, bias, lse, plain, hot, back)


TILE = 1024


def as_tiles(vector):
    return jnp.pad(vector, (0, TILE - vector.shape[0])).reshape(8, 128)


def advance(weight, moment, average, gradient, rate_value):
    new_moment = MOMENTUM * moment + gradient
    new_weight = weight - rate_value * (gradient + MOMENTUM * new_moment)
    new_average = AVERAGING * average + (1.0 - AVERAGING) * new_weight
    return (new_weight, new_moment, new_average)


def local(
    tokens,
    cotangent,
    qkv_weight,
    out_weight,
    expand_weight,
    reduce_weight,
    gains_biases,
    rel_tables,
    qkv_moment,
    out_moment,
    expand_moment,
    reduce_moment,
    gains_moment,
    rel_moment,
    qkv_average,
    out_average,
    expand_average,
    reduce_average,
    gains_average,
    rel_average,
):
    local_seq, local_images, model_width = tokens.shape
    tensor_count = lax.axis_size("tensor")
    tensor_index = lax.axis_index("tensor")
    local_rows = local_seq * local_images
    seq_length = local_seq * tensor_count
    head_width = qkv_weight.shape[2]
    hidden_width = expand_weight.shape[1]
    head_size = rel_tables.shape[2]
    grid_side = (rel_tables.shape[1] + 1) // 2
    qkv_full, out_full, expand_full, reduce_full = (
        lax.all_gather(qkv_weight.astype(NARROW), "dp", axis=1, tiled=True),
        lax.all_gather(out_weight.astype(NARROW), "dp", axis=1, tiled=True),
        lax.all_gather(expand_weight.astype(NARROW), "dp", axis=0, tiled=True),
        lax.all_gather(reduce_weight.astype(NARROW), "dp", axis=1, tiled=True),
    )
    qkv_joined = qkv_full.transpose(1, 0, 2).reshape(model_width, 3 * head_width)
    piece = gains_biases.shape[0]
    params_all = lax.all_gather(
        as_tiles(gains_biases), ("dp", "tensor"), axis=0, tiled=False
    ).reshape(-1, TILE)[:, :piece].reshape(-1)

    def segment(position):
        return params_all[position * model_width : (position + 1) * model_width]

    query_bias = lax.dynamic_slice_in_dim(
        params_all, 2 * model_width + tensor_index * head_width, head_width
    )
    value_bias = lax.dynamic_slice_in_dim(
        params_all, 3 * model_width + tensor_index * head_width, head_width
    )
    heads = head_width // head_size
    plain, turned, hot, back = attention_tables(rel_tables.astype(NARROW), grid_side)
    token_rows = tokens.reshape(local_rows, model_width).astype(SINGLE)
    normed_one, scaled_one, inverse_one = normalize(token_rows, segment(0), segment(1))
    gathered_one = lax.all_gather(normed_one.astype(NARROW), "tensor", axis=0, tiled=True)
    projected = jnp.dot(gathered_one, qkv_joined, preferred_element_type=SINGLE)
    qkv_bias = jnp.concatenate([query_bias, jnp.zeros((head_width,), SINGLE), value_bias])
    qkv_rows = (projected + qkv_bias).astype(NARROW)
    context_rows, bias_wide, logsums = attend_forward(
        qkv_rows, turned, hot, heads, head_size, grid_side
    )
    mid_rows = token_rows + (
        lax.psum_scatter(
            jnp.dot(context_rows, out_full, preferred_element_type=SINGLE).astype(NARROW),
            "tensor",
            scatter_dimension=0,
            tiled=True,
        ).astype(SINGLE)
        + segment(4)
    )
    normed_two, scaled_two, inverse_two = normalize(mid_rows, segment(5), segment(6))
    normed_two_low = normed_two.astype(NARROW)
    expand_bias = lax.dynamic_slice_in_dim(
        params_all, 8 * model_width + tensor_index * hidden_width, hidden_width
    )
    gathered_two = lax.all_gather(normed_two_low, "tensor", axis=0, tiled=True)
    hidden_pre = jnp.dot(gathered_two, expand_full, preferred_element_type=SINGLE) + expand_bias
    hidden_low = jax.nn.gelu(hidden_pre, approximate=False).astype(NARROW)
    mlp_sum = lax.psum_scatter(
        jnp.dot(hidden_low, reduce_full, preferred_element_type=SINGLE).astype(jnp.bfloat16),
        "tensor",
        scatter_dimension=0,
        tiled=True,
    ).astype(jnp.float32)
    block_rows = mid_rows + (mlp_sum + segment(7))
    block_out = block_rows.astype(NARROW).reshape(tokens.shape)
    cotangent_rows = cotangent.reshape(local_rows, model_width)
    grad_block = cotangent_rows.astype(SINGLE)
    grad_reduce_bias = jnp.sum(grad_block, axis=0)
    shard_rows = lax.all_gather(cotangent_rows, "tensor", axis=0, tiled=True)
    part_hidden = contract_cols(shard_rows, reduce_full)
    grad_hidden = part_hidden
    grad_hidden, grad_reduce = (grad_hidden, contract_rows(hidden_low, shard_rows))
    grad_pre = (grad_hidden * gelu_slope(hidden_pre)).astype(NARROW)
    grad_expand = contract_rows(gathered_two, grad_pre)
    grad_expand_bias = jnp.sum(grad_pre, axis=0, dtype=SINGLE)
    expand_bias_full = lax.dynamic_update_slice_in_dim(
        jnp.zeros((hidden_width * tensor_count,), SINGLE),
        grad_expand_bias,
        tensor_index * hidden_width,
        0,
    )
    grad_normed_two = lax.psum_scatter(
        contract_cols(grad_pre, expand_full).astype(jnp.bfloat16),
        "tensor",
        scatter_dimension=0,
        tiled=True,
    ).astype(jnp.float32)
    grad_mid_norm, grad_gain_two, grad_shift_two = normalize_back(
        grad_normed_two, scaled_two, inverse_two, segment(5)
    )
    grad_mid = grad_block + grad_mid_norm
    grad_attn_low = grad_mid.astype(NARROW)
    grad_out_bias = jnp.sum(grad_attn_low, axis=0, dtype=SINGLE)
    shard_rows = lax.all_gather(grad_attn_low, "tensor", axis=0, tiled=True)
    part_context = contract_cols(shard_rows, out_full)
    grad_context = part_context
    grad_context, grad_out = (grad_context, contract_rows(context_rows, shard_rows))
    grad_qkv_rows, grad_tables = attend_backward(
        qkv_rows, grad_context.astype(NARROW), bias_wide, logsums, plain, hot, back,
        heads, head_size, grid_side,
    )
    grad_query_rows = grad_qkv_rows[:, :head_width]
    grad_value_rows = grad_qkv_rows[:, 2 * head_width :]
    grad_query_bias = jnp.sum(grad_query_rows, axis=0, dtype=SINGLE)
    grad_value_bias = jnp.sum(grad_value_rows, axis=0, dtype=SINGLE)
    grad_qkv = (
        contract_rows(gathered_one, grad_qkv_rows)
        .reshape(model_width, 3, head_width)
        .transpose(1, 0, 2)
    )
    grad_normed_one = lax.psum_scatter(
        contract_cols(grad_qkv_rows, qkv_joined).astype(jnp.bfloat16),
        "tensor",
        scatter_dimension=0,
        tiled=True,
    ).astype(jnp.float32)
    grad_token_norm, grad_gain_one, grad_shift_one = normalize_back(
        grad_normed_one, scaled_one, inverse_one, segment(0)
    )
    token_grad = (grad_mid + grad_token_norm).reshape(tokens.shape)
    rel_own = grad_tables.reshape(2, 64, head_size)[:, : rel_tables.shape[1]]
    width_zeros = jnp.zeros((model_width,), SINGLE)
    grad_small = jnp.concatenate(
        [
            grad_gain_one,
            grad_shift_one,
            lax.dynamic_update_slice_in_dim(
                width_zeros, grad_query_bias, tensor_index * head_width, 0
            ),
            lax.dynamic_update_slice_in_dim(
                width_zeros, grad_value_bias, tensor_index * head_width, 0
            ),
            grad_out_bias,
            grad_gain_two,
            grad_shift_two,
            grad_reduce_bias,
            expand_bias_full,
        ]
    )
    devices = lax.axis_size("dp") * tensor_count
    rel_flat = rel_own.reshape(-1)
    rel_piece = -(-rel_flat.shape[0] // devices)
    rel_flat = jnp.pad(rel_flat, (0, rel_piece * devices - rel_flat.shape[0]))
    packed = jnp.concatenate(
        [grad_small.reshape(devices, piece), rel_flat.reshape(devices, rel_piece)], axis=1
    )
    small_sum = lax.psum_scatter(
        jax.vmap(as_tiles)(packed), ("dp", "tensor"), scatter_dimension=0, tiled=False
    )
    gains_grad = small_sum.reshape(-1)[:piece]
    rel_grad = lax.all_gather(small_sum, ("dp", "tensor"), axis=0, tiled=False)
    rel_grad = rel_grad.reshape(devices, TILE)[:, piece : piece + rel_piece].reshape(-1)
    rel_grad = rel_grad[: rel_tables.size].reshape(rel_tables.shape)
    qkv_grad, out_grad, expand_grad, reduce_grad = (
        lax.psum_scatter(grad_qkv.astype(NARROW), "dp", scatter_dimension=1, tiled=True).astype(SINGLE),
        lax.psum_scatter(grad_out.astype(NARROW), "dp", scatter_dimension=1, tiled=True).astype(SINGLE),
        lax.psum_scatter(grad_expand.astype(NARROW), "dp", scatter_dimension=0, tiled=True).astype(SINGLE),
        lax.psum_scatter(grad_reduce.astype(NARROW), "dp", scatter_dimension=1, tiled=True).astype(SINGLE),
    )
    new_qkv, moment_qkv, average_qkv = advance(
        qkv_weight, qkv_moment, qkv_average, qkv_grad, RATE_MAIN
    )
    new_out, moment_out, average_out = advance(
        out_weight, out_moment, out_average, out_grad, RATE_MAIN
    )
    new_expand, moment_expand, average_expand = advance(
        expand_weight, expand_moment, expand_average, expand_grad, RATE_MAIN
    )
    new_reduce, moment_reduce, average_reduce = advance(
        reduce_weight, reduce_moment, reduce_average, reduce_grad, RATE_MAIN
    )
    new_gains, moment_gains, average_gains = advance(
        gains_biases, gains_moment, gains_average, gains_grad, RATE_MAIN
    )
    new_rel, moment_rel, average_rel = advance(
        rel_tables, rel_moment, rel_average, rel_grad, RATE_TABLES
    )
    return (
        block_out,
        token_grad,
        qkv_grad,
        out_grad,
        expand_grad,
        reduce_grad,
        gains_grad,
        rel_grad,
        new_qkv,
        new_out,
        new_expand,
        new_reduce,
        new_gains,
        new_rel,
        moment_qkv,
        moment_out,
        moment_expand,
        moment_reduce,
        moment_gains,
        moment_rel,
        average_qkv,
        average_out,
        average_expand,
        average_reduce,
        average_gains,
        average_rel,
    )


def solution(mesh):
    placed = (
        P("tensor", "dp", None),
        P("tensor", "dp", None),
        P(None, "dp", "tensor"),
        P("tensor", "dp"),
        P("dp", "tensor"),
        P("tensor", "dp"),
        P(("dp", "tensor")),
        P(),
        P(None, "dp", "tensor"),
        P("tensor", "dp"),
        P("dp", "tensor"),
        P("tensor", "dp"),
        P(("dp", "tensor")),
        P(),
        P(None, "dp", "tensor"),
        P("tensor", "dp"),
        P("dp", "tensor"),
        P("tensor", "dp"),
        P(("dp", "tensor")),
        P(),
    )
    return jax.shard_map(
        local,
        mesh=mesh,
        in_specs=placed,
        out_specs=(
            P("tensor", "dp", None),
            P("tensor", "dp", None),
            P(None, "dp", "tensor"),
            P("tensor", "dp"),
            P("dp", "tensor"),
            P("tensor", "dp"),
            P(("dp", "tensor")),
            P(),
            P(None, "dp", "tensor"),
            P("tensor", "dp"),
            P("dp", "tensor"),
            P("tensor", "dp"),
            P(("dp", "tensor")),
            P(),
            P(None, "dp", "tensor"),
            P("tensor", "dp"),
            P("dp", "tensor"),
            P("tensor", "dp"),
            P(("dp", "tensor")),
            P(),
            P(None, "dp", "tensor"),
            P("tensor", "dp"),
            P("dp", "tensor"),
            P("tensor", "dp"),
            P(("dp", "tensor")),
            P(),
        ),
        check_vma=False,
    )
```

time: 1520 us -> 1040 us (0.68)
  local copies, waits for them, and re-layouts: 396 us -> 28.4 us
  waiting for transfers between devices: 805 us -> 683 us
  blocking collectives: 55.4 us -> 148 us
  matrix products: 170 us -> 81.5 us
  other arithmetic: 70 us -> 34.8 us
  Pallas kernels: 0 us -> 34.6 us
    add x18 -> x0, local copies, waits for them, and re-layouts: 299 us -> none  [the longest x16 299 us: block_scores(): scores = scores + row_bias[..., :, None] + col_bias[..., None, :]]
    all_gather x0 -> x2, blocking collectives: none -> 137 us  [the longest x1 71 us: local(): lax.all_gather(as_tiles(gains_biases), ('dp', 'tensor'), axis=0, tiled=Fa...]
    dot_general x34 -> x0, matrix products: 85.4 us -> none  [the longest x4 30 us: block_scores(): jnp.einsum('qhc,khc->hqk', query_block, key_rows, preferred_element_type=...]
    reduce_scatter x6, waiting for transfers between devices: 286 us -> 223 us  [the longest x1 51 us: local(): lax.psum_scatter(contract_cols(grad_qkv_rows, qkv_joined).astype(jnp.bflo...]
    reshape x7 -> x3, local copies, waits for them, and re-layouts: 51.4 us -> 0.34 us  [the longest x1 0.15 us: local(): rel_flat.reshape(devices, rel_piece)]
    unnamed x1 -> x0, blocking collectives: 42.7 us -> none
    reduce_scatter x1, waiting for transfers between devices: 90.8 us -> 49.2 us  [local(): lax.psum_scatter(jnp.dot(context_rows, out_full, preferred_element_type=S...]
    pallas_call x0 -> x2, Pallas kernels: none -> 34.6 us  [the longest x1 18.9 us: attend_backward(): pl.pallas_call(functools.partial(backward_kernel, heads, size, grid_side,...]
  transfers between devices with their start and end apart: 16 -> 16, of which waited for: 15 -> 15; matrix products, arithmetic and copies ran while one was open for 6% -> 9% of each run, Pallas kernels for 0% -> 2%
where the time goes in v1:
time: 1040 us; the launch traced here: 1030 us
  waiting for transfers between devices  683 us (66%)
  blocking collectives  148 us (14%)
  matrix products  81.5 us (8%)
  other arithmetic  34.8 us (3%)
  Pallas kernels  34.6 us (3%)
  local copies, waits for them, and re-layouts  28.4 us (3%)
  between operations  14.9 us (1%)
    unnamed x17, waiting for transfers between devices  124 us
    all_gather x1, blocking collectives, local(): lax.all_gather(as_tiles(gains_biases), ('dp', 'tensor'), axis=0, tiled=Fa...  71 us
    all_gather x1, blocking collectives, local(): rel_grad = lax.all_gather(small_sum, ('dp', 'tensor'), axis=0, tiled=False)  66.3 us
    all_gather x1, waiting for transfers between devices, local(): gathered_two = lax.all_gather(normed_two_low, 'tensor', axis=0, tiled=True)  56.8 us
    reduce_scatter x1, waiting for transfers between devices, local(): lax.psum_scatter(jnp.dot(hidden_low, reduce_full, preferred_element_type=...  51.5 us
    reduce_scatter x1, waiting for transfers between devices, local(): lax.psum_scatter(contract_cols(grad_qkv_rows, qkv_joined).astype(jnp.bflo...  51 us
    reduce_scatter x1, waiting for transfers between devices, local(): lax.psum_scatter(jnp.dot(context_rows, out_full, preferred_element_type=S...  49.2 us
    all_gather x1, waiting for transfers between devices, local(): shard_rows = lax.all_gather(grad_attn_low, 'tensor', axis=0, tiled=True)  46.5 us
  transfers between devices with their start and end apart: 16, of which 15 were waited for; matrix products, arithmetic and copies ran while one was open for 9% of the time, Pallas kernels for 2%

profile of v1, /device:TPU:0, one launch (start us, length us, event | category | flops | bytes accessed | tf_op | source)
XLA Modules:
  0.0 1026.8 jit_solution(7041880664388445337)
XLA Ops:
  7.3 2.0 convert_element_type.132
  9.3 0.7 pad_bitcast_fusion
  10.0 71.0 %all_gather.30 = f32[32,8,128]{2,1,0:T(8,128)S(1)} all-gather(f32[1,8,128]{2,1,0:T(8,128)S(1)} %pad_bitcast_fusion), channel_id=1, replica_groups=mesh['dp'=8,'tensor'=4] {'dp','tensor'}, dimensions={0}, use_global_device_ids=true | all-gather | bytes 135168 | tf_op jit(solution)/shard_map/all_gather | solution.py:287
  81.2 1.3 convert_reduce_fusion.4
  82.8 0.7 fusion.62
  83.5 1.1 fusion.31
  85.1 10.9 %all_gather.33 = bf16[320,1280]{0,1:T(8,128)(2,1)} all-gather(bf16[320,160]{0,1:T(8,128)(2,1)S(1)} %convert_element_type.136), channel_id=1, replica_groups=mesh['dp'=8,'tensor'=4] {'dp'}, dimensions={1}, use_global_device_ids=true | all-gather | bytes 921600 | tf_op jit(solution)/shard_map/all_gather | solution.py:281
  96.0 2.2 fusion.50
  98.2 5.5 copy.80
  103.7 32.3 %all-gather.9.cloned.1.call-done = bf16[1024,1280]{1,0:T(8,128)(2,1)} async-done(((bf16[256,1280]{1,0:T(8,128)(2,1)}), bf16[1024,1280]{1,0:T(8,128)(2,1)}) %all-gather.9.cloned.1.call-update) | async-done | bytes 2621456 | tf_op jit(solution)/shard_map/all_gather | solution.py:304
  136.0 5.5 add_convert_fusion.qkv_ref
  141.4 15.7 %attend_forward.1 = (bf16[1024,320]{1,0:T(8,128)(2,1)S(1)}, bf16[4,1024,128]{2,1,0:T(8,128)(2,1)S(1)}, f32[4,1,1024]{2,1,0:T(1,128)S(1)}) custom-call(bf16[1024,960]{1,0:T(8,128)(2,1)S(1)} %add_convert_fusion.qkv_ref, bf16[128,80]{1,0:T(8,128)(2,1)S(1)} %bitcast.113, bf16[1024,128]{1,0:T(8,128)(2,1)S(1)} %get-tuple-element.188.hot_ref), custom_call_target="tpu_custom_call" | custom-call | tf_op jit(solution)/shard_map/attend_forward/pallas_call | solution.py:189
  157.2 0.9 copy-done.4
  158.1 3.0 convolution_convert_fusion.2
  161.2 1.1 copy-done.13
  162.2 0.8 convert_element_type.140
  163.1 49.2 %reduce-scatter.9.cloned.1.call-done = bf16[256,1280]{1,0:T(8,128)(2,1)} async-done(((bf16[1024,1280]{1,0:T(8,128)(2,1)}), bf16[256,1280]{1,0:T(8,128)(2,1)}) %reduce-scatter.9.cloned.1.call-update) | async-done | bytes 655376 | tf_op jit(solution)/shard_map/reduce_scatter | solution.py:312
  212.3 1.4 fusion.51
  213.8 1.5 multiply_reduce_fusion
  215.2 1.2 add_convert_fusion.2
  217.1 29.8 %all-gather.15.cloned.1.call-done = bf16[1280,1280]{1,0:T(8,128)(2,1)} async-done(((bf16[160,1280]{1,0:T(8,128)(2,1)}), bf16[1280,1280]{1,0:T(8,128)(2,1)}) %all-gather.15.cloned.1.call-update) | async-done | bytes 3276816 | tf_op jit(solution)/shard_map/all_gather | solution.py:282
  246.9 56.8 %all-gather.13.cloned.1.call-done = bf16[1024,1280]{1,0:T(8,128)(2,1)} async-done(((bf16[256,1280]{1,0:T(8,128)(2,1)}), bf16[1024,1280]{1,0:T(8,128)(2,1)}) %all-gather.13.cloned.1.call-update) | async-done | bytes 2621456 | tf_op jit(solution)/shard_map/all_gather | solution.py:325
  303.7 17.9 %fusion.2 = (bf16[1024,1280]{1,0:T(8,128)(2,1)}, f32[1024,1280]{1,0:T(8,128)}) fusion(f32[1280]{0:T(1024)S(1)} %copy-done.37, bf16[1024,1280]{1,0:T(8,128)(2,1)} %all-gather.13.cloned.1.call-done, bf16[1280,1280]{1,0:T(8,128)(2,1)} %all-gather.15.cloned.1.call-done), kind=kOutput, calls=%fused_computation.6 | convolution fusion | flops 3441950720 | bytes 13767680 | tf_op jit(solution)/shard_map/dot_general | solution.py:326
  321.6 37.1 %all-gather.21.cloned.1.call-done = bf16[1024,1,1280]{2,0,1:T(8,128)(2,1)} async-done(((bf16[256,1,1280]{2,0,1:T(8,128)(2,1)}), bf16[1024,1,1280]{2,0,1:T(8,128)(2,1)}) %all-gather.21.cloned.1.call-update) | async-done | bytes 2621456 | tf_op jit(solution)/shard_map/all_gather | solution.py:339
  358.6 7.8 convolution_convert_fusion
  366.5 45.6 %reduce-scatter.23.cloned.1.call-done = bf16[1280,160]{0,1:T(8,128)(2,1)} async-done(((bf16[1280,1280]{0,1:T(8,128)(2,1)}), bf16[1280,160]{0,1:T(8,128)(2,1)}) %reduce-scatter.23.cloned.1.call-update) | async-done | bytes 409616 | tf_op jit(solution)/shard_map/reduce_scatter | solution.py:428
  412.1 3.8 add_multiply_fusion
  416.0 32.8 %all-gather.17.cloned.1.call-done = bf16[1280,1280]{0,1:T(8,128)(2,1)} async-done(((bf16[1280,160]{0,1:T(8,128)(2,1)}), bf16[1280,1280]{0,1:T(8,128)(2,1)}) %all-gather.17.cloned.1.call-update) | async-done | bytes 3276816 | tf_op jit(solution)/shard_map/all_gather | solution.py:283
  448.8 8.5 convert_reduce_fusion
  457.4 1.5 copy-done.43
  458.8 4.9 convolution_convert_fusion.4
  464.0 7.8 convolution_convert_fusion.5
  471.9 44.3 %reduce-scatter.13.cloned.1.call-done = bf16[256,1280]{1,0:T(8,128)(2,1)} async-done(((bf16[1024,1280]{1,0:T(8,128)(2,1)}), bf16[256,1280]{1,0:T(8,128)(2,1)}) %reduce-scatter.13.cloned.1.call-update) | async-done | bytes 655376 | tf_op jit(solution)/shard_map/reduce_scatter | solution.py:352
  516.2 2.5 fusion.42
  518.6 51.5 %reduce-scatter.11.cloned.1.call-done = bf16[256,1280]{1,0:T(8,128)(2,1)} async-done(((bf16[1024,1280]{1,0:T(8,128)(2,1)}), bf16[256,1280]{1,0:T(8,128)(2,1)}) %reduce-scatter.11.cloned.1.call-update) | async-done | bytes 655376 | tf_op jit(solution)/shard_map/reduce_scatter | solution.py:328
  570.2 4.2 convert_reduce_fusion.7
  574.5 7.8 convolution_convert_fusion.1
  582.4 46.5 %all-gather.19.cloned.1.call-done = bf16[1024,1280]{1,0:T(8,128)(2,1)} async-done(((bf16[256,1280]{1,0:T(8,128)(2,1)}), bf16[1024,1280]{1,0:T(8,128)(2,1)}) %all-gather.19.cloned.1.call-update) | async-done | bytes 2621456 | tf_op jit(solution)/shard_map/all_gather | solution.py:364
  628.9 4.2 convolution_convert_fusion.7
  633.5 3.7 convolution_convert_fusion.8
  637.1 1.5 copy.84.grad_ref
  638.7 18.9 %attend_backward.1 = (bf16[1024,960]{1,0:T(8,128)(2,1)S(1)}, f32[128,80]{1,0:T(8,128)S(1)}) custom-call(bf16[1024,960]{1,0:T(8,128)(2,1)} %copy-done, bf16[1024,320]{1,0:T(8,128)(2,1)S(1)} %copy.84.grad_ref, bf16[4,1024,128]{2,1,0:T(8,128)(2,1)S(1)} %get-tuple-element.32.bias_ref, f32[4,1,1024]{2,1,0:T(1,128)S(1)} %get-tuple-element.33.lse_ref, ...), custom_call_target="tpu_custom_call" | custom-call | tf_op jit(solution)/shard_map/attend_backward/pallas_call | solution.py:212
  657.6 4.3 convolution_convert_fusion.6
  661.8 5.2 copy.85
  667.1 1.5 copy-done.2
  668.7 6.1 convolution_convert_fusion.3
  675.0 0.8 copy-done.11
  676.3 1.4 reduce-scatter.21.cloned.1.call-done
  677.7 3.6 add_multiply_fusion.1
  682.3 34.3 %reduce-scatter.19.cloned.1.call-done = bf16[320,160]{0,1:T(8,128)(2,1)} async-done(((bf16[320,1280]{0,1:T(8,128)(2,1)}), bf16[320,160]{0,1:T(8,128)(2,1)}) %reduce-scatter.19.cloned.1.call-update) | async-done | bytes 102416 | tf_op jit(solution)/shard_map/reduce_scatter | solution.py:426
  716.6 1.9 add_multiply_fusion.3
  718.6 46.4 %reduce-scatter.17.cloned.1.call-done = bf16[3,160,320]{2,1,0:T(8,128)(2,1)} async-done(((bf16[3,1280,320]{2,1,0:T(8,128)(2,1)}), bf16[3,160,320]{2,1,0:T(8,128)(2,1)}) %reduce-scatter.17.cloned.1.call-update) | async-done | bytes 307216 | tf_op jit(solution)/shard_map/reduce_scatter | solution.py:425
  765.0 3.5 add_multiply_fusion.2
  768.5 51.0 %reduce-scatter.15.cloned.1.call-done = bf16[256,1280]{1,0:T(8,128)(2,1)} async-done(((bf16[1024,1280]{1,0:T(8,128)(2,1)}), bf16[256,1280]{1,0:T(8,128)(2,1)}) %reduce-scatter.15.cloned.1.call-update) | async-done | bytes 655376 | tf_op jit(solution)/shard_map/reduce_scatter | solution.py:381
  819.5 1.8 fusion.43
  821.6 0.7 copy.98
  822.9 2.4 copy.89
  825.3 123.6 %all-reduce.7.cloned.1.call-done = f32[32,8,128]{2,1,0:T(8,128)} async-done(((f32[32,8,128]{2,1,0:T(8,128)}), f32[32,8,128]{2,1,0:T(8,128)}) %all-reduce.7.cloned.1.call-update) | async-done | bytes 131088
  948.9 0.7 constant_dynamic-slice_fusion
  949.6 66.3 %all_gather.39 = f32[32,8,128]{2,1,0:T(8,128)S(1)} all-gather(f32[1,8,128]{2,1,0:T(8,128)S(1)} %constant_dynamic-slice_fusion), channel_id=1, replica_groups=mesh['dp'=8,'tensor'=4] {'dp','tensor'}, dimensions={0}, use_global_device_ids=true | all-gather | bytes 135168 | tf_op jit(solution)/shard_map/all_gather | solution.py:421
  1016.1 0.7 copy.90
  1016.8 0.7 copy.91
  1017.5 0.7 copy.92
  1018.2 0.7 copy.93
  (173 shorter events, 6.7 us)
Async XLA Ops:
  7.2 75.3 %copy-start.6 = (bf16[256,1,1280]{2,0,1:T(8,128)(2,1)S(1)}, bf16[256,1,1280]{2,0,1:T(8,128)(2,1)}, u32[]{:S(2)}) copy-start(bf16[256,1,1280]{2,0,1:T(8,128)(2,1)} %param.20) | copy-start | bytes 1966084
  7.2 77.5 %copy-start.20 = (f32[2,63,80]{2,0,1:T(2,128)S(1)}, f32[2,63,80]{2,0,1:T(2,128)}, u32[]{:S(2)}) copy-start(f32[2,63,80]{2,0,1:T(2,128)} %param.27) | copy-start | bytes 120964
  7.2 91.0 %all-gather.11.cloned.1.call-start = ((), (), s32[]{:S(2)}) async-start(), calls=%async_computation.9 | async-start | bytes 3317760 | tf_op jit(solution)/shard_map/all_gather | solution.py:280
  9.2 75.6 %copy-start.15 = (f32[320,160]{0,1:T(8,128)S(1)}, f32[320,160]{0,1:T(8,128)}, u32[]{:S(2)}) copy-start(f32[320,160]{0,1:T(8,128)} %param.23) | copy-start | bytes 614404
  9.3 126.7 %all-gather.9.cloned.1.call-start = ((), (), s32[]{:S(2)}) async-start(), calls=%async_computation.8 | async-start | bytes 3276800 | tf_op jit(solution)/shard_map/all_gather | solution.py:304
  82.5 2.3 copy-start.33
  82.8 1.9 copy-start.35
  84.7 127.6 %reduce-scatter.9.cloned.1.call-start = ((), (), s32[]{:S(2)}) async-start(), calls=%async_computation.10 | async-start | bytes 3276800 | tf_op jit(solution)/shard_map/reduce_scatter | solution.py:312
  136.0 22.1 %copy-start.17 = (bf16[320,1280]{0,1:T(8,128)(2,1)S(1)}, bf16[320,1280]{0,1:T(8,128)(2,1)}, u32[]{:S(2)}) copy-start(bf16[320,1280]{0,1:T(8,128)(2,1)} %all_gather.33) | copy-start | bytes 2457604
  141.4 19.6 %copy-start = (bf16[1024,960]{1,0:T(8,128)(2,1)}, bf16[1024,960]{1,0:T(8,128)(2,1)S(1)}, u32[]{:S(2)}) copy-start(bf16[1024,960]{1,0:T(8,128)(2,1)S(1)} %add_convert_fusion.qkv_ref) | copy-start | bytes 5898244
  157.2 0.9 copy-start.4
  161.1 1.1 copy-start.13
  161.1 51.2 %copy-start.7 = (bf16[256,1,1280]{2,0,1:T(8,128)(2,1)S(1)}, bf16[256,1,1280]{2,0,1:T(8,128)(2,1)}, u32[]{:S(2)}) copy-start(bf16[256,1,1280]{2,0,1:T(8,128)(2,1)} %param.20) | copy-start | bytes 1966084
  161.1 54.1 %copy-start.29 = (f32[1280]{0:T(1024)S(1)}, f32[1280]{0:T(1024)}, u32[]{:S(2)}) copy-start(f32[1280]{0:T(1024)} %get-tuple-element.180) | copy-start | bytes 15364
  161.1 85.8 %all-gather.15.cloned.1.call-start = ((), (), s32[]{:S(2)}) async-start(), calls=%async_computation.12 | async-start | bytes 3686400 | tf_op jit(solution)/shard_map/all_gather | solution.py:282
  163.0 140.6 %all-gather.13.cloned.1.call-start = ((), (), s32[]{:S(2)}) async-start(), calls=%async_computation.11 | async-start | bytes 3276800 | tf_op jit(solution)/shard_map/all_gather | solution.py:325
  212.3 3.0 copy-start.9
  213.7 89.9 %copy-start.37 = (f32[1280]{0:T(1024)S(1)}, f32[1280]{0:T(1024)}, u32[]{:S(2)}) copy-start(f32[1280]{0:T(1024)} %get-tuple-element.179) | copy-start | bytes 15364
  216.5 142.2 %all-gather.21.cloned.1.call-start = ((), (), s32[]{:S(2)}) async-start(), calls=%async_computation.22 | async-start | bytes 3276800 | tf_op jit(solution)/shard_map/all_gather | solution.py:339
  217.1 195.0 %reduce-scatter.23.cloned.1.call-start = ((), (), s32[]{:S(2)}) async-start(), calls=%async_computation.21 | async-start | bytes 3686400 | tf_op jit(solution)/shard_map/reduce_scatter | solution.py:428
  366.4 45.7 %copy-start.19 = (f32[1280,160]{0,1:T(8,128)S(1)}, f32[1280,160]{0,1:T(8,128)}, u32[]{:S(2)}) copy-start(f32[1280,160]{0,1:T(8,128)} %param.37) | copy-start | bytes 2457604
  366.5 82.4 %all-gather.17.cloned.1.call-start = ((), (), s32[]{:S(2)}) async-start(), calls=%async_computation.13 | async-start | bytes 3686400 | tf_op jit(solution)/shard_map/all_gather | solution.py:283
  415.9 100.2 %reduce-scatter.13.cloned.1.call-start = ((), (), s32[]{:S(2)}) async-start(), calls=%async_computation.15 | async-start | bytes 3276800 | tf_op jit(solution)/shard_map/reduce_scatter | solution.py:352
  448.8 10.0 copy-start.41
  457.4 1.5 copy-start.43
  463.7 106.4 %reduce-scatter.11.cloned.1.call-start = ((), (), s32[]{:S(2)}) async-start(), calls=%async_computation.14 | async-start | bytes 3276800 | tf_op jit(solution)/shard_map/reduce_scatter | solution.py:328
  471.8 98.4 %copy-start.10 = (bf16[256,1,1280]{2,0,1:T(8,128)(2,1)S(1)}, bf16[256,1,1280]{2,0,1:T(8,128)(2,1)}, u32[]{:S(2)}) copy-start(bf16[256,1,1280]{2,0,1:T(8,128)(2,1)} %param.21) | copy-start | bytes 1966084
  471.8 157.0 %all-gather.19.cloned.1.call-start = ((), (), s32[]{:S(2)}) async-start(), calls=%async_computation.16 | async-start | bytes 3276800 | tf_op jit(solution)/shard_map/all_gather | solution.py:364
  574.4 103.2 %reduce-scatter.21.cloned.1.call-start = ((), (), s32[]{:S(2)}) async-start(), calls=%async_computation.20 | async-start | bytes 3686400 | tf_op jit(solution)/shard_map/reduce_scatter | solution.py:427
  582.3 46.6 %copy-start.5 = (bf16[1024,320]{1,0:T(8,128)(2,1)S(1)}, bf16[1024,320]{1,0:T(8,128)(2,1)}, u32[]{:S(2)}) copy-start(bf16[1024,320]{1,0:T(8,128)(2,1)} %copy-done.4) | copy-start | bytes 1966084
  582.3 51.1 %copy-start.18 = (bf16[320,1280]{0,1:T(8,128)(2,1)S(1)}, bf16[320,1280]{0,1:T(8,128)(2,1)}, u32[]{:S(2)}) copy-start(bf16[320,1280]{0,1:T(8,128)(2,1)} %all_gather.33) | copy-start | bytes 2457604
  582.4 134.3 %reduce-scatter.19.cloned.1.call-start = ((), (), s32[]{:S(2)}) async-start(), calls=%async_computation.19 | async-start | bytes 1105920 | tf_op jit(solution)/shard_map/reduce_scatter | solution.py:426
  633.1 131.9 %reduce-scatter.17.cloned.1.call-start = ((), (), s32[]{:S(2)}) async-start(), calls=%async_computation.18 | async-start | bytes 3317760 | tf_op jit(solution)/shard_map/reduce_scatter | solution.py:425
  633.5 5.2 copy-start.3
  638.7 18.9 %copy-start.42 = (bf16[1024,1280]{1,0:T(8,128)(2,1)S(1)}, bf16[1024,1280]{1,0:T(8,128)(2,1)}, u32[]{:S(2)}) copy-start(bf16[1024,1280]{1,0:T(8,128)(2,1)} %all-gather.9.cloned.1.call-done) | copy-start | bytes 7864324
  657.5 4.3 copy-start.1
  667.1 1.6 copy-start.2
  667.1 152.4 %reduce-scatter.15.cloned.1.call-start = ((), (), s32[]{:S(2)}) async-start(), calls=%async_computation.17 | async-start | bytes 3276800 | tf_op jit(solution)/shard_map/reduce_scatter | solution.py:381
  674.7 1.1 copy-start.11
  674.7 274.2 %all-reduce.7.cloned.1.call-start = ((), (), s32[]{:S(2)}) async-start(), calls=%async_computation.23 | async-start | bytes 262144
  676.3 5.0 copy-start.24
  676.3 40.4 %copy-start.16 = (f32[320,160]{0,1:T(8,128)S(1)}, f32[320,160]{0,1:T(8,128)}, u32[]{:S(2)}) copy-start(f32[320,160]{0,1:T(8,128)} %param.23) | copy-start | bytes 614404
  676.3 40.4 %copy-start.22 = (f32[320,160]{0,1:T(8,128)S(1)}, f32[320,160]{0,1:T(8,128)}, u32[]{:S(2)}) copy-start(f32[320,160]{0,1:T(8,128)} %param.35) | copy-start | bytes 614404
  676.3 40.4 %copy-start.23 = (f32[320,160]{0,1:T(8,128)S(1)}, f32[320,160]{0,1:T(8,128)}, u32[]{:S(2)}) copy-start(f32[320,160]{0,1:T(8,128)} %param.29) | copy-start | bytes 614404
  718.5 100.9 %copy-start.8 = (bf16[256,1,1280]{2,0,1:T(8,128)(2,1)S(1)}, bf16[256,1,1280]{2,0,1:T(8,128)(2,1)}, u32[]{:S(2)}) copy-start(bf16[256,1,1280]{2,0,1:T(8,128)(2,1)} %param.20) | copy-start | bytes 1966084
  718.5 100.9 %copy-start.34 = (f32[256]{0:T(256)S(1)}, f32[256]{0:T(256)}, u32[]{:S(2)}) copy-start(f32[256]{0:T(256)} %copy-done.33) | copy-start | bytes 3076
  718.5 100.9 %copy-start.36 = (f32[256]{0:T(256)S(1)}, f32[256]{0:T(256)}, u32[]{:S(2)}) copy-start(f32[256]{0:T(256)} %copy-done.35) | copy-start | bytes 3076
  718.5 102.8 %copy-start.28 = (f32[15360]{0:T(1024)S(1)}, f32[15360]{0:T(1024)}, u32[]{:S(2)}) copy-start(f32[15360]{0:T(1024)} %custom-call) | copy-start | bytes 184324
  718.5 102.8 %copy-start.32 = (f32[1280]{0:T(1024)S(1)}, f32[1280]{0:T(1024)}, u32[]{:S(2)}) copy-start(f32[1280]{0:T(1024)} %get-tuple-element.172) | copy-start | bytes 15364
  718.5 102.8 %copy-start.31 = (f32[1280]{0:T(1024)S(1)}, f32[1280]{0:T(1024)}, u32[]{:S(2)}) copy-start(f32[1280]{0:T(1024)} %get-tuple-element.142) | copy-start | bytes 15364
  718.6 102.8 %copy-start.30 = (f32[1280]{0:T(1024)S(1)}, f32[1280]{0:T(1024)}, u32[]{:S(2)}) copy-start(f32[1280]{0:T(1024)} %get-tuple-element.148) | copy-start | bytes 15364
  718.6 102.9 %copy-start.25 = (f32[5120]{0:T(1024)S(1)}, f32[5120]{0:T(1024)}, u32[]{:S(2)}) copy-start(f32[5120]{0:T(1024)} %copy-done.24) | copy-start | bytes 61444
  718.6 103.8 %copy-start.12 = (f32[256,1280]{1,0:T(8,128)S(1)}, f32[256,1280]{1,0:T(8,128)}, u32[]{:S(2)}) copy-start(f32[256,1280]{1,0:T(8,128)} %get-tuple-element.174) | copy-start | bytes 3932164
  819.5 2.9 copy-start.14
  822.9 193.9 %copy-start.21 = (f32[2,63,80]{2,0,1:T(2,128)S(1)}, f32[2,63,80]{2,0,1:T(2,128)}, u32[]{:S(2)}) copy-start(f32[2,63,80]{2,0,1:T(2,128)} %param.27) | copy-start | bytes 120964
  822.9 193.9 %copy-start.26 = (f32[2,63,80]{2,0,1:T(2,128)S(1)}, f32[2,63,80]{2,0,1:T(2,128)}, u32[]{:S(2)}) copy-start(f32[2,63,80]{2,0,1:T(2,128)} %param.39) | copy-start | bytes 120964
  822.9 193.9 %copy-start.27 = (f32[2,63,80]{2,0,1:T(2,128)S(1)}, f32[2,63,80]{2,0,1:T(2,128)}, u32[]{:S(2)}) copy-start(f32[2,63,80]{2,0,1:T(2,128)} %param.33) | copy-start | bytes 120964
  822.9 196.6 %copy-start.38 = (f32[480]{0:T(512)S(1)}, f32[480]{0:T(512)}, u32[]{:S(2)}) copy-start(f32[480]{0:T(512)} %param.26) | copy-start | bytes 5764
  822.9 196.6 %copy-start.39 = (f32[480]{0:T(512)S(1)}, f32[480]{0:T(512)}, u32[]{:S(2)}) copy-start(f32[480]{0:T(512)} %param.38) | copy-start | bytes 5764
  822.9 196.6 %copy-start.40 = (f32[480]{0:T(512)S(1)}, f32[480]{0:T(512)}, u32[]{:S(2)}) copy-start(f32[480]{0:T(512)} %param.32) | copy-start | bytes 5764
Sparse Core Ops, SparseCore 0:
  10.5 34.2 all-gather.10
  84.8 51.1 all-gather.8
  161.2 51.0 reduce-scatter.8
  214.6 32.2 all-gather.14
  248.9 54.7 all-gather.12
  305.1 53.5 all-gather.20
  366.6 45.4 reduce-scatter.22
  416.0 32.7 all-gather.16
  463.9 52.2 reduce-scatter.12
  518.3 51.7 reduce-scatter.10
  574.6 54.2 all-gather.18
  632.1 45.4 reduce-scatter.20
  680.9 35.7 reduce-scatter.18
  719.9 45.0 reduce-scatter.16
  767.2 52.2 reduce-scatter.14
  824.8 124.0 all-reduce.6

commit v2 on v1

--- a/solution.py
+++ b/solution.py
@@ -64,8 +64,7 @@
     heads, size, grid_side, block, qkv_ref, table_ref, hot_ref,
     out_ref, bias_ref, lse_ref, query_ext, key_ext, bias_wide, context_t,
 ):
-    seq = qkv_ref.shape[0]
-    width = heads * size
+    seq = qkv_ref.shape[1]
     scale = size ** (-0.5)
     lane = lax.broadcasted_iota(jnp.int32, (grid_side, 128), 1)
     query_ext[:, 0:128] = jnp.zeros((seq, 128), NARROW)
@@ -73,10 +72,10 @@
     key_ext[:, 128:256] = hot_ref[...]
     for head in range(heads):
         low = head * size
-        query = qkv_ref[:, low : low + size]
-        value = qkv_ref[:, 2 * width + low : 2 * width + low + size]
+        query = qkv_ref[0, :, low : low + size]
+        value = qkv_ref[2, :, low : low + size]
         query_ext[:, 0:size] = query
-        key_ext[:, 0:size] = qkv_ref[:, width + low : width + low + size]
+        key_ext[:, 0:size] = qkv_ref[1, :, low : low + size]
         bias_wide[...] = dot_nt(query, table_ref[...])
         for row in range(grid_side):
             rows = pl.ds(row * grid_side, grid_side)
@@ -106,8 +105,7 @@
     heads, size, grid_side, block, qkv_ref, grad_ref, bias_ref, lse_ref, table_ref, hot_ref, rev_ref,
     out_ref, rel_ref, query_ext, key_ext, key_rev, spread, grad_keys, grad_values, grad_query,
 ):
-    seq = qkv_ref.shape[0]
-    width = heads * size
+    seq = qkv_ref.shape[1]
     scale = size ** (-0.5)
     lane = lax.broadcasted_iota(jnp.int32, (grid_side, 128), 1)
     query_ext[:, 0:128] = jnp.zeros((seq, 128), NARROW)
@@ -118,9 +116,9 @@
     rel_total = jnp.zeros(rel_ref.shape, SINGLE)
     for head in range(heads):
         low = head * size
-        query = qkv_ref[:, low : low + size]
-        key = qkv_ref[:, width + low : width + low + size]
-        value = qkv_ref[:, 2 * width + low : 2 * width + low + size]
+        query = qkv_ref[0, :, low : low + size]
+        key = qkv_ref[1, :, low : low + size]
+        value = qkv_ref[2, :, low : low + size]
         grad = grad_ref[:, low : low + size]
         query_ext[:, 0:size] = query
         query_ext[:, 128:256] = bias_ref[head]
@@ -155,9 +153,9 @@
                 part_col = pltpu.roll(part_col, 64 - grid_side, 1, stride=1, stride_axis=0)
                 spread[row * grid_side : (row + 1) * grid_side, :] = (part_row + part_col).astype(NARROW)
         total_query = grad_query[:, 0:size] * scale + dot_nn(spread[...], table_ref[...])
-        out_ref[:, low : low + size] = total_query.astype(NARROW)
-        out_ref[:, width + low : width + low + size] = (grad_keys[...] * scale).astype(NARROW)
-        out_ref[:, 2 * width + low : 2 * width + low + size] = grad_values[...].astype(NARROW)
+        out_ref[0, :, low : low + size] = total_query.astype(NARROW)
+        out_ref[1, :, low : low + size] = (grad_keys[...] * scale).astype(NARROW)
+        out_ref[2, :, low : low + size] = grad_values[...].astype(NARROW)
         rel_total = rel_total + dot_tn(spread[...], query)
     rel_ref[...] = rel_total
 
@@ -184,7 +182,7 @@
 
 
 def attend_forward(qkv_rows, turned, hot, heads, size, grid_side):
-    seq = qkv_rows.shape[0]
+    seq = qkv_rows.shape[1]
     block = min(256, seq)
     return pl.pallas_call(
         functools.partial(forward_kernel, heads, size, grid_side, block),
@@ -207,12 +205,12 @@
 
 
 def attend_backward(qkv_rows, grad_rows, bias, lse, plain, hot, back, heads, size, grid_side):
-    seq = qkv_rows.shape[0]
+    seq = qkv_rows.shape[1]
     block = min(256, seq)
     return pl.pallas_call(
         functools.partial(backward_kernel, heads, size, grid_side, block),
         out_shape=(
-            jax.ShapeDtypeStruct((seq, 3 * heads * size), NARROW),
+            jax.ShapeDtypeStruct((3, seq, heads * size), NARROW),
             jax.ShapeDtypeStruct((128, size), SINGLE),
         ),
         in_specs=whole_vmem(7),
@@ -229,6 +227,370 @@
         compiler_params=pltpu.CompilerParams(vmem_limit_bytes=48 << 20),
         name="attend_backward",
     )(qkv_rows, grad_rows, bias, lse, plain, hot, back)
+
+
+MESH_IDS = pl.DeviceIdType.MESH
+
+
+def place_of(index, inner):
+    return (index // inner, index % inner)
+
+
+def greet_all(me, count, inner):
+    barrier = pltpu.get_barrier_semaphore()
+
+    def signal(step, carry):
+        pl.semaphore_signal(
+            barrier, inc=1, device_id=place_of((me + step) % count, inner), device_id_type=MESH_IDS
+        )
+        return carry
+
+    lax.fori_loop(1, count, signal, 0)
+    pl.semaphore_wait(barrier, count - 1)
+
+
+def exchange(me, count, inner, source, target, send_sem, recv_sem):
+    def piece(step):
+        other = (me + step) % count
+        return pltpu.make_async_remote_copy(
+            src_ref=source(other),
+            dst_ref=target.at[me],
+            send_sem=send_sem.at[step],
+            recv_sem=recv_sem.at[step],
+            device_id=place_of(other, inner),
+            device_id_type=MESH_IDS,
+        )
+
+    def start(step, carry):
+        piece(step).start()
+        return carry
+
+    def finish(step, carry):
+        sender = (me + count - step) % count
+        pltpu.make_async_remote_copy(
+            src_ref=source(sender),
+            dst_ref=target.at[sender],
+            send_sem=send_sem.at[step],
+            recv_sem=recv_sem.at[step],
+            device_id=place_of(sender, inner),
+            device_id_type=MESH_IDS,
+        ).wait_recv()
+        piece(step).wait_send()
+        return carry
+
+    lax.fori_loop(1, count, start, 0)
+    lax.fori_loop(1, count, finish, 0)
+
+
+def small_gather_kernel(outer, inner, own_ref, all_ref, send_sem, recv_sem):
+    count = outer * inner
+    me = lax.axis_index("dp") * inner + lax.axis_index("tensor")
+    greet_all(me, count, inner)
+    all_ref[me] = own_ref[...]
+    exchange(me, count, inner, lambda other: own_ref, all_ref, send_sem, recv_sem)
+
+
+def small_sum_kernel(
+    outer, inner, packed_ref, total_ref, all_ref, landing, send_one, recv_one, send_two, recv_two
+):
+    count = outer * inner
+    me = lax.axis_index("dp") * inner + lax.axis_index("tensor")
+    greet_all(me, count, inner)
+    landing[me] = packed_ref[me]
+    exchange(me, count, inner, lambda other: packed_ref.at[other], landing, send_one, recv_one)
+    total = jnp.sum(landing[...], axis=0)
+    total_ref[...] = total
+    all_ref[me] = total
+    exchange(me, count, inner, lambda other: total_ref, all_ref, send_two, recv_two)
+
+
+def small_gather(own, outer, inner, collective_id):
+    count = outer * inner
+    return pl.pallas_call(
+        functools.partial(small_gather_kernel, outer, inner),
+        out_shape=jax.ShapeDtypeStruct((count,) + own.shape, own.dtype),
+        in_specs=whole_vmem(1),
+        out_specs=whole_vmem(1)[0],
+        scratch_shapes=[pltpu.SemaphoreType.DMA((count,))] * 2,
+        compiler_params=pltpu.CompilerParams(collective_id=collective_id, has_side_effects=True),
+        name="small_gather",
+    )(own)
+
+
+def small_sum(packed, outer, inner, collective_id):
+    count = outer * inner
+    return pl.pallas_call(
+        functools.partial(small_sum_kernel, outer, inner),
+        out_shape=(
+            jax.ShapeDtypeStruct(packed.shape[1:], packed.dtype),
+            jax.ShapeDtypeStruct(packed.shape, packed.dtype),
+        ),
+        in_specs=whole_vmem(1),
+        out_specs=tuple(whole_vmem(2)),
+        scratch_shapes=[pltpu.VMEM(packed.shape, packed.dtype)]
+        + [pltpu.SemaphoreType.DMA((count,))] * 4,
+        compiler_params=pltpu.CompilerParams(collective_id=collective_id, has_side_effects=True),
+        name="small_sum",
+    )(packed)
+
+
+def greet_line(me, parts):
+    barrier = pltpu.get_barrier_semaphore()
+
+    @pl.when(me > 0)
+    def _():
+        pl.semaphore_signal(barrier, inc=1, device_id={"tensor": me - 1}, device_id_type=MESH_IDS)
+
+    @pl.when(me < parts - 1)
+    def _():
+        pl.semaphore_signal(barrier, inc=1, device_id={"tensor": me + 1}, device_id_type=MESH_IDS)
+
+    @pl.when((me > 0) & (me < parts - 1))
+    def _():
+        pl.semaphore_wait(barrier, 2)
+
+    @pl.when((me == 0) | (me == parts - 1))
+    def _():
+        pl.semaphore_wait(barrier, 1)
+
+
+def gather_kernel(parts, chunks, inputs, finish_rows, own_ref, *refs):
+    extra = refs[:inputs]
+    all_ref = refs[inputs]
+    results = refs[inputs + 1 : -2]
+    send_sem, recv_sem = refs[-2:]
+    me = lax.axis_index("tensor")
+    rows = own_ref.shape[0]
+    chunk = rows // chunks
+    greet_line(me, parts)
+
+    def block(shard, piece):
+        return all_ref.at[pl.ds(pl.multiple_of(shard * rows + piece * chunk, chunk), chunk)]
+
+    def outgoing(way, step, piece):
+        shard = me - step if way == 0 else me + step
+        source = own_ref.at[pl.ds(piece * chunk, chunk)] if step == 0 else block(shard, piece)
+        return pltpu.make_async_remote_copy(
+            src_ref=source,
+            dst_ref=block(shard, piece),
+            send_sem=send_sem.at[way, step, piece],
+            recv_sem=recv_sem.at[way, step + 1, piece],
+            device_id={"tensor": me + 1 if way == 0 else me - 1},
+            device_id_type=MESH_IDS,
+        )
+
+    def incoming(way, step, piece):
+        shard = me - step if way == 0 else me + step
+        return pltpu.make_async_remote_copy(
+            src_ref=block(shard, piece),
+            dst_ref=block(shard, piece),
+            send_sem=send_sem.at[way, step, piece],
+            recv_sem=recv_sem.at[way, step, piece],
+            device_id={"tensor": me - 1 if way == 0 else me + 1},
+            device_id_type=MESH_IDS,
+        )
+
+    def held(way, step):
+        return me - step >= 0 if way == 0 else me + step < parts
+
+    def passes(way, step):
+        return held(way, step) & ((me < parts - 1) if way == 0 else (me > 0))
+
+    for step in range(parts):
+        for piece in range(chunks):
+            for way in range(2):
+                if step:
+
+                    @pl.when(held(way, step))
+                    def _():
+                        incoming(way, step, piece).wait_recv()
+
+                if step < parts - 1:
+
+                    @pl.when(passes(way, step))
+                    def _():
+                        outgoing(way, step, piece).start()
+
+        if step == 0:
+            mine = pl.ds(pl.multiple_of(me * rows, rows), rows)
+            all_ref[mine, :] = own_ref[...]
+            finish_rows(own_ref[...], mine, extra, results)
+        else:
+            for way in range(2):
+
+                @pl.when(held(way, step))
+                def _():
+                    shard = me - step if way == 0 else me + step
+                    place = pl.ds(pl.multiple_of(shard * rows, rows), rows)
+                    finish_rows(all_ref[place, :], place, extra, results)
+
+    for step in range(parts - 1):
+        for piece in range(chunks):
+            for way in range(2):
+
+                @pl.when(passes(way, step))
+                def _():
+                    outgoing(way, step, piece).wait_send()
+
+
+def gather_rows(own, extra, results, finish_rows, parts, collective_id, name):
+    chunks = 4
+    return pl.pallas_call(
+        functools.partial(gather_kernel, parts, chunks, len(extra), finish_rows),
+        out_shape=(jax.ShapeDtypeStruct((parts * own.shape[0], own.shape[1]), own.dtype),)
+        + tuple(results),
+        in_specs=whole_vmem(1 + len(extra)),
+        out_specs=tuple(whole_vmem(1 + len(results))),
+        scratch_shapes=[
+            pltpu.SemaphoreType.DMA((2, parts, chunks)),
+            pltpu.SemaphoreType.DMA((2, parts, chunks)),
+        ],
+        compiler_params=pltpu.CompilerParams(
+            collective_id=collective_id, has_side_effects=True, vmem_limit_bytes=40 << 20
+        ),
+        name=name,
+    )(own, *extra)
+
+
+def scatter_kernel(
+    parts, chunks, turned, left_ref, weight_ref, out_ref, product, landing, send_sem, recv_sem
+):
+    me = lax.axis_index("tensor")
+    rows = out_ref.shape[0]
+    chunk = rows // chunks
+    greet_line(me, parts)
+
+    def own_block(shard, piece):
+        return pl.ds(pl.multiple_of(shard * rows + piece * chunk, chunk), chunk)
+
+    def outgoing(way, far, piece, source):
+        return pltpu.make_async_remote_copy(
+            src_ref=source,
+            dst_ref=landing.at[way, far - 1, pl.ds(piece * chunk, chunk)],
+            send_sem=send_sem.at[way, far, piece],
+            recv_sem=recv_sem.at[way, far - 1, piece],
+            device_id={"tensor": me + 1 if way == 0 else me - 1},
+            device_id_type=MESH_IDS,
+        )
+
+    def wait_landing(way, far, piece):
+        spot = landing.at[way, far, pl.ds(piece * chunk, chunk)]
+        pltpu.make_async_remote_copy(
+            src_ref=spot,
+            dst_ref=spot,
+            send_sem=send_sem.at[way, far, piece],
+            recv_sem=recv_sem.at[way, far, piece],
+            device_id={"tensor": me - 1 if way == 0 else me + 1},
+            device_id_type=MESH_IDS,
+        ).wait_recv()
+
+    def first(way):
+        return me == 0 if way == 0 else me == parts - 1
+
+    for step in range(parts):
+        shard = jnp.where(me < parts // 2, parts - 1 - step, step)
+        place = pl.ds(pl.multiple_of(shard * rows, rows), rows)
+        total = None
+        for part in range(left_ref.shape[0]):
+            term = (dot_nt if turned else dot_nn)(left_ref[part, place, :], weight_ref[part])
+            total = term if total is None else total + term
+        product[place, :] = total.astype(NARROW)
+        far = parts - 1 - step
+        if far:
+            for way in range(2):
+
+                @pl.when(first(way))
+                def _():
+                    shard = me + far if way == 0 else me - far
+                    for piece in range(chunks):
+                        outgoing(way, far, piece, product.at[own_block(shard, piece)]).start()
+
+    def relays(way, far):
+        return (~first(way)) & ((me + far < parts) if way == 0 else (me - far >= 0))
+
+    for far in range(parts - 2, 0, -1):
+        for piece in range(chunks):
+            for way in range(2):
+
+                @pl.when(relays(way, far))
+                def _():
+                    wait_landing(way, far, piece)
+                    shard = me + far if way == 0 else me - far
+                    spot = (way, far, pl.ds(piece * chunk, chunk))
+                    landing[spot] = (
+                        landing[spot].astype(SINGLE)
+                        + product[own_block(shard, piece), :].astype(SINGLE)
+                    ).astype(NARROW)
+                    outgoing(way, far, piece, landing.at[spot]).start()
+
+    for piece in range(chunks):
+        place = pl.ds(piece * chunk, chunk)
+        out_ref[place, :] = product[own_block(me, piece), :].astype(SINGLE)
+        for way in range(2):
+
+            @pl.when(~first(way))
+            def _():
+                wait_landing(way, 0, piece)
+                out_ref[place, :] += landing[way, 0, place].astype(SINGLE)
+
+    for far in range(parts - 1, 0, -1):
+        for piece in range(chunks):
+            for way in range(2):
+                shard = me + far if way == 0 else me - far
+
+                @pl.when(first(way))
+                def _():
+                    outgoing(way, far, piece, product.at[own_block(shard, piece)]).wait_send()
+
+                if far < parts - 1:
+
+                    @pl.when(relays(way, far))
+                    def _():
+                        spot = landing.at[way, far, pl.ds(piece * chunk, chunk)]
+                        outgoing(way, far, piece, spot).wait_send()
+
+
+def scatter_rows(left, weight, turned, parts, collective_id, name):
+    chunks = 4
+    total_rows = left.shape[1]
+    rows = total_rows // parts
+    width = weight.shape[1] if turned else weight.shape[2]
+    return pl.pallas_call(
+        functools.partial(scatter_kernel, parts, chunks, turned),
+        out_shape=jax.ShapeDtypeStruct((rows, width), SINGLE),
+        in_specs=whole_vmem(2),
+        out_specs=whole_vmem(1)[0],
+        scratch_shapes=[
+            pltpu.VMEM((total_rows, width), NARROW),
+            pltpu.VMEM((2, parts - 1, rows, width), NARROW),
+            pltpu.SemaphoreType.DMA((2, parts, chunks)),
+            pltpu.SemaphoreType.DMA((2, parts, chunks)),
+        ],
+        compiler_params=pltpu.CompilerParams(
+            collective_id=collective_id, has_side_effects=True, vmem_limit_bytes=40 << 20
+        ),
+        name=name,
+    )(left, weight)
+
+
+def project_rows(values, place, extra, results):
+    weight_ref, bias_ref = extra
+    for part in range(weight_ref.shape[0]):
+        total = dot_nn(values, weight_ref[part]) + bias_ref[part]
+        results[0][part, place, :] = total.astype(NARROW)
+
+
+def expand_rows(values, place, extra, results):
+    weight_ref, bias_ref = extra
+    hidden = dot_nn(values, weight_ref[...]) + bias_ref[...]
+    cumulative = 0.5 * (1.0 + lax.erf(hidden * 0.7071067811865476))
+    density = 0.3989422804014327 * jnp.exp(-0.5 * hidden * hidden)
+    results[0][place, :] = (hidden * cumulative).astype(NARROW)
+    results[1][place, :] = cumulative + hidden * density
+
+
+def context_grad_rows(values, place, extra, results):
+    results[0][place, :] = dot_nt(values, extra[0][...]).astype(NARROW)
 
 
 TILE = 1024
@@ -282,11 +644,10 @@
         lax.all_gather(expand_weight.astype(NARROW), "dp", axis=0, tiled=True),
         lax.all_gather(reduce_weight.astype(NARROW), "dp", axis=1, tiled=True),
     )
-    qkv_joined = qkv_full.transpose(1, 0, 2).reshape(model_width, 3 * head_width)
     piece = gains_biases.shape[0]
-    params_all = lax.all_gather(
-        as_tiles(gains_biases), ("dp", "tensor"), axis=0, tiled=False
-    ).reshape(-1, TILE)[:, :piece].reshape(-1)
+    outer = lax.axis_size("dp")
+    params_all = small_gather(as_tiles(gains_biases), outer, tensor_count, 0)
+    params_all = params_all.reshape(-1, TILE)[:, :piece].reshape(-1)
 
     def segment(position):
         return params_all[position * model_width : (position + 1) * model_width]
@@ -301,30 +662,32 @@
     plain, turned, hot, back = attention_tables(rel_tables.astype(NARROW), grid_side)
     token_rows = tokens.reshape(local_rows, model_width).astype(SINGLE)
     normed_one, scaled_one, inverse_one = normalize(token_rows, segment(0), segment(1))
-    gathered_one = lax.all_gather(normed_one.astype(NARROW), "tensor", axis=0, tiled=True)
-    projected = jnp.dot(gathered_one, qkv_joined, preferred_element_type=SINGLE)
-    qkv_bias = jnp.concatenate([query_bias, jnp.zeros((head_width,), SINGLE), value_bias])
-    qkv_rows = (projected + qkv_bias).astype(NARROW)
+    qkv_bias = jnp.stack([query_bias, jnp.zeros((head_width,), SINGLE), value_bias])
+    gathered_one, qkv_rows = gather_rows(
+        normed_one.astype(NARROW),
+        (qkv_full, qkv_bias[:, None]),
+        (jax.ShapeDtypeStruct((3, seq_length, head_width), NARROW),),
+        project_rows, tensor_count, 2, "gather_project",
+    )
     context_rows, bias_wide, logsums = attend_forward(
         qkv_rows, turned, hot, heads, head_size, grid_side
     )
-    mid_rows = token_rows + (
-        lax.psum_scatter(
-            jnp.dot(context_rows, out_full, preferred_element_type=SINGLE).astype(NARROW),
-            "tensor",
-            scatter_dimension=0,
-            tiled=True,
-        ).astype(SINGLE)
-        + segment(4)
-    )
+    attn_sum = scatter_rows(context_rows[None], out_full[None], False, tensor_count, 3, "scatter_out")
+    mid_rows = token_rows + (attn_sum + segment(4))
     normed_two, scaled_two, inverse_two = normalize(mid_rows, segment(5), segment(6))
     normed_two_low = normed_two.astype(NARROW)
     expand_bias = lax.dynamic_slice_in_dim(
         params_all, 8 * model_width + tensor_index * hidden_width, hidden_width
     )
-    gathered_two = lax.all_gather(normed_two_low, "tensor", axis=0, tiled=True)
-    hidden_pre = jnp.dot(gathered_two, expand_full, preferred_element_type=SINGLE) + expand_bias
-    hidden_low = jax.nn.gelu(hidden_pre, approximate=False).astype(NARROW)
+    gathered_two, hidden_low, hidden_slope = gather_rows(
+        normed_two_low,
+        (expand_full, expand_bias[None]),
+        (
+            jax.ShapeDtypeStruct((seq_length, hidden_width), NARROW),
+            jax.ShapeDtypeStruct((seq_length, hidden_width), SINGLE),
+        ),
+        expand_rows, tensor_count, 4, "gather_expand",
+    )
     mlp_sum = lax.psum_scatter(
         jnp.dot(hidden_low, reduce_full, preferred_element_type=SINGLE).astype(jnp.bfloat16),
         "tensor",
@@ -340,7 +703,7 @@
     part_hidden = contract_cols(shard_rows, reduce_full)
     grad_hidden = part_hidden
     grad_hidden, grad_reduce = (grad_hidden, contract_rows(hidden_low, shard_rows))
-    grad_pre = (grad_hidden * gelu_slope(hidden_pre)).astype(NARROW)
+    grad_pre = (grad_hidden * hidden_slope).astype(NARROW)
     grad_expand = contract_rows(gathered_two, grad_pre)
     grad_expand_bias = jnp.sum(grad_pre, axis=0, dtype=SINGLE)
     expand_bias_full = lax.dynamic_update_slice_in_dim(
@@ -349,41 +712,32 @@
         tensor_index * hidden_width,
         0,
     )
-    grad_normed_two = lax.psum_scatter(
-        contract_cols(grad_pre, expand_full).astype(jnp.bfloat16),
-        "tensor",
-        scatter_dimension=0,
-        tiled=True,
-    ).astype(jnp.float32)
+    grad_normed_two = scatter_rows(
+        grad_pre[None], expand_full[None], True, tensor_count, 5, "scatter_expand"
+    )
     grad_mid_norm, grad_gain_two, grad_shift_two = normalize_back(
         grad_normed_two, scaled_two, inverse_two, segment(5)
     )
     grad_mid = grad_block + grad_mid_norm
     grad_attn_low = grad_mid.astype(NARROW)
     grad_out_bias = jnp.sum(grad_attn_low, axis=0, dtype=SINGLE)
-    shard_rows = lax.all_gather(grad_attn_low, "tensor", axis=0, tiled=True)
-    part_context = contract_cols(shard_rows, out_full)
-    grad_context = part_context
-    grad_context, grad_out = (grad_context, contract_rows(context_rows, shard_rows))
+    shard_rows, grad_context = gather_rows(
+        grad_attn_low,
+        (out_full,),
+        (jax.ShapeDtypeStruct((seq_length, head_width), NARROW),),
+        context_grad_rows, tensor_count, 6, "gather_context",
+    )
+    grad_out = contract_rows(context_rows, shard_rows)
     grad_qkv_rows, grad_tables = attend_backward(
-        qkv_rows, grad_context.astype(NARROW), bias_wide, logsums, plain, hot, back,
+        qkv_rows, grad_context, bias_wide, logsums, plain, hot, back,
         heads, head_size, grid_side,
     )
-    grad_query_rows = grad_qkv_rows[:, :head_width]
-    grad_value_rows = grad_qkv_rows[:, 2 * head_width :]
-    grad_query_bias = jnp.sum(grad_query_rows, axis=0, dtype=SINGLE)
-    grad_value_bias = jnp.sum(grad_value_rows, axis=0, dtype=SINGLE)
-    grad_qkv = (
-        contract_rows(gathered_one, grad_qkv_rows)
-        .reshape(model_width, 3, head_width)
-        .transpose(1, 0, 2)
-    )
-    grad_normed_one = lax.psum_scatter(
-        contract_cols(grad_qkv_rows, qkv_joined).astype(jnp.bfloat16),
-        "tensor",
-        scatter_dimension=0,
-        tiled=True,
-    ).astype(jnp.float32)
+    grad_query_bias = jnp.sum(grad_qkv_rows[0], axis=0, dtype=SINGLE)
+    grad_value_bias = jnp.sum(grad_qkv_rows[2], axis=0, dtype=SINGLE)
+    grad_qkv = jnp.stack([contract_rows(gathered_one, grad_qkv_rows[part]) for part in range(3)])
+    grad_normed_one = scatter_rows(
+        grad_qkv_rows, qkv_full, True, tensor_count, 7, "scatter_qkv"
+    )
     grad_token_norm, grad_gain_one, grad_shift_one = normalize_back(
         grad_normed_one, scaled_one, inverse_one, segment(0)
     )
@@ -414,11 +768,8 @@
     packed = jnp.concatenate(
         [grad_small.reshape(devices, piece), rel_flat.reshape(devices, rel_piece)], axis=1
     )
-    small_sum = lax.psum_scatter(
-        jax.vmap(as_tiles)(packed), ("dp", "tensor"), scatter_dimension=0, tiled=False
-    )
-    gains_grad = small_sum.reshape(-1)[:piece]
-    rel_grad = lax.all_gather(small_sum, ("dp", "tensor"), axis=0, tiled=False)
+    own_sum, rel_grad = small_sum(jax.vmap(as_tiles)(packed), outer, tensor_count, 1)
+    gains_grad = own_sum.reshape(-1)[:piece]
     rel_grad = rel_grad.reshape(devices, TILE)[:, piece : piece + rel_piece].reshape(-1)
     rel_grad = rel_grad[: rel_tables.size].reshape(rel_tables.shape)
     qkv_grad, out_grad, expand_grad, reduce_grad = (

time: 1040 us -> 629 us (0.60)
  waiting for transfers between devices: 683 us -> 81.8 us
  Pallas kernels: 34.6 us -> 382 us
  blocking collectives: 148 us -> 12.8 us
  matrix products: 81.5 us -> 32.7 us
  local copies, waits for them, and re-layouts: 28.4 us -> 64.5 us
    pallas_call x0 -> x8, Pallas kernels: none -> 348 us  [the longest x3 171 us: scatter_rows(): pl.pallas_call(functools.partial(scatter_kernel, parts, chunks, turned),...]
    reduce_scatter x4 -> x0, waiting for transfers between devices: 191 us -> none  [the longest x1 51 us: local(): lax.psum_scatter(contract_cols(grad_qkv_rows, qkv_joined).astype(jnp.bflo...]
    all_gather x2 -> x0, blocking collectives: 137 us -> none  [the longest x1 71 us: local(): lax.all_gather(as_tiles(gains_biases), ('dp', 'tensor'), axis=0, tiled=Fa...]
    all_gather x3 -> x0, waiting for transfers between devices: 136 us -> none  [the longest x1 56.8 us: local(): gathered_two = lax.all_gather(normed_two_low, 'tensor', axis=0, tiled=True)]
    unnamed x17 -> x10, waiting for transfers between devices: 124 us -> 0.81 us
    reduce_scatter x1, waiting for transfers between devices: 51.5 us -> 0.02 us  [local(): lax.psum_scatter(jnp.dot(hidden_low, reduce_full, preferred_element_type=...]
    unnamed x107 -> x169, local copies, waits for them, and re-layouts: 12.5 us -> 59.9 us
    all_gather x1, waiting for transfers between devices: 37.1 us -> 0.01 us  [local(): shard_rows = lax.all_gather(cotangent_rows, 'tensor', axis=0, tiled=True)]
  transfers between devices with their start and end apart: 16 -> 9, of which waited for: 15 -> 3; matrix products, arithmetic and copies ran while one was open for 9% -> 12% of each run, Pallas kernels for 2% -> 62%
where the time goes in v2:
time: 629 us; the launch traced here: 620 us
  Pallas kernels  382 us (61%)
  waiting for transfers between devices  81.8 us (13%)
  local copies, waits for them, and re-layouts  64.5 us (10%)
  matrix products  32.7 us (5%)
  other arithmetic  29.8 us (5%)
  between operations  15.4 us (2%)
  blocking collectives  12.8 us (2%)
    pallas_call x3, Pallas kernels, scatter_rows(): pl.pallas_call(functools.partial(scatter_kernel, parts, chunks, turned),...  171 us
    pallas_call x3, Pallas kernels, gather_rows(): pl.pallas_call(functools.partial(gather_kernel, parts, chunks, len(extra)...  147 us
    unnamed x169, local copies, waits for them, and re-layouts  59.9 us
    reduce_scatter x1, waiting for transfers between devices, local(): lax.psum_scatter(grad_reduce.astype(NARROW), 'dp', scatter_dimension=1, t...  45.8 us
    all_gather x1, waiting for transfers between devices, local(): lax.all_gather(reduce_weight.astype(NARROW), 'dp', axis=1, tiled=True)  32.8 us
    dot_general x6, matrix products, contract_rows(): lax.dot_general(left_side, right_side, (((0,), (0,)), ((), ())), preferre...  18.7 us
    pallas_call x1, Pallas kernels, attend_backward(): pl.pallas_call(functools.partial(backward_kernel, heads, size, grid_side,...  18.3 us
    pallas_call x1, Pallas kernels, small_sum(): pl.pallas_call(functools.partial(small_sum_kernel, outer, inner), out_sha...  17.8 us
  transfers between devices with their start and end apart: 9, of which 3 were waited for; matrix products, arithmetic and copies ran while one was open for 12% of the time, Pallas kernels for 62%

profile of v2, /device:TPU:0, one launch (start us, length us, event | category | flops | bytes accessed | tf_op | source)
XLA Modules:
  0.0 619.7 jit_solution(6002919620833430684)
XLA Ops:
  7.3 2.0 convert_element_type.97
  9.3 0.8 convert_element_type.102
  10.2 0.7 all-gather.12.cloned.1.call-update
  11.5 13.2 %small_gather.1 = f32[32,8,128]{2,1,0:T(8,128)} custom-call(f32[8,128]{1,0:T(8,128)} %pad_bitcast_fusion.own_ref), custom_call_target="tpu_custom_call" | custom-call | tf_op jit(solution)/shard_map/small_gather/pallas_call | solution.py:309
  24.7 0.9 copy.115
  26.2 12.8 %all_gather.16 = bf16[320,1280]{0,1:T(8,128)(2,1)S(1)} all-gather(bf16[320,160]{0,1:T(8,128)(2,1)S(1)} %convert_element_type.100), channel_id=1, replica_groups=mesh['dp'=8,'tensor'=4] {'dp'}, dimensions={1}, use_global_device_ids=true | all-gather | bytes 921600 | tf_op jit(solution)/shard_map/all_gather | solution.py:643
  40.9 2.2 fusion.35
  43.5 2.2 all-gather.6.cloned.1.call-done.refs_0_.weight_ref
  45.7 1.8 copy-done.2
  47.5 48.0 %gather_project.1 = (bf16[1024,1280]{1,0:T(8,128)(2,1)S(1)}, bf16[3,1024,320]{2,1,0:T(8,128)(2,1)S(1)}) custom-call(bf16[256,1280]{1,0:T(8,128)(2,1)S(1)} %fusion.14.own_ref, bf16[3,1280,320]{2,1,0:T(8,128)(2,1)S(1)} %copy-done.2, f32[3,1,320]{2,1,0:T(1,128)S(1)} %broadcast_in_dim.16.refs_1_), custom_call_target="tpu_custom_call" | custom-call | tf_op jit(solution)/shard_map/gather_project/pallas_call | solution.py:438
  95.6 1.5 copy-done.23
  97.1 15.5 %attend_forward.1 = (bf16[1024,320]{1,0:T(8,128)(2,1)S(1)}, bf16[4,1024,128]{2,1,0:T(8,128)(2,1)S(1)}, f32[4,1,1024]{2,1,0:T(1,128)S(1)}) custom-call(bf16[3,1024,320]{2,1,0:T(8,128)(2,1)S(1)} %get-tuple-element.40.qkv_ref, bf16[128,80]{1,0:T(8,128)(2,1)S(1)} %bitcast.112, bf16[1024,128]{1,0:T(8,128)(2,1)S(1)} %get-tuple-element.181.hot_ref), custom_call_target="tpu_custom_call" | custom-call | tf_op jit(solution)/shard_map/attend_forward/pallas_call | solution.py:187
  112.6 62.7 %scatter_out.1 = f32[256,1280]{1,0:T(8,128)S(1)} custom-call(bf16[1,1024,320]{2,1,0:T(8,128)(2,1)S(1)} %bitcast.110, bf16[1,320,1280]{2,1,0:T(8,128)(2,1)S(1)} %bitcast.108), custom_call_target="tpu_custom_call" | custom-call | tf_op jit(solution)/shard_map/scatter_out/pallas_call | solution.py:558
  175.9 0.8 copy-done.29
  177.1 1.9 copy-done
  179.0 49.5 %gather_expand.1 = (bf16[1024,1280]{1,0:T(8,128)(2,1)S(1)}, bf16[1024,1280]{1,0:T(8,128)(2,1)S(1)}, f32[1024,1280]{1,0:T(8,128)S(1)}) custom-call(bf16[256,1280]{1,0:T(8,128)(2,1)S(1)} %add_convert_fusion.1.own_ref, bf16[1280,1280]{1,0:T(8,128)(2,1)S(1)} %copy-done, f32[1,1280]{1,0:T(1,128)S(1)} %broadcast_in_dim.19.refs_1_), custom_call_target="tpu_custom_call" | custom-call | tf_op jit(solution)/shard_map/gather_expand/pallas_call | solution.py:438
  228.5 2.3 copy-done.22
  230.9 1.5 copy-done.25
  232.4 1.5 copy-done.27
  233.9 7.8 %convolution_convert_fusion = bf16[1280,1280]{0,1:T(8,128)(2,1)} fusion(bf16[1024,1280]{1,0:T(8,128)(2,1)} %copy-done.27, bf16[1024,1,1280]{2,0,1:T(8,128)(2,1)} %all-gather.12.cloned.1.call-done), kind=kOutput, calls=%fused_computation | convolution fusion | flops 3357081600 | bytes 8519680 | tf_op jit(solution)/shard_map/dot_general | solution.py:40
  241.8 45.8 %reduce-scatter.14.cloned.1.call-done = bf16[1280,160]{0,1:T(8,128)(2,1)} async-done(((bf16[1280,1280]{0,1:T(8,128)(2,1)}), bf16[1280,160]{0,1:T(8,128)(2,1)}) %reduce-scatter.14.cloned.1.call-update) | async-done | bytes 409616 | tf_op jit(solution)/shard_map/reduce_scatter | solution.py:779
  287.6 4.0 add_multiply_fusion.1
  291.7 32.8 %all-gather.10.cloned.1.call-done = bf16[1280,1280]{0,1:T(8,128)(2,1)} async-done(((bf16[1280,160]{0,1:T(8,128)(2,1)}), bf16[1280,1280]{0,1:T(8,128)(2,1)}) %all-gather.10.cloned.1.call-update) | async-done | bytes 3276816 | tf_op jit(solution)/shard_map/all_gather | solution.py:645
  324.6 6.8 %convolution_convert_fusion.2 = bf16[1024,1280]{1,0:T(8,128)(2,1)} fusion(bf16[1024,1280]{1,0:T(8,128)(2,1)S(1)} %copy-done.28, bf16[1280,1280]{0,1:T(8,128)(2,1)} %all-gather.10.cloned.1.call-done), kind=kOutput, calls=%fused_computation.4 | convolution fusion | flops 3356753920 | bytes 8519680 | tf_op jit(solution)/shard_map/dot_general | solution.py:692
  331.5 1.7 copy-done.69
  333.1 7.2 %convert_reduce_fusion = (f32[1280]{0:T(1024)}, bf16[1024,1280]{1,0:T(8,128)(2,1)S(1)}) fusion(f32[1024,1280]{1,0:T(8,128)} %copy-done.22, bf16[1280,1280]{0,1:T(8,128)(2,1)} %all-gather.10.cloned.1.call-done, bf16[1024,1,1280]{2,0,1:T(8,128)(2,1)S(1)} %copy-done.69), kind=kOutput, calls=%fused_computation.2 | convolution fusion | flops 3360684800 | bytes 13767680 | tf_op jit(solution)/shard_map/dot_general | solution.py:46
  340.4 5.1 convolution_convert_fusion.1
  345.4 1.4 copy-done.14
  347.0 1.0 copy-done.40
  348.0 1.3 copy.80
  349.9 2.6 copy.79
  352.6 2.4 copy.83
  355.0 1.8 convert_reduce_fusion.1
  356.8 1.7 copy-done.15
  358.5 64.0 %scatter_expand.1 = f32[256,1280]{1,0:T(8,128)S(1)} custom-call(bf16[1,1024,1280]{2,1,0:T(8,128)(2,1)S(1)} %bitcast.109, bf16[1,1280,1280]{2,1,0:T(8,128)(2,1)S(1)} %bitcast.107), custom_call_target="tpu_custom_call" | custom-call | tf_op jit(solution)/shard_map/scatter_expand/pallas_call | solution.py:558
  422.5 1.0 copy-done.6
  423.6 0.9 dynamic_update_slice.11
  424.5 2.4 multiply_reduce_fusion
  427.1 3.6 convert_reduce_fusion.5
  430.7 49.0 %gather_context.1 = (bf16[1024,1280]{1,0:T(8,128)(2,1)S(1)}, bf16[1024,320]{1,0:T(8,128)(2,1)S(1)}) custom-call(bf16[256,1280]{1,0:T(8,128)(2,1)S(1)} %get-tuple-element.163.own_ref, bf16[320,1280]{1,0:T(8,128)(2,1)S(1)} %copy-done.10), custom_call_target="tpu_custom_call" | custom-call | tf_op jit(solution)/shard_map/gather_context/pallas_call | solution.py:438
  479.8 2.6 convolution_convert_fusion.3
  482.6 18.3 %attend_backward.1 = (bf16[3,1024,320]{2,1,0:T(8,128)(2,1)S(1)}, f32[128,80]{1,0:T(8,128)S(1)}) custom-call(bf16[3,1024,320]{2,1,0:T(8,128)(2,1)} %copy-done.8, bf16[1024,320]{1,0:T(8,128)(2,1)S(1)} %get-tuple-element.44.grad_ref, bf16[4,1024,128]{2,1,0:T(8,128)(2,1)S(1)} %copy-done.18, f32[4,1,1024]{2,1,0:T(1,128)S(1)} %get-tuple-element.46.lse_ref, ...), custom_call_target="tpu_custom_call" | custom-call | tf_op jit(solution)/shard_map/attend_backward/pallas_call | solution.py:210
  500.9 1.1 fusion.2
  502.0 1.1 fusion.3
  503.1 1.1 fusion.4
  504.4 6.3 %copy.94 = bf16[3,1280,320]{2,0,1:T(4,128)(2,1)} copy(bf16[3,1280,320]{1,2,0:T(8,128)(2,1)S(1)} %pad_maximum_fusion) | data formatting | bytes 4915200
  510.7 8.3 %reshape.160 = bf16[1280,960]{1,0:T(8,128)(2,1)} reshape(bf16[1280,3,320]{2,1,0:T(4,128)(2,1)} %bitcast.114) | data formatting | bytes 4915200
  519.1 3.8 add_multiply_fusion.2
  523.7 1.7 copy-done.13
  525.4 44.2 %scatter_qkv.1 = f32[256,1280]{1,0:T(8,128)S(1)} custom-call(bf16[3,1024,320]{2,1,0:T(8,128)(2,1)S(1)} %copy-done.13, bf16[3,1280,320]{2,1,0:T(8,128)(2,1)S(1)} %copy-done.3), custom_call_target="tpu_custom_call" | custom-call | tf_op jit(solution)/shard_map/scatter_qkv/pallas_call | solution.py:558
  569.6 1.1 copy-done.4
  572.0 0.7 copy.99
  572.7 17.8 %small_sum.1 = (f32[8,128]{1,0:T(8,128)}, f32[32,8,128]{2,1,0:T(8,128)}) custom-call(f32[32,8,128]{2,1,0:T(8,128)} %bitcast.116), custom_call_target="tpu_custom_call" | custom-call | tf_op jit(solution)/shard_map/small_sum/pallas_call | solution.py:322
  590.4 0.9 copy.114
  594.4 1.8 fusion.19
  596.2 2.4 copy.85
  599.3 1.9 add_multiply_fusion.3
  601.2 2.2 reshape.161
  603.4 1.4 copy.95
  604.8 1.1 copy.86
  605.9 1.8 add_multiply_fusion
  607.8 2.5 copy.88
  610.3 1.2 copy.90
  611.5 1.2 copy.92
  (218 shorter events, 11.5 us)
Async XLA Ops:
  7.2 2.1 copy-start.39
  7.2 38.5 %all-gather.6.cloned.1.call-start = ((), (), s32[]{:S(2)}) async-start(), calls=%async_computation.5 | async-start | bytes 3317760 | tf_op jit(solution)/shard_map/all_gather | solution.py:642
  9.2 16.8 %copy-start.43 = (f32[2,63,80]{2,0,1:T(2,128)S(1)}, f32[2,63,80]{2,0,1:T(2,128)}, u32[]{:S(2)}) copy-start(f32[2,63,80]{2,0,1:T(2,128)} %param.27) | copy-start | bytes 120964
  9.3 167.8 %all-gather.8.cloned.1.call-start = ((), (), s32[]{:S(2)}) async-start(), calls=%async_computation.6 | async-start | bytes 3686400 | tf_op jit(solution)/shard_map/all_gather | solution.py:644
  10.1 16.0 %copy-start.41 = (f32[320,160]{0,1:T(8,128)S(1)}, f32[320,160]{0,1:T(8,128)}, u32[]{:S(2)}) copy-start(f32[320,160]{0,1:T(8,128)} %param.23) | copy-start | bytes 614404
  10.1 223.8 %all-gather.12.cloned.1.call-start = ((), (), s32[]{:S(2)}) async-start(), calls=%async_computation.12 | async-start | bytes 3276800 | tf_op jit(solution)/shard_map/all_gather | solution.py:702
  10.9 276.8 %reduce-scatter.14.cloned.1.call-start = ((), (), s32[]{:S(2)}) async-start(), calls=%async_computation.11 | async-start | bytes 3686400 | tf_op jit(solution)/shard_map/reduce_scatter | solution.py:779
  26.2 14.2 %copy-start.31 = (bf16[256,1,1280]{2,0,1:T(8,128)(2,1)S(1)}, bf16[256,1,1280]{2,0,1:T(8,128)(2,1)}, u32[]{:S(2)}) copy-start(bf16[256,1,1280]{2,0,1:T(8,128)(2,1)} %param.20) | copy-start | bytes 1966084
  39.6 73.0 %copy-start.9 = (bf16[320,1280]{1,0:T(8,128)(2,1)}, bf16[320,1280]{1,0:T(8,128)(2,1)S(1)}, u32[]{:S(2)}) copy-start(bf16[320,1280]{1,0:T(8,128)(2,1)S(1)} %copy.76.refs_0_) | copy-start | bytes 2457604
  40.3 3.2 copy-start.47
  40.3 135.7 %copy-start.49 = (f32[1280]{0:T(1024)}, f32[1280]{0:T(1024)S(1)}, u32[]{:S(2)}) copy-start(f32[1280]{0:T(1024)S(1)} %get-tuple-element.174) | copy-start | bytes 15364
  40.6 55.0 %copy-start.58 = (f32[256]{0:T(256)}, f32[256]{0:T(256)S(1)}, u32[]{:S(2)}) copy-start(f32[256]{0:T(256)S(1)} %broadcast_multiply_fusion.5) | copy-start | bytes 3076
  40.9 54.7 %copy-start.62 = (f32[256]{0:T(256)}, f32[256]{0:T(256)S(1)}, u32[]{:S(2)}) copy-start(f32[256]{0:T(256)S(1)} %add_rsqrt_fusion.1) | copy-start | bytes 3076
  45.7 1.8 copy-start.2
  97.0 15.5 %copy-start.8 = (bf16[3,1024,320]{2,1,0:T(8,128)(2,1)}, bf16[3,1024,320]{2,1,0:T(8,128)(2,1)S(1)}, u32[]{:S(2)}) copy-start(bf16[3,1024,320]{2,1,0:T(8,128)(2,1)S(1)} %get-tuple-element.40.qkv_ref) | copy-start | bytes 5898244
  112.5 62.8 %copy-start.17 = (bf16[4,1024,128]{2,1,0:T(8,128)(2,1)}, bf16[4,1024,128]{2,1,0:T(8,128)(2,1)S(1)}, u32[]{:S(2)}) copy-start(bf16[4,1024,128]{2,1,0:T(8,128)(2,1)S(1)} %get-tuple-element.45.bias_ref) | copy-start | bytes 3145732
  112.6 62.8 %copy-start.19 = (bf16[1024,320]{1,0:T(8,128)(2,1)}, bf16[1024,320]{1,0:T(8,128)(2,1)S(1)}, u32[]{:S(2)}) copy-start(bf16[1024,320]{1,0:T(8,128)(2,1)S(1)} %get-tuple-element.41) | copy-start | bytes 1966084
  175.9 52.6 %copy-start.60 = (f32[256]{0:T(256)}, f32[256]{0:T(256)S(1)}, u32[]{:S(2)}) copy-start(f32[256]{0:T(256)S(1)} %add_rsqrt_fusion) | copy-start | bytes 3076
  177.0 1.9 copy-start
  228.5 2.3 copy-start.22
  241.8 82.8 %copy-start.28 = (bf16[1024,1280]{1,0:T(8,128)(2,1)S(1)}, bf16[1024,1280]{1,0:T(8,128)(2,1)}, u32[]{:S(2)}) copy-start(bf16[1024,1280]{1,0:T(8,128)(2,1)} %copy-done.27) | copy-start | bytes 7864324
  241.8 82.8 %all-gather.10.cloned.1.call-start = ((), (), s32[]{:S(2)}) async-start(), calls=%async_computation.7 | async-start | bytes 3686400 | tf_op jit(solution)/shard_map/all_gather | solution.py:645
  291.7 135.3 %reduce-scatter.8.cloned.1.call-start = ((), (), s32[]{:S(2)}) async-start(), calls=%async_computation.8 | async-start | bytes 3276800 | tf_op jit(solution)/shard_map/reduce_scatter | solution.py:691
  331.4 187.6 %reduce-scatter.12.cloned.1.call-start = ((), (), s32[]{:S(2)}) async-start(), calls=%async_computation.10 | async-start | bytes 3686400 | tf_op jit(solution)/shard_map/reduce_scatter | solution.py:778
  333.1 7.2 %copy-start.26 = (bf16[1024,1280]{1,0:T(8,128)(2,1)S(1)}, bf16[1024,1280]{1,0:T(8,128)(2,1)}, u32[]{:S(2)}) copy-start(bf16[1024,1280]{1,0:T(8,128)(2,1)} %copy-done.25) | copy-start | bytes 7864324
  346.9 252.3 %reduce-scatter.10.cloned.1.call-start = ((), (), s32[]{:S(2)}) async-start(), calls=%async_computation.9 | async-start | bytes 1105920 | tf_op jit(solution)/shard_map/reduce_scatter | solution.py:777
  349.9 6.9 %copy-start.1 = (bf16[1280,1280]{1,0:T(8,128)(2,1)S(1)}, bf16[1280,1280]{1,0:T(8,128)(2,1)}, u32[]{:S(2)}) copy-start(bf16[1280,1280]{1,0:T(8,128)(2,1)} %all-gather.8.cloned.1.call-done.refs_0_) | copy-start | bytes 9830404
  424.4 2.6 copy-start.7
  424.4 2.6 copy-start.30
  424.5 2.6 copy-start.50
  424.5 2.6 copy-start.54
  424.5 2.6 copy-start.57
  424.5 2.6 copy-start.61
  427.1 3.6 copy-start.10
  430.7 49.0 %copy-start.20 = (bf16[1024,320]{1,0:T(8,128)(2,1)S(1)}, bf16[1024,320]{1,0:T(8,128)(2,1)}, u32[]{:S(2)}) copy-start(bf16[1024,320]{1,0:T(8,128)(2,1)} %copy-done.19) | copy-start | bytes 1966084
  479.7 2.8 copy-start.16
  479.7 2.8 copy-start.18
  479.8 2.8 copy-start.21
  482.3 118.8 %reduce-scatter.16.cloned.1.call-start = ((), (), s32[]{:S(2)}) async-start(), calls=%async_computation.13 | async-start | bytes 2949120
  482.6 18.3 %copy-start.24 = (bf16[1024,1280]{1,0:T(8,128)(2,1)S(1)}, bf16[1024,1280]{1,0:T(8,128)(2,1)}, u32[]{:S(2)}) copy-start(bf16[1024,1280]{1,0:T(8,128)(2,1)} %copy-done.23) | copy-start | bytes 7864324
  500.9 2.2 copy-start.11
  519.1 3.8 copy-start.12
  519.1 4.6 copy-start.3
  525.4 45.3 %copy-start.32 = (bf16[256,1,1280]{2,0,1:T(8,128)(2,1)S(1)}, bf16[256,1,1280]{2,0,1:T(8,128)(2,1)}, u32[]{:S(2)}) copy-start(bf16[256,1,1280]{2,0,1:T(8,128)(2,1)} %param.20) | copy-start | bytes 1966084
  525.4 45.3 %copy-start.48 = (f32[1280]{0:T(1024)S(1)}, f32[1280]{0:T(1024)}, u32[]{:S(2)}) copy-start(f32[1280]{0:T(1024)} %copy-done.47) | copy-start | bytes 15364
  525.4 45.3 %copy-start.59 = (f32[256]{0:T(256)S(1)}, f32[256]{0:T(256)}, u32[]{:S(2)}) copy-start(f32[256]{0:T(256)} %copy-done.58) | copy-start | bytes 3076
  525.4 45.3 %copy-start.63 = (f32[256]{0:T(256)S(1)}, f32[256]{0:T(256)}, u32[]{:S(2)}) copy-start(f32[256]{0:T(256)} %copy-done.62) | copy-start | bytes 3076
  570.7 21.6 %copy-start.44 = (f32[2,63,80]{2,0,1:T(2,128)S(1)}, f32[2,63,80]{2,0,1:T(2,128)}, u32[]{:S(2)}) copy-start(f32[2,63,80]{2,0,1:T(2,128)} %param.27) | copy-start | bytes 120964
  570.7 21.6 %copy-start.51 = (f32[2,63,80]{2,0,1:T(2,128)S(1)}, f32[2,63,80]{2,0,1:T(2,128)}, u32[]{:S(2)}) copy-start(f32[2,63,80]{2,0,1:T(2,128)} %param.39) | copy-start | bytes 120964
  570.7 21.6 %copy-start.52 = (f32[2,63,80]{2,0,1:T(2,128)S(1)}, f32[2,63,80]{2,0,1:T(2,128)}, u32[]{:S(2)}) copy-start(f32[2,63,80]{2,0,1:T(2,128)} %param.33) | copy-start | bytes 120964
  571.4 23.0 %copy-start.5 = (f32[256,1280]{1,0:T(8,128)S(1)}, f32[256,1280]{1,0:T(8,128)}, u32[]{:S(2)}) copy-start(f32[256,1280]{1,0:T(8,128)} %copy-done.4) | copy-start | bytes 3932164
  571.4 23.0 %copy-start.33 = (bf16[256,1,1280]{2,0,1:T(8,128)(2,1)S(1)}, bf16[256,1,1280]{2,0,1:T(8,128)(2,1)}, u32[]{:S(2)}) copy-start(bf16[256,1,1280]{2,0,1:T(8,128)(2,1)} %param.20) | copy-start | bytes 1966084
  596.2 2.5 copy-start.65
  596.2 2.5 copy-start.66
  596.2 2.5 copy-start.67
  596.2 2.5 copy-start.68
  596.2 3.1 copy-start.42
  596.2 3.0 copy-start.45
  596.2 3.0 copy-start.46
  601.2 4.7 copy-start.36
  603.4 2.5 copy-start.34
  603.4 2.5 copy-start.35
  607.8 2.6 copy-start.38
  607.8 3.8 copy-start.37
  (15 other events, 20.4 us)
Sparse Core Ops, SparseCore 0:
  10.5 35.1 all-gather.5
  48.2 32.0 all-gather.7
  81.8 70.4 all-gather.11
  241.9 45.6 reduce-scatter.13
  291.8 32.7 all-gather.9
  331.5 69.2 reduce-scatter.7
  404.2 48.9 reduce-scatter.11
  482.5 34.4 reduce-scatter.9
  520.3 43.5 reduce-scatter.15

commit v3 on v2

--- a/solution.py
+++ b/solution.py
@@ -249,7 +249,7 @@
     pl.semaphore_wait(barrier, count - 1)
 
 
-def exchange(me, count, inner, source, target, send_sem, recv_sem):
+def exchange_parts(me, count, inner, source, target, send_sem, recv_sem):
     def piece(step):
         other = (me + step) % count
         return pltpu.make_async_remote_copy(
@@ -278,16 +278,32 @@
         piece(step).wait_send()
         return carry
 
-    lax.fori_loop(1, count, start, 0)
-    lax.fori_loop(1, count, finish, 0)
-
-
-def small_gather_kernel(outer, inner, own_ref, all_ref, send_sem, recv_sem):
-    count = outer * inner
-    me = lax.axis_index("dp") * inner + lax.axis_index("tensor")
-    greet_all(me, count, inner)
-    all_ref[me] = own_ref[...]
-    exchange(me, count, inner, lambda other: own_ref, all_ref, send_sem, recv_sem)
+    return (
+        lambda: lax.fori_loop(1, count, start, 0),
+        lambda: lax.fori_loop(1, count, finish, 0),
+    )
+
+
+def exchange(*parts):
+    start, finish = exchange_parts(*parts)
+    start()
+    finish()
+
+
+def first_gather_kernel(
+    outer, parts, chunks, own_ref, small_ref, all_ref, small_all_ref,
+    send_sem, recv_sem, small_send, small_recv,
+):
+    count = outer * parts
+    me = lax.axis_index("dp") * parts + lax.axis_index("tensor")
+    greet_all(me, count, parts)
+    start, finish = exchange_parts(
+        me, count, parts, lambda other: small_ref, small_all_ref, small_send, small_recv
+    )
+    start()
+    small_all_ref[me] = small_ref[...]
+    relay_rows(parts, chunks, own_ref, all_ref, send_sem, recv_sem, lambda values, place: None)
+    finish()
 
 
 def small_sum_kernel(
@@ -304,17 +320,22 @@
     exchange(me, count, inner, lambda other: total_ref, all_ref, send_two, recv_two)
 
 
-def small_gather(own, outer, inner, collective_id):
-    count = outer * inner
+def first_gather(own, small, outer, parts, collective_id):
+    chunks = 4
+    count = outer * parts
     return pl.pallas_call(
-        functools.partial(small_gather_kernel, outer, inner),
-        out_shape=jax.ShapeDtypeStruct((count,) + own.shape, own.dtype),
-        in_specs=whole_vmem(1),
-        out_specs=whole_vmem(1)[0],
-        scratch_shapes=[pltpu.SemaphoreType.DMA((count,))] * 2,
+        functools.partial(first_gather_kernel, outer, parts, chunks),
+        out_shape=(
+            jax.ShapeDtypeStruct((parts * own.shape[0], own.shape[1]), own.dtype),
+            jax.ShapeDtypeStruct((count,) + small.shape, small.dtype),
+        ),
+        in_specs=whole_vmem(2),
+        out_specs=tuple(whole_vmem(2)),
+        scratch_shapes=[pltpu.SemaphoreType.DMA((2, parts, chunks))] * 2
+        + [pltpu.SemaphoreType.DMA((count,))] * 2,
         compiler_params=pltpu.CompilerParams(collective_id=collective_id, has_side_effects=True),
-        name="small_gather",
-    )(own)
+        name="first_gather",
+    )(own, small)
 
 
 def small_sum(packed, outer, inner, collective_id):
@@ -359,10 +380,17 @@
     all_ref = refs[inputs]
     results = refs[inputs + 1 : -2]
     send_sem, recv_sem = refs[-2:]
+    greet_line(lax.axis_index("tensor"), parts)
+    relay_rows(
+        parts, chunks, own_ref, all_ref, send_sem, recv_sem,
+        lambda values, place: finish_rows(values, place, extra, results),
+    )
+
+
+def relay_rows(parts, chunks, own_ref, all_ref, send_sem, recv_sem, finish_rows):
     me = lax.axis_index("tensor")
     rows = own_ref.shape[0]
     chunk = rows // chunks
-    greet_line(me, parts)
 
     def block(shard, piece):
         return all_ref.at[pl.ds(pl.multiple_of(shard * rows + piece * chunk, chunk), chunk)]
@@ -414,7 +442,7 @@
         if step == 0:
             mine = pl.ds(pl.multiple_of(me * rows, rows), rows)
             all_ref[mine, :] = own_ref[...]
-            finish_rows(own_ref[...], mine, extra, results)
+            finish_rows(own_ref[...], mine)
         else:
             for way in range(2):
 
@@ -422,7 +450,7 @@
                 def _():
                     shard = me - step if way == 0 else me + step
                     place = pl.ds(pl.multiple_of(shard * rows, rows), rows)
-                    finish_rows(all_ref[place, :], place, extra, results)
+                    finish_rows(all_ref[place, :], place)
 
     for step in range(parts - 1):
         for piece in range(chunks):
@@ -638,15 +666,18 @@
     hidden_width = expand_weight.shape[1]
     head_size = rel_tables.shape[2]
     grid_side = (rel_tables.shape[1] + 1) // 2
-    qkv_full, out_full, expand_full, reduce_full = (
-        lax.all_gather(qkv_weight.astype(NARROW), "dp", axis=1, tiled=True),
-        lax.all_gather(out_weight.astype(NARROW), "dp", axis=1, tiled=True),
-        lax.all_gather(expand_weight.astype(NARROW), "dp", axis=0, tiled=True),
-        lax.all_gather(reduce_weight.astype(NARROW), "dp", axis=1, tiled=True),
-    )
+    qkv_full = lax.all_gather(qkv_weight.astype(NARROW), "dp", axis=1, tiled=True)
+    columns_full = lax.all_gather(
+        jnp.concatenate([out_weight, reduce_weight]).astype(NARROW), "dp", axis=1, tiled=True
+    )
+    out_full, reduce_full = (columns_full[:head_width], columns_full[head_width:])
+    expand_full = lax.all_gather(expand_weight.astype(NARROW), "dp", axis=0, tiled=True)
     piece = gains_biases.shape[0]
     outer = lax.axis_size("dp")
-    params_all = small_gather(as_tiles(gains_biases), outer, tensor_count, 0)
+    cotangent_rows = cotangent.reshape(local_rows, model_width)
+    output_grads, params_all = first_gather(
+        cotangent_rows, as_tiles(gains_biases), outer, tensor_count, 0
+    )
     params_all = params_all.reshape(-1, TILE)[:, :piece].reshape(-1)
 
     def segment(position):
@@ -688,18 +719,10 @@
         ),
         expand_rows, tensor_count, 4, "gather_expand",
     )
-    mlp_sum = lax.psum_scatter(
-        jnp.dot(hidden_low, reduce_full, preferred_element_type=SINGLE).astype(jnp.bfloat16),
-        "tensor",
-        scatter_dimension=0,
-        tiled=True,
-    ).astype(jnp.float32)
-    block_rows = mid_rows + (mlp_sum + segment(7))
-    block_out = block_rows.astype(NARROW).reshape(tokens.shape)
-    cotangent_rows = cotangent.reshape(local_rows, model_width)
+    mlp_part = jnp.dot(hidden_low, reduce_full, preferred_element_type=SINGLE).astype(NARROW)
     grad_block = cotangent_rows.astype(SINGLE)
     grad_reduce_bias = jnp.sum(grad_block, axis=0)
-    shard_rows = lax.all_gather(cotangent_rows, "tensor", axis=0, tiled=True)
+    shard_rows = output_grads
     part_hidden = contract_cols(shard_rows, reduce_full)
     grad_hidden = part_hidden
     grad_hidden, grad_reduce = (grad_hidden, contract_rows(hidden_low, shard_rows))
@@ -712,6 +735,13 @@
         tensor_index * hidden_width,
         0,
     )
+    grad_reduce, grad_expand = (grad_reduce.astype(NARROW), grad_expand.astype(NARROW))
+    grad_pre, grad_reduce, mlp_part, grad_expand = lax.optimization_barrier(
+        (grad_pre, grad_reduce, mlp_part, grad_expand)
+    )
+    reduce_sum = lax.psum_scatter(grad_reduce, "dp", scatter_dimension=1, tiled=True)
+    mlp_sum = lax.psum_scatter(mlp_part, "tensor", scatter_dimension=0, tiled=True)
+    expand_sum = lax.psum_scatter(grad_expand, "dp", scatter_dimension=0, tiled=True)
     grad_normed_two = scatter_rows(
         grad_pre[None], expand_full[None], True, tensor_count, 5, "scatter_expand"
     )
@@ -727,14 +757,26 @@
         (jax.ShapeDtypeStruct((seq_length, head_width), NARROW),),
         context_grad_rows, tensor_count, 6, "gather_context",
     )
-    grad_out = contract_rows(context_rows, shard_rows)
+    grad_out = contract_rows(context_rows, shard_rows).astype(NARROW)
+    late_rows = lax.optimization_barrier((mid_rows, shard_rows))[0]
+    block_rows = late_rows + (mlp_sum.astype(SINGLE) + segment(7))
+    block_out = block_rows.astype(NARROW).reshape(tokens.shape)
+    grad_context, grad_out, reduce_sum = lax.optimization_barrier(
+        (grad_context, grad_out, reduce_sum)
+    )
     grad_qkv_rows, grad_tables = attend_backward(
         qkv_rows, grad_context, bias_wide, logsums, plain, hot, back,
         heads, head_size, grid_side,
     )
     grad_query_bias = jnp.sum(grad_qkv_rows[0], axis=0, dtype=SINGLE)
     grad_value_bias = jnp.sum(grad_qkv_rows[2], axis=0, dtype=SINGLE)
-    grad_qkv = jnp.stack([contract_rows(gathered_one, grad_qkv_rows[part]) for part in range(3)])
+    grad_qkv = jnp.concatenate(
+        [contract_rows(gathered_one, grad_qkv_rows[part]).astype(NARROW) for part in range(3)],
+        axis=1,
+    )
+    grad_qkv_rows, grad_qkv, block_out = lax.optimization_barrier(
+        (grad_qkv_rows, grad_qkv, block_out)
+    )
     grad_normed_one = scatter_rows(
         grad_qkv_rows, qkv_full, True, tensor_count, 7, "scatter_qkv"
     )
@@ -773,11 +815,17 @@
     rel_grad = rel_grad.reshape(devices, TILE)[:, piece : piece + rel_piece].reshape(-1)
     rel_grad = rel_grad[: rel_tables.size].reshape(rel_tables.shape)
     qkv_grad, out_grad, expand_grad, reduce_grad = (
-        lax.psum_scatter(grad_qkv.astype(NARROW), "dp", scatter_dimension=1, tiled=True).astype(SINGLE),
+        lax.psum_scatter(grad_qkv, "dp", scatter_dimension=0, tiled=True)
+        .astype(SINGLE)
+        .reshape(-1, 3, head_width)
+        .transpose(1, 0, 2),
         lax.psum_scatter(grad_out.astype(NARROW), "dp", scatter_dimension=1, tiled=True).astype(SINGLE),
-        lax.psum_scatter(grad_expand.astype(NARROW), "dp", scatter_dimension=0, tiled=True).astype(SINGLE),
-        lax.psum_scatter(grad_reduce.astype(NARROW), "dp", scatter_dimension=1, tiled=True).astype(SINGLE),
-    )
+        expand_sum.astype(SINGLE),
+        reduce_sum.astype(SINGLE),
+    )
+    reduce_moment = lax.optimization_barrier((reduce_moment, grad_normed_two))[0]
+    expand_moment = lax.optimization_barrier((expand_moment, grad_tables))[0]
+    out_moment = lax.optimization_barrier((out_moment, grad_normed_one))[0]
     new_qkv, moment_qkv, average_qkv = advance(
         qkv_weight, qkv_moment, qkv_average, qkv_grad, RATE_MAIN
     )

time: 629 us -> 573 us (0.911)
  waiting for transfers between devices: 81.8 us -> 1.21 us
  Pallas kernels: 382 us -> 415 us
  blocking collectives: 12.8 us -> 0 us
  local copies, waits for them, and re-layouts: 64.5 us -> 72.6 us
    reduce_scatter x4 -> x2, waiting for transfers between devices: 45.8 us -> 0.02 us  [the longest x1 0.02 us: local(): lax.psum_scatter(grad_expand, 'dp', scatter_dimension=0, tiled=True)]
    pallas_call x1, Pallas kernels: 13.2 us -> 56.7 us  [first_gather(): pl.pallas_call(functools.partial(first_gather_kernel, outer, parts, chunk...]
    pallas_call x3, Pallas kernels: 171 us -> 129 us  [scatter_rows(): pl.pallas_call(functools.partial(scatter_kernel, parts, chunks, turned),...]
    all_gather x2 -> x1, waiting for transfers between devices: 32.9 us -> 0.01 us  [local(): lax.all_gather(jnp.concatenate([out_weight, reduce_weight]).astype(NARROW...]
    pallas_call x3, Pallas kernels: 147 us -> 176 us  [gather_rows(): pl.pallas_call(functools.partial(gather_kernel, parts, chunks, len(extra)...]
    all_gather x1 -> x0, blocking collectives: 12.8 us -> none  [local(): lax.all_gather(out_weight.astype(NARROW), 'dp', axis=1, tiled=True)]
    unnamed x169 -> x174, local copies, waits for them, and re-layouts: 59.9 us -> 61.6 us
  transfers between devices with their start and end apart: 9 -> 8, of which waited for: 3 -> 0; matrix products, arithmetic and copies ran while one was open for 12% -> 14% of each run, Pallas kernels for 62% -> 65%
where the time goes in v3:
time: 573 us; the launch traced here: 564 us
  Pallas kernels  415 us (72%)
  local copies, waits for them, and re-layouts  72.6 us (13%)
  matrix products  30.9 us (5%)
  other arithmetic  28.3 us (5%)
  between operations  15.6 us (3%)
    pallas_call x3, Pallas kernels, gather_rows(): pl.pallas_call(functools.partial(gather_kernel, parts, chunks, len(extra)...  176 us
    pallas_call x3, Pallas kernels, scatter_rows(): pl.pallas_call(functools.partial(scatter_kernel, parts, chunks, turned),...  129 us
    unnamed x174, local copies, waits for them, and re-layouts  61.6 us
    pallas_call x1, Pallas kernels, first_gather(): pl.pallas_call(functools.partial(first_gather_kernel, outer, parts, chunk...  56.7 us
    dot_general x6, matrix products, contract_rows(): lax.dot_general(left_side, right_side, (((0,), (0,)), ((), ())), preferre...  19 us
    pallas_call x1, Pallas kernels, small_sum(): pl.pallas_call(functools.partial(small_sum_kernel, outer, inner), out_sha...  18.5 us
    pallas_call x1, Pallas kernels, attend_backward(): pl.pallas_call(functools.partial(backward_kernel, heads, size, grid_side,...  18.4 us
    pallas_call x1, Pallas kernels, attend_forward(): pl.pallas_call(functools.partial(forward_kernel, heads, size, grid_side,...  15.5 us
  transfers between devices with their start and end apart: 8, of which 0 were waited for; matrix products, arithmetic and copies ran while one was open for 14% of the time, Pallas kernels for 65%

profile of v3, /device:TPU:0, one launch (start us, length us, event | category | flops | bytes accessed | tf_op | source)
XLA Modules:
  0.0 563.8 jit_solution(13798347185310708737)
XLA Ops:
  7.3 2.0 convert_element_type.98
  9.4 1.0 pad_maximum_fusion.1
  12.0 56.7 %first_gather.1 = (bf16[1024,1280]{1,0:T(8,128)(2,1)}, f32[32,8,128]{2,1,0:T(8,128)}) custom-call(bf16[256,1280]{1,0:T(8,128)(2,1)} %bitcast.111, f32[8,128]{1,0:T(8,128)} %pad_bitcast_fusion.small_ref), custom_call_target="tpu_custom_call" | custom-call | tf_op jit(solution)/shard_map/first_gather/pallas_call | solution.py:326
  68.7 1.0 copy.145
  71.4 2.2 fusion.31
  74.0 1.9 copy-done.2
  75.9 46.8 %gather_project.1 = (bf16[1024,1280]{1,0:T(8,128)(2,1)S(1)}, bf16[3,1024,320]{2,1,0:T(8,128)(2,1)S(1)}) custom-call(bf16[256,1280]{1,0:T(8,128)(2,1)S(1)} %fusion.11.own_ref, bf16[3,1280,320]{2,1,0:T(8,128)(2,1)S(1)} %copy-done.2, f32[3,1,320]{2,1,0:T(1,128)S(1)} %broadcast_in_dim.16.refs_1_), custom_call_target="tpu_custom_call" | custom-call | tf_op jit(solution)/shard_map/gather_project/pallas_call | solution.py:466
  122.7 1.5 copy-done.20
  124.2 15.5 %attend_forward.1 = (bf16[1024,320]{1,0:T(8,128)(2,1)S(1)}, bf16[4,1024,128]{2,1,0:T(8,128)(2,1)S(1)}, f32[4,1,1024]{2,1,0:T(1,128)S(1)}) custom-call(bf16[3,1024,320]{2,1,0:T(8,128)(2,1)S(1)} %get-tuple-element.57.qkv_ref, bf16[128,80]{1,0:T(8,128)(2,1)S(1)} %bitcast.104, bf16[1024,128]{1,0:T(8,128)(2,1)S(1)} %get-tuple-element.210.hot_ref), custom_call_target="tpu_custom_call" | custom-call | tf_op jit(solution)/shard_map/attend_forward/pallas_call | solution.py:187
  139.7 1.4 copy-done.4
  141.1 1.0 copy-done.16
  142.1 1.5 slice-done.2
  144.2 42.7 %scatter_out.1 = f32[256,1280]{1,0:T(8,128)S(1)} custom-call(bf16[1,1024,320]{2,1,0:T(8,128)(2,1)S(1)} %bitcast.101, bf16[1,320,1280]{2,1,0:T(8,128)(2,1)S(1)} %bitcast.100), custom_call_target="tpu_custom_call" | custom-call | tf_op jit(solution)/shard_map/scatter_out/pallas_call | solution.py:586
  188.3 1.9 copy-done
  190.2 46.1 %gather_expand.1 = (bf16[1024,1280]{1,0:T(8,128)(2,1)S(1)}, bf16[1024,1280]{1,0:T(8,128)(2,1)S(1)}, f32[1024,1280]{1,0:T(8,128)S(1)}) custom-call(bf16[256,1280]{1,0:T(8,128)(2,1)S(1)} %add_convert_fusion.1.own_ref, bf16[1280,1280]{1,0:T(8,128)(2,1)S(1)} %copy-done, f32[1,1280]{1,0:T(1,128)S(1)} %broadcast_in_dim.19.refs_1_), custom_call_target="tpu_custom_call" | custom-call | tf_op jit(solution)/shard_map/gather_expand/pallas_call | solution.py:466
  236.3 5.1 convolution_convert_fusion.1
  241.4 4.8 convert_reduce_fusion
  246.3 5.1 convolution_convert_fusion
  251.4 1.6 copy-done.11
  252.9 7.1 %convolution_convert_fusion.2 = bf16[1024,1280]{1,0:T(8,128)(2,1)} fusion(bf16[1024,1280]{1,0:T(8,128)(2,1)S(1)} %copy-done.23, bf16[1600,1280]{0,1:T(8,128)(2,1)} %all-gather.6.cloned.1.call-done), kind=kOutput, calls=%fused_computation.4 | convolution fusion | flops 3356753920 | bytes 8519680 | tf_op jit(solution)/shard_map/dot_general | solution.py:722
  260.0 5.6 %copy.119 = bf16[1280,1280]{0,1:T(8,128)(2,1)} copy(bf16[1280,1280]{1,0:T(8,128)(2,1)} %convolution_convert_fusion.1) | data formatting | bytes 6553600
  267.5 1.5 copy.100
  269.0 2.1 copy.98
  271.0 2.7 copy.104
  273.8 1.8 copy.103
  275.6 1.9 copy-done.12
  277.5 42.2 %scatter_expand.1 = f32[256,1280]{1,0:T(8,128)S(1)} custom-call(bf16[1,1024,1280]{2,1,0:T(8,128)(2,1)S(1)} %bitcast.102, bf16[1,1280,1280]{2,1,0:T(8,128)(2,1)S(1)} %bitcast.99), custom_call_target="tpu_custom_call" | custom-call | tf_op jit(solution)/shard_map/scatter_expand/pallas_call | solution.py:586
  319.7 1.1 multiply_reduce_fusion
  320.9 2.4 convert_reduce_fusion.5
  323.2 83.6 %gather_context.1 = (bf16[1024,1280]{1,0:T(8,128)(2,1)S(1)}, bf16[1024,320]{1,0:T(8,128)(2,1)S(1)}) custom-call(bf16[256,1280]{1,0:T(8,128)(2,1)S(1)} %get-tuple-element.192.own_ref, bf16[320,1280]{1,0:T(8,128)(2,1)S(1)} %copy-done.6), custom_call_target="tpu_custom_call" | custom-call | tf_op jit(solution)/shard_map/gather_context/pallas_call | solution.py:466
  406.9 0.9 copy-done.18
  407.8 2.8 copy.99
  410.5 0.9 dynamic_update_slice.11
  411.4 1.9 convolution_convert_fusion.6
  413.4 2.2 copy.120
  415.5 1.4 copy.123
  417.0 1.2 copy-done.17
  418.2 1.1 copy-done.19
  419.4 18.4 %attend_backward.1 = (bf16[3,1024,320]{2,1,0:T(8,128)(2,1)S(1)}, f32[128,80]{1,0:T(8,128)S(1)}) custom-call(bf16[3,1024,320]{2,1,0:T(8,128)(2,1)} %copy-done.4, bf16[1024,320]{1,0:T(8,128)(2,1)S(1)} %copy-done.19, bf16[4,1024,128]{2,1,0:T(8,128)(2,1)S(1)} %copy-done.17, f32[4,1,1024]{2,1,0:T(1,128)S(1)} %get-tuple-element.69.lse_ref, ...), custom_call_target="tpu_custom_call" | custom-call | tf_op jit(solution)/shard_map/attend_backward/pallas_call | solution.py:210
  437.8 2.0 convolution_convert_fusion.5
  439.7 2.0 convolution_convert_fusion.4
  441.8 4.5 add_multiply_fusion
  446.6 2.2 copy.108
  448.8 2.6 copy.111
  451.4 2.6 copy.114
  454.0 2.6 copy.117
  457.3 2.9 convolution_convert_fusion.3
  460.3 1.6 pad_maximum_fusion
  462.1 2.1 fusion.25
  464.2 4.5 copy.121
  468.7 1.1 copy-done.33
  470.3 3.0 add_multiply_fusion.1
  473.9 44.4 %scatter_qkv.1 = f32[256,1280]{1,0:T(8,128)S(1)} custom-call(bf16[3,1024,320]{2,1,0:T(8,128)(2,1)S(1)} %copy-done.8, bf16[3,1280,320]{2,1,0:T(8,128)(2,1)S(1)} %copy-done.3), custom_call_target="tpu_custom_call" | custom-call | tf_op jit(solution)/shard_map/scatter_qkv/pallas_call | solution.py:586
  518.5 0.9 copy.97
  519.3 1.2 fusion.17
  521.6 18.5 %small_sum.1 = (f32[8,128]{1,0:T(8,128)}, f32[32,8,128]{2,1,0:T(8,128)}) custom-call(f32[32,8,128]{2,1,0:T(8,128)} %bitcast.113), custom_call_target="tpu_custom_call" | custom-call | tf_op jit(solution)/shard_map/small_sum/pallas_call | solution.py:343
  540.0 0.9 copy.144
  541.9 0.9 fusion.33
  544.8 1.1 fusion.16
  546.1 2.4 copy.106
  549.1 1.0 copy.124
  551.0 0.8 copy.110
  553.5 1.2 copy.122
  555.0 1.6 add_multiply_fusion.2
  (227 shorter events, 17.1 us)
Async XLA Ops:
  7.2 2.1 copy-start.34
  7.2 2.2 copy-start.42
  7.2 66.7 %all-gather.4.cloned.1.call-start = ((), (), s32[]{:S(2)}) async-start(), calls=%async_computation.5 | async-start | bytes 3317760 | tf_op jit(solution)/shard_map/all_gather | solution.py:669
  9.3 132.8 %all-gather.6.cloned.1.call-start = ((), (), s32[]{:S(2)}) async-start(), calls=%async_computation.6 | async-start | bytes 4792320 | tf_op jit(solution)/shard_map/all_gather | solution.py:670
  10.4 59.7 %copy-start.49 = (f32[2,63,80]{2,0,1:T(2,128)S(1)}, f32[2,63,80]{2,0,1:T(2,128)}, u32[]{:S(2)}) copy-start(f32[2,63,80]{2,0,1:T(2,128)} %param.27) | copy-start | bytes 120964
  10.5 177.8 %all-gather.8.cloned.1.call-start = ((), (), s32[]{:S(2)}) async-start(), calls=%async_computation.7 | async-start | bytes 3686400 | tf_op jit(solution)/shard_map/all_gather | solution.py:674
  11.3 59.6 %copy-start.27 = (bf16[256,1,1280]{2,0,1:T(8,128)(2,1)S(1)}, bf16[256,1,1280]{2,0,1:T(8,128)(2,1)}, u32[]{:S(2)}) copy-start(bf16[256,1,1280]{2,0,1:T(8,128)(2,1)} %param.20) | copy-start | bytes 1966084
  11.3 402.0 %reduce-scatter.16.cloned.1.call-start = ((), (), s32[]{:S(2)}) async-start(), calls=%async_computation.10 | async-start | bytes 3686400
  71.4 51.3 %copy-start.57 = (f32[256]{0:T(256)}, f32[256]{0:T(256)S(1)}, u32[]{:S(2)}) copy-start(f32[256]{0:T(256)S(1)} %add_rsqrt_fusion.1) | copy-start | bytes 3076
  73.6 50.6 %copy-start.13 = (bf16[1024,128]{1,0:T(8,128)(2,1)}, bf16[1024,128]{1,0:T(8,128)(2,1)S(1)}, u32[]{:S(2)}) copy-start(bf16[1024,128]{1,0:T(8,128)(2,1)S(1)} %get-tuple-element.210.hot_ref) | copy-start | bytes 786436
  74.0 1.9 copy-start.2
  142.1 2.1 copy-start.9
  144.2 42.7 %copy-start.5 = (bf16[320,1280]{1,0:T(8,128)(2,1)}, bf16[320,1280]{1,0:T(8,128)(2,1)S(1)}, u32[]{:S(2)}) copy-start(bf16[320,1280]{1,0:T(8,128)(2,1)S(1)} %copy.125.refs_0_) | copy-start | bytes 2457604
  144.2 42.7 %copy-start.28 = (bf16[256,1,1280]{2,0,1:T(8,128)(2,1)S(1)}, bf16[256,1,1280]{2,0,1:T(8,128)(2,1)}, u32[]{:S(2)}) copy-start(bf16[256,1,1280]{2,0,1:T(8,128)(2,1)} %param.20) | copy-start | bytes 1966084
  188.3 1.9 copy-start
  190.2 46.1 %copy-start.66 = (bf16[1024,1280]{1,0:T(8,128)(2,1)S(1)}, bf16[1024,1280]{1,0:T(8,128)(2,1)}, u32[]{:S(2)}) copy-start(bf16[1024,1280]{1,0:T(8,128)(2,1)} %get-tuple-element.59) | copy-start | bytes 7864324
  190.2 51.2 %slice-start = ((s8[4259840]{0:T(1024)(128)(4,1)}), s8[65536]{0:T(1024)(128)(4,1)S(1)}, s32[]{:S(2)}) async-start(s8[4259840]{0:T(1024)(128)(4,1)} %bitcast.108), calls=%async_computation.13 | async-start | bytes 131072
  236.3 5.2 copy-start.22
  236.3 5.1 slice-start.1
  246.3 6.7 %copy-start.23 = (bf16[1024,1280]{1,0:T(8,128)(2,1)S(1)}, bf16[1024,1280]{1,0:T(8,128)(2,1)}, u32[]{:S(2)}) copy-start(bf16[1024,1280]{1,0:T(8,128)(2,1)} %copy-done.22) | copy-start | bytes 7864324
  251.4 1.6 copy-start.11
  265.7 196.2 %reduce-scatter.12.cloned.1.call-start = ((), (), s32[]{:S(2)}) async-start(), calls=%async_computation.8 | async-start | bytes 3276800 | tf_op jit(solution)/shard_map/reduce_scatter | solution.py:743
  266.3 202.4 %reduce-scatter.14.cloned.1.call-start = ((), (), s32[]{:S(2)}) async-start(), calls=%async_computation.9 | async-start | bytes 3686400 | tf_op jit(solution)/shard_map/reduce_scatter | solution.py:744
  266.9 282.2 %reduce-scatter.20.cloned.1.call-start = ((), (), s32[]{:S(2)}) async-start(), calls=%async_computation.12 | async-start | bytes 1105920
  269.0 6.6 %copy-start.1 = (bf16[1280,1280]{1,0:T(8,128)(2,1)S(1)}, bf16[1280,1280]{1,0:T(8,128)(2,1)}, u32[]{:S(2)}) copy-start(bf16[1280,1280]{1,0:T(8,128)(2,1)} %all-gather.8.cloned.1.call-done.refs_0_) | copy-start | bytes 9830404
  275.6 1.9 copy-start.12
  277.5 42.2 %copy-start.25 = (f32[256,1280]{1,0:T(8,128)S(1)}, f32[256,1280]{1,0:T(8,128)}, u32[]{:S(2)}) copy-start(f32[256,1280]{1,0:T(8,128)} %copy-done.24) | copy-start | bytes 3932164
  320.8 2.4 copy-start.6
  407.8 3.7 copy-start.10
  413.3 2.2 copy-start.31
  413.4 3.6 copy-start.14
  413.4 3.7 copy-start.15
  419.4 18.4 %copy-start.21 = (bf16[1024,1280]{1,0:T(8,128)(2,1)S(1)}, bf16[1024,1280]{1,0:T(8,128)(2,1)}, u32[]{:S(2)}) copy-start(bf16[1024,1280]{1,0:T(8,128)(2,1)} %copy-done.20) | copy-start | bytes 7864324
  437.8 19.6 %copy-start.7 = (bf16[3,1024,320]{2,1,0:T(8,128)(2,1)}, bf16[3,1024,320]{2,1,0:T(8,128)(2,1)S(1)}, u32[]{:S(2)}) copy-start(bf16[3,1024,320]{2,1,0:T(8,128)(2,1)S(1)} %get-tuple-element.75.left_ref) | copy-start | bytes 5898244
  441.7 111.8 %reduce-scatter.18.cloned.1.call-start = ((), (), s32[]{:S(2)}) async-start(), calls=%async_computation.11 | async-start | bytes 2949120
  457.3 2.9 copy-start.45
  457.3 2.9 copy-start.46
  460.3 1.8 copy-start.26
  460.3 1.8 copy-start.52
  468.7 1.6 copy-start.44
  470.3 3.0 copy-start.3
  470.3 3.6 copy-start.8
  473.9 44.5 %copy-start.50 = (f32[320,160]{0,1:T(8,128)S(1)}, f32[320,160]{0,1:T(8,128)}, u32[]{:S(2)}) copy-start(f32[320,160]{0,1:T(8,128)} %param.29) | copy-start | bytes 614404
  473.9 45.4 %copy-start.29 = (bf16[256,1,1280]{2,0,1:T(8,128)(2,1)S(1)}, bf16[256,1,1280]{2,0,1:T(8,128)(2,1)}, u32[]{:S(2)}) copy-start(bf16[256,1,1280]{2,0,1:T(8,128)(2,1)} %param.20) | copy-start | bytes 1966084
  473.9 45.4 %copy-start.58 = (f32[256]{0:T(256)S(1)}, f32[256]{0:T(256)}, u32[]{:S(2)}) copy-start(f32[256]{0:T(256)} %copy-done.57) | copy-start | bytes 3076
  518.4 2.1 copy-start.51
  518.4 2.2 copy-start.54
  518.4 2.2 copy-start.56
  518.4 2.2 copy-start.55
  518.4 2.2 copy-start.53
  520.5 24.3 %copy-start.30 = (f32[256,1280]{1,0:T(8,128)S(1)}, f32[256,1280]{1,0:T(8,128)}, u32[]{:S(2)}) copy-start(f32[256,1280]{1,0:T(8,128)} %get-tuple-element.193) | copy-start | bytes 3932164
  520.7 24.1 %copy-start.62 = (f32[256]{0:T(256)S(1)}, f32[256]{0:T(256)}, u32[]{:S(2)}) copy-start(f32[256]{0:T(256)} %get-tuple-element.169) | copy-start | bytes 3076
  520.7 24.1 %copy-start.61 = (f32[256]{0:T(256)S(1)}, f32[256]{0:T(256)}, u32[]{:S(2)}) copy-start(f32[256]{0:T(256)} %get-tuple-element.170) | copy-start | bytes 3076
  546.0 2.5 copy-start.60
  546.0 2.5 copy-start.63
  546.0 2.5 copy-start.64
  546.0 2.5 copy-start.65
  546.0 4.9 copy-start.39
  546.0 4.9 copy-start.40
  546.1 4.9 copy-start.41
  552.7 2.2 copy-start.37
  552.7 2.3 copy-start.47
  552.7 2.3 copy-start.48
  555.0 1.6 copy-start.36
  (14 other events, 16.7 us)
Sparse Core Ops, SparseCore 0:
  10.5 34.3 all-gather.3
  47.3 36.8 all-gather.5
  86.7 32.7 all-gather.7
  265.8 45.4 reduce-scatter.15
  313.5 69.7 reduce-scatter.11
  386.6 48.5 reduce-scatter.13
  441.8 35.6 reduce-scatter.19
  480.8 43.4 reduce-scatter.17

commit v4 on v3

--- a/solution.py
+++ b/solution.py
@@ -719,13 +719,14 @@
         ),
         expand_rows, tensor_count, 4, "gather_expand",
     )
-    mlp_part = jnp.dot(hidden_low, reduce_full, preferred_element_type=SINGLE).astype(NARROW)
     grad_block = cotangent_rows.astype(SINGLE)
     grad_reduce_bias = jnp.sum(grad_block, axis=0)
-    shard_rows = output_grads
+    mlp_part = jnp.dot(hidden_low, reduce_full, preferred_element_type=SINGLE).astype(NARROW)
+    shard_rows, mlp_part = lax.optimization_barrier((output_grads, mlp_part))
+    mlp_sum = lax.psum_scatter(mlp_part, "tensor", scatter_dimension=0, tiled=True)
     part_hidden = contract_cols(shard_rows, reduce_full)
     grad_hidden = part_hidden
-    grad_hidden, grad_reduce = (grad_hidden, contract_rows(hidden_low, shard_rows))
+    grad_hidden, grad_reduce = (grad_hidden, contract_rows(shard_rows, hidden_low))
     grad_pre = (grad_hidden * hidden_slope).astype(NARROW)
     grad_expand = contract_rows(gathered_two, grad_pre)
     grad_expand_bias = jnp.sum(grad_pre, axis=0, dtype=SINGLE)
@@ -736,11 +737,10 @@
         0,
     )
     grad_reduce, grad_expand = (grad_reduce.astype(NARROW), grad_expand.astype(NARROW))
-    grad_pre, grad_reduce, mlp_part, grad_expand = lax.optimization_barrier(
-        (grad_pre, grad_reduce, mlp_part, grad_expand)
-    )
-    reduce_sum = lax.psum_scatter(grad_reduce, "dp", scatter_dimension=1, tiled=True)
-    mlp_sum = lax.psum_scatter(mlp_part, "tensor", scatter_dimension=0, tiled=True)
+    grad_pre, grad_reduce, grad_expand = lax.optimization_barrier(
+        (grad_pre, grad_reduce, grad_expand)
+    )
+    reduce_sum = lax.psum_scatter(grad_reduce, "dp", scatter_dimension=0, tiled=True)
     expand_sum = lax.psum_scatter(grad_expand, "dp", scatter_dimension=0, tiled=True)
     grad_normed_two = scatter_rows(
         grad_pre[None], expand_full[None], True, tensor_count, 5, "scatter_expand"
@@ -750,6 +750,10 @@
     )
     grad_mid = grad_block + grad_mid_norm
     grad_attn_low = grad_mid.astype(NARROW)
+    late_rows = lax.optimization_barrier((mid_rows, grad_normed_two))[0]
+    block_rows = late_rows + (mlp_sum.astype(SINGLE) + segment(7))
+    block_out = block_rows.astype(NARROW).reshape(tokens.shape)
+    grad_attn_low, block_out = lax.optimization_barrier((grad_attn_low, block_out))
     grad_out_bias = jnp.sum(grad_attn_low, axis=0, dtype=SINGLE)
     shard_rows, grad_context = gather_rows(
         grad_attn_low,
@@ -757,13 +761,8 @@
         (jax.ShapeDtypeStruct((seq_length, head_width), NARROW),),
         context_grad_rows, tensor_count, 6, "gather_context",
     )
-    grad_out = contract_rows(context_rows, shard_rows).astype(NARROW)
-    late_rows = lax.optimization_barrier((mid_rows, shard_rows))[0]
-    block_rows = late_rows + (mlp_sum.astype(SINGLE) + segment(7))
-    block_out = block_rows.astype(NARROW).reshape(tokens.shape)
-    grad_context, grad_out, reduce_sum = lax.optimization_barrier(
-        (grad_context, grad_out, reduce_sum)
-    )
+    grad_out = contract_rows(shard_rows, context_rows).astype(NARROW)
+    grad_context, reduce_sum = lax.optimization_barrier((grad_context, reduce_sum))
     grad_qkv_rows, grad_tables = attend_backward(
         qkv_rows, grad_context, bias_wide, logsums, plain, hot, back,
         heads, head_size, grid_side,
@@ -771,11 +770,12 @@
     grad_query_bias = jnp.sum(grad_qkv_rows[0], axis=0, dtype=SINGLE)
     grad_value_bias = jnp.sum(grad_qkv_rows[2], axis=0, dtype=SINGLE)
     grad_qkv = jnp.concatenate(
-        [contract_rows(gathered_one, grad_qkv_rows[part]).astype(NARROW) for part in range(3)],
+        [contract_rows(gathered_one, grad_qkv_rows[part]).astype(NARROW) for part in range(3)]
+        + [grad_out],
         axis=1,
     )
-    grad_qkv_rows, grad_qkv, block_out = lax.optimization_barrier(
-        (grad_qkv_rows, grad_qkv, block_out)
+    grad_qkv_rows, grad_qkv, expand_sum = lax.optimization_barrier(
+        (grad_qkv_rows, grad_qkv, expand_sum)
     )
     grad_normed_one = scatter_rows(
         grad_qkv_rows, qkv_full, True, tensor_count, 7, "scatter_qkv"
@@ -814,15 +814,10 @@
     gains_grad = own_sum.reshape(-1)[:piece]
     rel_grad = rel_grad.reshape(devices, TILE)[:, piece : piece + rel_piece].reshape(-1)
     rel_grad = rel_grad[: rel_tables.size].reshape(rel_tables.shape)
-    qkv_grad, out_grad, expand_grad, reduce_grad = (
-        lax.psum_scatter(grad_qkv, "dp", scatter_dimension=0, tiled=True)
-        .astype(SINGLE)
-        .reshape(-1, 3, head_width)
-        .transpose(1, 0, 2),
-        lax.psum_scatter(grad_out.astype(NARROW), "dp", scatter_dimension=1, tiled=True).astype(SINGLE),
-        expand_sum.astype(SINGLE),
-        reduce_sum.astype(SINGLE),
-    )
+    heads_sum = lax.psum_scatter(grad_qkv, "dp", scatter_dimension=0, tiled=True).astype(SINGLE)
+    qkv_grad = heads_sum[:, : 3 * head_width].reshape(-1, 3, head_width).transpose(1, 0, 2)
+    out_grad = heads_sum[:, 3 * head_width :].T
+    expand_grad, reduce_grad = (expand_sum.astype(SINGLE), reduce_sum.astype(SINGLE).T)
     reduce_moment = lax.optimization_barrier((reduce_moment, grad_normed_two))[0]
     expand_moment = lax.optimization_barrier((expand_moment, grad_tables))[0]
     out_moment = lax.optimization_barrier((out_moment, grad_normed_one))[0]

time: 573 us -> 543 us (0.948)
  local copies, waits for them, and re-layouts: 72.6 us -> 56.8 us
  Pallas kernels: 415 us -> 400 us
    pallas_call x3, Pallas kernels: 176 us -> 141 us  [gather_rows(): pl.pallas_call(functools.partial(gather_kernel, parts, chunks, len(extra)...]
    pallas_call x3, Pallas kernels: 129 us -> 149 us  [scatter_rows(): pl.pallas_call(functools.partial(scatter_kernel, parts, chunks, turned),...]
    unnamed x174 -> x195, local copies, waits for them, and re-layouts: 61.6 us -> 49.5 us
  transfers between devices with their start and end apart: 8 -> 7, of which waited for: 0 -> 0; matrix products, arithmetic and copies ran while one was open for 14% -> 12% of each run, Pallas kernels for 65% -> 66%
where the time goes in v4:
time: 543 us; the launch traced here: 534 us
  Pallas kernels  400 us (74%)
  local copies, waits for them, and re-layouts  56.8 us (10%)
  matrix products  32.7 us (6%)
  other arithmetic  27.2 us (5%)
  between operations  15.8 us (3%)
    pallas_call x3, Pallas kernels, scatter_rows(): pl.pallas_call(functools.partial(scatter_kernel, parts, chunks, turned),...  149 us
    pallas_call x3, Pallas kernels, gather_rows(): pl.pallas_call(functools.partial(gather_kernel, parts, chunks, len(extra)...  141 us
    pallas_call x1, Pallas kernels, first_gather(): pl.pallas_call(functools.partial(first_gather_kernel, outer, parts, chunk...  56.8 us
    unnamed x195, local copies, waits for them, and re-layouts  49.5 us
    pallas_call x1, Pallas kernels, attend_backward(): pl.pallas_call(functools.partial(backward_kernel, heads, size, grid_side,...  18.8 us
    pallas_call x1, Pallas kernels, small_sum(): pl.pallas_call(functools.partial(small_sum_kernel, outer, inner), out_sha...  18.7 us
    dot_general x6, matrix products, contract_rows(): lax.dot_general(left_side, right_side, (((0,), (0,)), ((), ())), preferre...  16.8 us
    pallas_call x1, Pallas kernels, attend_forward(): pl.pallas_call(functools.partial(forward_kernel, heads, size, grid_side,...  15.5 us
  transfers between devices with their start and end apart: 7, of which 0 were waited for; matrix products, arithmetic and copies ran while one was open for 12% of the time, Pallas kernels for 66%

profile of v4, /device:TPU:0, one launch (start us, length us, event | category | flops | bytes accessed | tf_op | source)
XLA Modules:
  0.0 533.8 jit_solution(12403251811645427567)
XLA Ops:
  7.3 2.0 convert_element_type.96
  9.4 1.0 pad_maximum_fusion.1
  10.5 0.8 convert_element_type.100
  12.0 56.8 %first_gather.1 = (bf16[1024,1280]{1,0:T(8,128)(2,1)}, f32[32,8,128]{2,1,0:T(8,128)}) custom-call(bf16[256,1280]{1,0:T(8,128)(2,1)} %bitcast.113, f32[8,128]{1,0:T(8,128)} %pad_bitcast_fusion.small_ref), custom_call_target="tpu_custom_call" | custom-call | tf_op jit(solution)/shard_map/first_gather/pallas_call | solution.py:326
  68.8 1.0 copy.120
  71.5 2.2 fusion.31
  74.1 1.9 copy-done.2
  76.0 46.8 %gather_project.1 = (bf16[1024,1280]{1,0:T(8,128)(2,1)S(1)}, bf16[3,1024,320]{2,1,0:T(8,128)(2,1)S(1)}) custom-call(bf16[256,1280]{1,0:T(8,128)(2,1)S(1)} %fusion.11.own_ref, bf16[3,1280,320]{2,1,0:T(8,128)(2,1)S(1)} %copy-done.2, f32[3,1,320]{2,1,0:T(1,128)S(1)} %broadcast_in_dim.16.refs_1_), custom_call_target="tpu_custom_call" | custom-call | tf_op jit(solution)/shard_map/gather_project/pallas_call | solution.py:466
  122.8 1.5 copy-done.22
  124.3 15.5 %attend_forward.1 = (bf16[1024,320]{1,0:T(8,128)(2,1)S(1)}, bf16[4,1024,128]{2,1,0:T(8,128)(2,1)S(1)}, f32[4,1,1024]{2,1,0:T(1,128)S(1)}) custom-call(bf16[3,1024,320]{2,1,0:T(8,128)(2,1)S(1)} %get-tuple-element.59.qkv_ref, bf16[128,80]{1,0:T(8,128)(2,1)S(1)} %bitcast.109, bf16[1024,128]{1,0:T(8,128)(2,1)S(1)} %get-tuple-element.214.hot_ref), custom_call_target="tpu_custom_call" | custom-call | tf_op jit(solution)/shard_map/attend_forward/pallas_call | solution.py:187
  139.8 1.4 copy-done.6
  141.2 1.0 copy-done.16
  142.3 2.5 slice.75
  144.8 1.5 copy.100.refs_0_
  146.3 42.7 %scatter_out.1 = f32[256,1280]{1,0:T(8,128)S(1)} custom-call(bf16[1,1024,320]{2,1,0:T(8,128)(2,1)S(1)} %bitcast.107, bf16[1,320,1280]{2,1,0:T(8,128)(2,1)S(1)} %bitcast.105), custom_call_target="tpu_custom_call" | custom-call | tf_op jit(solution)/shard_map/scatter_out/pallas_call | solution.py:586
  190.7 1.9 copy-done
  192.7 46.1 %gather_expand.1 = (bf16[1024,1280]{1,0:T(8,128)(2,1)S(1)}, bf16[1024,1280]{1,0:T(8,128)(2,1)S(1)}, f32[1024,1280]{1,0:T(8,128)S(1)}) custom-call(bf16[256,1280]{1,0:T(8,128)(2,1)S(1)} %add_convert_fusion.1.own_ref, bf16[1280,1280]{1,0:T(8,128)(2,1)S(1)} %copy-done, f32[1,1280]{1,0:T(1,128)S(1)} %broadcast_in_dim.19.refs_1_), custom_call_target="tpu_custom_call" | custom-call | tf_op jit(solution)/shard_map/gather_expand/pallas_call | solution.py:466
  238.8 2.3 copy-done.21
  241.1 1.6 copy-done.24
  242.7 1.5 copy-done.28
  244.2 7.1 %convolution_convert_fusion.2 = bf16[1024,1280]{1,0:T(8,128)(2,1)} fusion(bf16[1024,1280]{1,0:T(8,128)(2,1)S(1)} %get-tuple-element.62, bf16[1600,1280]{0,1:T(8,128)(2,1)} %all-gather.6.cloned.1.call-done), kind=kOutput, calls=%fused_computation.4 | convolution fusion | flops 3356753920 | bytes 8519680 | tf_op jit(solution)/shard_map/dot_general | solution.py:724
  251.4 1.7 copy-done.29
  253.1 7.5 %convolution_convert_fusion.1 = bf16[1280,1280]{1,0:T(8,128)(2,1)} fusion(bf16[1024,1280]{1,0:T(8,128)(2,1)} %get-tuple-element.63, bf16[1024,1280]{1,0:T(8,128)(2,1)S(1)} %copy-done.29), kind=kOutput, calls=%fused_computation.1 | convolution fusion | flops 3357081600 | bytes 8519680 | tf_op jit(solution)/shard_map/dot_general | solution.py:40
  260.5 8.8 %convert_reduce_fusion = (f32[1280]{0:T(1024)}, bf16[1024,1280]{1,0:T(8,128)(2,1)S(1)}) fusion(f32[1024,1280]{1,0:T(8,128)} %copy-done.21, bf16[1024,1280]{1,0:T(8,128)(2,1)} %get-tuple-element.63, bf16[1600,1280]{0,1:T(8,128)(2,1)} %all-gather.6.cloned.1.call-done), kind=kOutput, calls=%fused_computation.2 | convolution fusion | flops 3360684800 | bytes 13767680 | tf_op jit(solution)/shard_map/dot_general | solution.py:46
  269.3 5.1 convolution_convert_fusion
  274.5 1.5 copy-done.13
  276.6 1.1 copy.102
  278.4 1.7 copy-done.14
  280.1 61.1 %scatter_expand.1 = f32[256,1280]{1,0:T(8,128)S(1)} custom-call(bf16[1,1024,1280]{2,1,0:T(8,128)(2,1)S(1)} %bitcast.106, bf16[1,1280,1280]{2,1,0:T(8,128)(2,1)S(1)} %bitcast.104), custom_call_target="tpu_custom_call" | custom-call | tf_op jit(solution)/shard_map/scatter_expand/pallas_call | solution.py:586
  341.3 1.1 multiply_reduce_fusion
  342.4 1.6 fusion.41
  344.0 2.3 fusion.25
  346.4 48.3 %gather_context.1 = (bf16[1024,1280]{1,0:T(8,128)(2,1)S(1)}, bf16[1024,320]{1,0:T(8,128)(2,1)S(1)}) custom-call(bf16[256,1280]{1,0:T(8,128)(2,1)S(1)} %get-tuple-element.70.own_ref, bf16[320,1280]{1,0:T(8,128)(2,1)S(1)} %copy-done.8), custom_call_target="tpu_custom_call" | custom-call | tf_op jit(solution)/shard_map/gather_context/pallas_call | solution.py:466
  394.8 1.5 copy-done.26
  396.3 18.8 %attend_backward.1 = (bf16[3,1024,320]{2,1,0:T(8,128)(2,1)S(1)}, f32[128,80]{1,0:T(8,128)S(1)}) custom-call(bf16[3,1024,320]{2,1,0:T(8,128)(2,1)} %copy-done.6, bf16[1024,320]{1,0:T(8,128)(2,1)S(1)} %get-tuple-element.73.grad_ref, bf16[4,1024,128]{2,1,0:T(8,128)(2,1)S(1)} %copy-done.17, f32[4,1,1024]{2,1,0:T(1,128)S(1)} %get-tuple-element.75.lse_ref, ...), custom_call_target="tpu_custom_call" | custom-call | tf_op jit(solution)/shard_map/attend_backward/pallas_call | solution.py:210
  415.2 1.1 convolution_convert_fusion.3
  416.3 1.5 copy-done.23
  417.8 1.1 convolution_convert_fusion.6
  418.8 1.1 convolution_convert_fusion.5
  419.9 1.1 convolution_convert_fusion.4
  421.0 1.9 pad_maximum_fusion
  422.9 5.6 %copy.98 = bf16[1280,1280]{1,0:T(8,128)(2,1)} copy(bf16[1280,1280]{0,1:T(8,128)(2,1)} %pad_maximum_fusion) | data formatting | bytes 6553600
  428.5 0.9 copy-done.46
  429.4 0.9 copy.84
  430.3 0.9 copy.87
  431.5 1.7 copy-done.10
  433.2 45.4 %scatter_qkv.1 = f32[256,1280]{1,0:T(8,128)S(1)} custom-call(bf16[3,1024,320]{2,1,0:T(8,128)(2,1)S(1)} %copy-done.10, bf16[3,1280,320]{2,1,0:T(8,128)(2,1)S(1)} %copy-done.3), custom_call_target="tpu_custom_call" | custom-call | tf_op jit(solution)/shard_map/scatter_qkv/pallas_call | solution.py:586
  478.6 1.0 copy-done.4
  479.9 1.8 convert_reduce_fusion.3
  482.2 1.2 fusion.17
  484.8 18.7 %small_sum.1 = (f32[8,128]{1,0:T(8,128)}, f32[32,8,128]{2,1,0:T(8,128)}) custom-call(f32[32,8,128]{2,1,0:T(8,128)} %bitcast.114), custom_call_target="tpu_custom_call" | custom-call | tf_op jit(solution)/shard_map/small_sum/pallas_call | solution.py:343
  503.5 0.9 copy.119
  507.4 1.8 fusion.16
  509.4 2.4 copy.89
  512.4 1.9 add_multiply_fusion
  514.4 0.8 copy-done.50
  515.3 1.9 add_multiply_fusion.1
  517.2 1.2 copy.99
  518.7 0.7 slice_bitcast_fusion
  519.9 0.8 copy.92
  520.7 0.8 copy.94
  521.5 0.8 copy.96
  522.7 0.9 copy.90
  523.7 2.8 add_multiply_fusion.2
  (245 shorter events, 12.9 us)
Async XLA Ops:
  7.2 2.1 copy-start.35
  7.2 2.2 copy-start.45
  7.2 66.8 %all-gather.4.cloned.1.call-start = ((), (), s32[]{:S(2)}) async-start(), calls=%async_computation.4 | async-start | bytes 3317760 | tf_op jit(solution)/shard_map/all_gather | solution.py:669
  9.3 133.0 %all-gather.6.cloned.1.call-start = ((), (), s32[]{:S(2)}) async-start(), calls=%async_computation.5 | async-start | bytes 4792320 | tf_op jit(solution)/shard_map/all_gather | solution.py:670
  10.4 59.7 %copy-start.54 = (f32[2,63,80]{2,0,1:T(2,128)S(1)}, f32[2,63,80]{2,0,1:T(2,128)}, u32[]{:S(2)}) copy-start(f32[2,63,80]{2,0,1:T(2,128)} %param.27) | copy-start | bytes 120964
  10.5 180.3 %all-gather.8.cloned.1.call-start = ((), (), s32[]{:S(2)}) async-start(), calls=%async_computation.6 | async-start | bytes 3686400 | tf_op jit(solution)/shard_map/all_gather | solution.py:674
  11.3 59.7 %copy-start.33 = (bf16[256,1,1280]{2,0,1:T(8,128)(2,1)S(1)}, bf16[256,1,1280]{2,0,1:T(8,128)(2,1)}, u32[]{:S(2)}) copy-start(bf16[256,1,1280]{2,0,1:T(8,128)(2,1)} %param.20) | copy-start | bytes 1966084
  11.3 332.7 %reduce-scatter.7.cloned.1.call-start = ((), (), s32[]{:S(2)}) async-start(), calls=%async_computation.7 | async-start | bytes 3276800 | tf_op jit(solution)/shard_map/reduce_scatter | solution.py:726
  70.9 3.2 copy-start.58
  70.9 118.8 %copy-start.60 = (f32[1280]{0:T(1024)}, f32[1280]{0:T(1024)S(1)}, u32[]{:S(2)}) copy-start(f32[1280]{0:T(1024)S(1)} %get-tuple-element.207) | copy-start | bytes 15364
  71.2 51.6 %copy-start.69 = (f32[256]{0:T(256)}, f32[256]{0:T(256)S(1)}, u32[]{:S(2)}) copy-start(f32[256]{0:T(256)S(1)} %broadcast_multiply_fusion.5) | copy-start | bytes 3076
  71.5 51.3 %copy-start.73 = (f32[256]{0:T(256)}, f32[256]{0:T(256)S(1)}, u32[]{:S(2)}) copy-start(f32[256]{0:T(256)S(1)} %add_rsqrt_fusion.1) | copy-start | bytes 3076
  142.2 4.1 copy-start.18
  146.3 42.7 %copy-start.7 = (bf16[320,1280]{1,0:T(8,128)(2,1)}, bf16[320,1280]{1,0:T(8,128)(2,1)S(1)}, u32[]{:S(2)}) copy-start(bf16[320,1280]{1,0:T(8,128)(2,1)S(1)} %copy.100.refs_0_) | copy-start | bytes 2457604
  189.6 49.1 %copy-start.71 = (f32[256]{0:T(256)}, f32[256]{0:T(256)S(1)}, u32[]{:S(2)}) copy-start(f32[256]{0:T(256)S(1)} %add_rsqrt_fusion) | copy-start | bytes 3076
  190.7 1.9 copy-start
  238.7 2.4 copy-start.21
  251.3 144.9 %reduce-scatter.9.cloned.1.call-start = ((), (), s32[]{:S(2)}) async-start(), calls=%async_computation.8 | async-start | bytes 3686400 | tf_op jit(solution)/shard_map/reduce_scatter | solution.py:743
  260.5 8.8 %copy-start.25 = (bf16[1024,1280]{1,0:T(8,128)(2,1)S(1)}, bf16[1024,1280]{1,0:T(8,128)(2,1)}, u32[]{:S(2)}) copy-start(bf16[1024,1280]{1,0:T(8,128)(2,1)} %copy-done.24) | copy-start | bytes 7864324
  276.0 2.3 copy-start.1
  276.0 146.9 %reduce-scatter.11.cloned.1.call-start = ((), (), s32[]{:S(2)}) async-start(), calls=%async_computation.9 | async-start | bytes 3686400 | tf_op jit(solution)/shard_map/reduce_scatter | solution.py:744
  276.6 240.6 %reduce-scatter.13.cloned.1.call-start = ((), (), s32[]{:S(2)}) async-start(), calls=%async_computation.10 | async-start | bytes 3686400
  280.1 61.1 %copy-start.31 = (f32[256,1280]{1,0:T(8,128)S(1)}, f32[256,1280]{1,0:T(8,128)}, u32[]{:S(2)}) copy-start(f32[256,1280]{1,0:T(8,128)} %copy-done.30) | copy-start | bytes 3932164
  280.1 61.1 %copy-start.61 = (f32[1280]{0:T(1024)S(1)}, f32[1280]{0:T(1024)}, u32[]{:S(2)}) copy-start(f32[1280]{0:T(1024)} %copy-done.60) | copy-start | bytes 15364
  280.1 61.1 %copy-start.68 = (f32[256]{0:T(256)S(1)}, f32[256]{0:T(256)}, u32[]{:S(2)}) copy-start(f32[256]{0:T(256)} %copy-done.67) | copy-start | bytes 3076
  280.1 61.1 %copy-start.72 = (f32[256]{0:T(256)S(1)}, f32[256]{0:T(256)}, u32[]{:S(2)}) copy-start(f32[256]{0:T(256)} %copy-done.71) | copy-start | bytes 3076
  344.0 2.4 copy-start.11
  344.0 2.4 copy-start.8
  346.4 49.9 %copy-start.15 = (bf16[1024,128]{1,0:T(8,128)(2,1)S(1)}, bf16[1024,128]{1,0:T(8,128)(2,1)}, u32[]{:S(2)}) copy-start(bf16[1024,128]{1,0:T(8,128)(2,1)} %get-tuple-element.213.rev_ref) | copy-start | bytes 786436
  346.4 49.9 %copy-start.17 = (bf16[4,1024,128]{2,1,0:T(8,128)(2,1)S(1)}, bf16[4,1024,128]{2,1,0:T(8,128)(2,1)}, u32[]{:S(2)}) copy-start(bf16[4,1024,128]{2,1,0:T(8,128)(2,1)} %copy-done.16) | copy-start | bytes 3145732
  346.4 49.9 %copy-start.20 = (bf16[2,64,80]{2,1,0:T(8,128)(2,1)S(1)}, bf16[2,64,80]{2,1,0:T(8,128)(2,1)}, u32[]{:S(2)}) copy-start(bf16[2,64,80]{2,1,0:T(8,128)(2,1)} %pad.17.clone) | copy-start | bytes 61444
  396.3 18.9 %copy-start.19 = (bf16[1024,320]{1,0:T(8,128)(2,1)S(1)}, bf16[1024,320]{1,0:T(8,128)(2,1)}, u32[]{:S(2)}) copy-start(bf16[1024,320]{1,0:T(8,128)(2,1)} %copy-done.18) | copy-start | bytes 1966084
  396.3 18.9 %copy-start.27 = (bf16[1024,1280]{1,0:T(8,128)(2,1)S(1)}, bf16[1024,1280]{1,0:T(8,128)(2,1)}, u32[]{:S(2)}) copy-start(bf16[1024,1280]{1,0:T(8,128)(2,1)} %copy-done.26) | copy-start | bytes 7864324
  415.2 4.7 copy-start.9
  415.2 2.6 copy-start.23
  428.5 2.7 copy-start.76
  428.5 3.0 copy-start.3
  433.2 46.5 %copy-start.57 = (f32[320,160]{0,1:T(8,128)S(1)}, f32[320,160]{0,1:T(8,128)}, u32[]{:S(2)}) copy-start(f32[320,160]{0,1:T(8,128)} %param.29) | copy-start | bytes 614404
  479.7 2.5 copy-start.34
  479.7 2.5 copy-start.59
  479.7 2.5 copy-start.70
  479.7 2.5 copy-start.74
  479.9 2.4 copy-start.5
  483.4 21.9 %copy-start.55 = (f32[2,63,80]{2,0,1:T(2,128)S(1)}, f32[2,63,80]{2,0,1:T(2,128)}, u32[]{:S(2)}) copy-start(f32[2,63,80]{2,0,1:T(2,128)} %param.27) | copy-start | bytes 120964
  483.4 21.9 %copy-start.62 = (f32[2,63,80]{2,0,1:T(2,128)S(1)}, f32[2,63,80]{2,0,1:T(2,128)}, u32[]{:S(2)}) copy-start(f32[2,63,80]{2,0,1:T(2,128)} %param.39) | copy-start | bytes 120964
  483.4 21.9 %copy-start.63 = (f32[2,63,80]{2,0,1:T(2,128)S(1)}, f32[2,63,80]{2,0,1:T(2,128)}, u32[]{:S(2)}) copy-start(f32[2,63,80]{2,0,1:T(2,128)} %param.33) | copy-start | bytes 120964
  483.6 23.8 %copy-start.80 = (f32[256]{0:T(256)S(1)}, f32[256]{0:T(256)}, u32[]{:S(2)}) copy-start(f32[256]{0:T(256)} %get-tuple-element.173) | copy-start | bytes 3076
  483.6 23.8 %copy-start.79 = (f32[256]{0:T(256)S(1)}, f32[256]{0:T(256)}, u32[]{:S(2)}) copy-start(f32[256]{0:T(256)} %get-tuple-element.174) | copy-start | bytes 3076
  483.6 23.8 %copy-start.75 = (f32[256]{0:T(256)S(1)}, f32[256]{0:T(256)}, u32[]{:S(2)}) copy-start(f32[256]{0:T(256)} %copy-done.73) | copy-start | bytes 3076
  507.4 4.9 copy-start.51
  509.3 2.5 copy-start.78
  509.3 2.5 copy-start.81
  509.3 2.5 copy-start.82
  509.3 2.5 copy-start.83
  509.3 3.1 copy-start.36
  509.3 3.0 copy-start.47
  509.3 3.0 copy-start.48
  512.4 1.9 copy-start.38
  512.4 2.0 copy-start.49
  512.4 2.8 copy-start.50
  512.4 2.9 copy-start.52
  520.7 2.0 copy-start.44
  521.5 2.1 copy-start.39
  522.7 3.8 copy-start.40
  (27 other events, 38.6 us)
Sparse Core Ops, SparseCore 0:
  10.5 34.3 all-gather.3
  47.3 36.8 all-gather.5
  86.7 32.7 all-gather.7
  251.5 67.9 reduce-scatter.6
  322.7 49.8 reduce-scatter.8
  375.9 46.7 reduce-scatter.10
  428.7 46.4 reduce-scatter.12
